TPU v7x, 8 devices: a whole 2x2x1 slice. The times are simulated.
8 devices in a mesh: dp: 1 (over z), hp: 2 (over y), sp: 4 (over x, core).
Axes of the slice: x: 2, y: 2, z: 1, core: 2. Of those that a mesh axis runs over, the one named last changes fastest.
Arguments:
- x_in: bfloat16 [4096, 4096], P(('dp', 'sp', 'hp'))
- w_q: bfloat16 [4096, 4096], P(None, 'hp')
- w_k: bfloat16 [4096, 4096], P(None, 'hp')
- w_v: bfloat16 [4096, 4096], P(None, 'hp')
- w_o: bfloat16 [4096, 4096], P('hp')
Outputs:
- output: bfloat16 [4096, 4096], P(('dp', 'sp', 'hp'))
All inputs are finite; a program needn't handle non-finite values.
Results may differ from a plain program's by a relative error of at most 0.00691038.
Values are sent between devices in bfloat16 or wider.
A program may use at most 1 GiB of HBM per device.

v0:
```python
import functools
import math

import jax
import jax.numpy as jnp
from jax import lax
from jax.experimental import pallas as pl
from jax.experimental.pallas import tpu as pltpu
from jax.sharding import PartitionSpec as P


HEAD_DIM = 128
EXP2_SCALE = math.log2(math.e) / math.sqrt(HEAD_DIM)


def attend_kernel(shape, heads, first, last, *refs):
    refs = list(refs)
    take = lambda n: [refs.pop(0) for _ in range(n)]
    q_refs = take(shape[0])
    groups = [(take(k), take(v)) for k, v in shape[1:]]
    state_in = None if first else take(3)
    outs = refs
    at = lambda h: slice(h * HEAD_DIM, (h + 1) * HEAD_DIM)
    queries = [jnp.concatenate([r[:, at(h)] for r in q_refs], axis=0) for h in range(heads)]

    def scores_of(h, g):
        parts = [
            lax.dot_general(k[:, at(h)], queries[h], (((1,), (1,)), ((), ())), preferred_element_type=jnp.float32)
            for k in groups[g][0]
        ]
        return parts[0] if len(parts) == 1 else jnp.concatenate(parts, axis=0)

    items = [(h, g) for g in range(len(groups)) for h in range(heads)]
    depth = 2
    state = {} if first else {h: (state_in[0][h], state_in[1][h], state_in[2][at(h), :]) for h in range(heads)}
    ahead = [scores_of(*items[i]) for i in range(min(depth, len(items)))]
    for i, (h, g) in enumerate(items):
        if i + depth < len(items):
            ahead.append(scores_of(*items[i + depth]))
        scores = ahead.pop(0)
        new_max = jnp.max(scores, axis=0, keepdims=True) * EXP2_SCALE
        if h in state:
            new_max = jnp.maximum(state[h][0], new_max)
        probs = jnp.exp2(scores * EXP2_SCALE - new_max)
        part_sum = jnp.sum(probs, axis=0, keepdims=True)
        probs = probs.astype(jnp.bfloat16)
        part, row = None, 0
        for v in groups[g][1]:
            count = v.shape[1]
            piece = jnp.dot(v[at(h), :], probs[row:row + count], preferred_element_type=jnp.float32)
            part = piece if part is None else part + piece
            row += count
        if h in state:
            run_max, run_sum, acc = state[h]
            fade = jnp.exp2(run_max - new_max)
            state[h] = (new_max, run_sum * fade + part_sum, acc * fade + part)
        else:
            state[h] = (new_max, part_sum, part)
    for h in range(heads):
        run_max, run_sum, acc = state[h]
        if last:
            outs[0][:, at(h)] = (acc / run_sum).T.astype(jnp.bfloat16)
        else:
            outs[0][h], outs[1][h], outs[2][at(h), :] = run_max, run_sum, acc


def attend(queries, groups, state, last, block=1):
    rows, heads = sum(q.shape[0] for q in queries), queries[0].shape[1] // HEAD_DIM
    width = block * HEAD_DIM
    first = state is None
    state_specs = [
        pl.BlockSpec((block, 1, rows), lambda h: (h, 0, 0)),
        pl.BlockSpec((block, 1, rows), lambda h: (h, 0, 0)),
        pl.BlockSpec((width, rows), lambda h: (h, 0)),
    ]
    state_shapes = [jax.ShapeDtypeStruct((heads, 1, rows), jnp.float32)] * 2
    state_shapes.append(jax.ShapeDtypeStruct((heads * HEAD_DIM, rows), jnp.float32))
    tall = lambda a: pl.BlockSpec((a.shape[0], width), lambda h: (0, h))
    wide = lambda a: pl.BlockSpec((width, a.shape[1]), lambda h: (h, 0))
    operands, in_specs, shape, key_rows = list(queries), [tall(q) for q in queries], [len(queries)], 0
    for keys, values_t in groups:
        operands += [*keys, *values_t]
        in_specs += [tall(k) for k in keys] + [wide(v) for v in values_t]
        shape.append((len(keys), len(values_t)))
        key_rows += sum(k.shape[0] for k in keys)
    count = len(operands)
    o_shape = jax.ShapeDtypeStruct((rows, heads * HEAD_DIM), jnp.bfloat16)
    return pl.pallas_call(
        functools.partial(attend_kernel, tuple(shape), block, first, last),
        grid=(heads // block,),
        in_specs=in_specs + ([] if first else state_specs),
        out_specs=pl.BlockSpec((rows, width), lambda h: (0, h)) if last else state_specs,
        out_shape=o_shape if last else state_shapes,
        input_output_aliases={} if first or last else {count + j: j for j in range(3)},
        cost_estimate=pl.CostEstimate(
            flops=8 * rows * key_rows * heads * HEAD_DIM,
            bytes_accessed=2 * heads * HEAD_DIM * (rows + 2 * key_rows),
            transcendentals=rows * key_rows * heads,
        ),
        compiler_params=pltpu.CompilerParams(vmem_limit_bytes=48 * 2**20),
    )(*operands, *(state or ()))


def project_kernel(flips, width, x_ref, *refs):
    count = len(flips)
    w_refs, o_refs, (ring, sems) = refs[:count], refs[count:2 * count], refs[2 * count:]
    steps = [w.shape[1] // width for w in w_refs]
    firsts = [sum(steps[:i]) for i in range(count)]

    def copy(i, step, slot):
        columns = pl.ds(pl.multiple_of(step * width, width), width)
        return pltpu.make_async_copy(w_refs[i].at[:, columns], ring.at[slot], sems.at[slot])

    def fetch(n):
        for i in range(count):
            @pl.when(jnp.logical_and(n >= firsts[i], n < firsts[i] + steps[i]))
            def _():
                copy(i, n - firsts[i], lax.rem(n, 3)).start()

    fetch(jnp.int32(0))
    fetch(jnp.int32(1))
    for i in range(count):
        def step(j, carry, i=i):
            n = firsts[i] + j
            slot = lax.rem(n, 3)
            fetch(n + 2)
            copy(i, j, slot).wait()
            block = jnp.dot(x_ref[...], ring[slot], preferred_element_type=jnp.float32)
            columns = pl.ds(pl.multiple_of(j * width, width), width)
            if flips[i]:
                o_refs[i][columns, :] = block.T.astype(jnp.bfloat16)
            else:
                o_refs[i][:, columns] = block.astype(jnp.bfloat16)
            return carry

        lax.fori_loop(0, steps[i], step, 0)


def project(x, weights, flips, width=512):
    rows, depth = x.shape
    shapes = [(w.shape[1], rows) if f else (rows, w.shape[1]) for w, f in zip(weights, flips)]
    return pl.pallas_call(
        functools.partial(project_kernel, tuple(flips), width),
        in_specs=[pl.BlockSpec(memory_space=pltpu.VMEM)] + [pl.BlockSpec(memory_space=pl.ANY)] * len(weights),
        out_specs=[pl.BlockSpec(memory_space=pltpu.VMEM)] * len(weights),
        out_shape=[jax.ShapeDtypeStruct(s, jnp.bfloat16) for s in shapes],
        scratch_shapes=[pltpu.VMEM((3, depth, width), jnp.bfloat16), pltpu.SemaphoreType.DMA((3,))],
        cost_estimate=pl.CostEstimate(
            flops=2 * rows * depth * sum(w.shape[1] for w in weights),
            bytes_accessed=2 * depth * sum(w.shape[1] for w in weights),
            transcendentals=0,
        ),
        compiler_params=pltpu.CompilerParams(vmem_limit_bytes=40 * 2**20),
    )(x, *weights)


def fold_kernel(depths, has_base, first_unit, lhs_ref, *refs):
    total = refs[len(depths)][...] if has_base else None
    for i, depth in enumerate(depths):
        start = pl.multiple_of(first_unit[i] * 128, 128)
        part = jnp.dot(lhs_ref[:, pl.ds(start, depth)], refs[i][...], preferred_element_type=jnp.float32)
        total = part if total is None else total + part
    refs[-1][...] = total.astype(refs[-1].dtype)


def fold(lhs, pieces, units, base, dtype, width=512):
    rows, columns = lhs.shape[0], pieces[0].shape[1]
    depths = tuple(p.shape[0] for p in pieces)
    out_spec = pl.BlockSpec((rows, width), lambda j, r: (0, j))
    return pl.pallas_call(
        functools.partial(fold_kernel, depths, base is not None),
        grid_spec=pltpu.PrefetchScalarGridSpec(
            num_scalar_prefetch=1,
            grid=(columns // width,),
            in_specs=[pl.BlockSpec(lhs.shape, lambda j, r: (0, 0))]
            + [pl.BlockSpec((d, width), lambda j, r: (0, j)) for d in depths]
            + ([out_spec] if base is not None else []),
            out_specs=out_spec,
        ),
        out_shape=jax.ShapeDtypeStruct((rows, columns), dtype),
        cost_estimate=pl.CostEstimate(
            flops=2 * rows * columns * sum(depths),
            bytes_accessed=2 * columns * sum(depths),
            transcendentals=0,
        ),
        compiler_params=pltpu.CompilerParams(vmem_limit_bytes=48 * 2**20),
    )(jnp.stack(units).astype(jnp.int32), lhs, *pieces, *(() if base is None else (base,)))


def after(value, *tokens):
    return lax.optimization_barrier((value, *tokens))[0]


def solution(mesh):
    hp_swap = [(0, 1), (1, 0)]
    x_swap = [(0, 2), (1, 3), (2, 0), (3, 1)]
    core_swap = [(0, 1), (1, 0), (2, 3), (3, 2)]

    def device_fn(x_own, w_q, w_k, w_v, w_o):
        sp = lax.axis_index('sp')
        chip, core = sp // 2, sp % 2
        half = x_own.shape[0] // 2
        over_y = lambda a: lax.ppermute(a, 'hp', hp_swap)
        over_x = lambda a: lax.ppermute(a, 'sp', x_swap)
        over_core = lambda a: lax.ppermute(a, 'sp', core_swap)

        unit_a = lambda chip_, core_: chip_ * 10 + core_ * 3
        unit_b = lambda core_: 6 + core_ * 2

        x_f0 = over_y(x_own[:half])
        (k_o,) = project(x_own, [w_k], [False])
        k_xo = over_x(k_o)
        x_f1 = over_y(after(x_own, k_o)[half:])
        v_o, q_o = project(after(x_own, k_o), [w_v, w_q], [True, False])
        v_xo = over_x(v_o)
        rows_a = lax.dynamic_slice_in_dim(after(w_o, v_o), unit_a(chip, core) * 128, 384, 0)
        rows_b = lax.dynamic_slice_in_dim(after(w_o, v_o), unit_b(core) * 128, 256, 0)
        wa = over_y(rows_a)
        wb = over_y(after(rows_b, rows_a))
        k_so, v_so = over_core(after(k_o, v_o)), over_core(v_o)

        all_w, all_f = [w_k, w_v, w_q], [False, True, False]
        k_r0, v_r0, q_r0 = project(after(x_f0, rows_a, rows_b), all_w, all_f)
        k_xr0, v_xr0 = over_x(k_r0), over_x(v_r0)
        k_sr0, v_sr0 = over_core(k_r0), over_core(v_r0)
        own, own_s = ([k_o], [v_o]), ([k_so], [v_so])
        state_o = attend([after(q_o, q_r0)], [own, own_s], None, False, 4)

        k_r1, v_r1, q_r1 = project(after(x_f1, state_o[0]), all_w, all_f)
        k_xr1, v_xr1 = over_x(k_r1), over_x(v_r1)
        k_sr1, v_sr1 = over_core(k_r1), over_core(v_r1)
        k_sxo, v_sxo = over_core(after(k_xo, q_r0)), over_core(after(v_xo, v_r1))
        far, far_s = ([k_r0, k_r1], [v_r0, v_r1]), ([k_sr0, k_sr1], [v_sr0, v_sr1])
        xo, xo_s = ([k_xo], [v_xo]), ([k_sxo], [v_sxo])
        state_r = attend([q_r0, q_r1], [own, own_s, far, far_s, xo, xo_s], None, False, 2)
        k_sxr0, v_sxr0 = over_core(after(k_xr0, state_r[0])), over_core(after(v_xr0, state_r[0]))
        state_o = attend([after(q_o, state_r[0])], [far, far_s, xo, xo_s], state_o, False, 2)
        wx = over_x(after(wa, state_o[0]))
        wa_s = over_core(after(wa, state_o[0]))
        late = ([k_xr0, k_sxr0], [v_xr0, v_sxr0])
        state_r = attend([after(q_r0, state_o[0]), q_r1], [late], state_r, False, 8)
        state_o = attend([after(q_o, state_r[0])], [late], state_o, False, 8)

        k_sxr1, v_sxr1 = over_core(after(k_xr1, state_o[0])), over_core(after(v_xr1, state_o[0]))
        latest = ([k_xr1, k_sxr1], [v_xr1, v_sxr1])
        o_r = attend([q_r0, q_r1], [latest], state_r, True, 8)
        o_f = over_y(o_r)
        o_own = attend([after(q_o, o_r)], [latest], state_o, True, 8)
        wb_s = over_core(after(wb, o_own))
        total = fold(o_own, [w_o], [sp * 0], None, jnp.float32)
        o_f = after(o_f, total)
        total = fold(
            o_f,
            [wa, wa_s, wb, wb_s],
            [unit_a(chip, core), unit_a(chip, 1 - core), unit_b(core), unit_b(1 - core)],
            total,
            jnp.float32,
        )
        wx = after(wx, total)
        wx_s = over_core(wx)
        return fold(o_f, [wx, wx_s], [unit_a(1 - chip, core), unit_a(1 - chip, 1 - core)], total, jnp.bfloat16)

    seq_spec = P(('dp', 'sp', 'hp'), None)
    in_specs = (seq_spec, P(None, 'hp'), P(None, 'hp'), P(None, 'hp'), P('hp', None))
    return jax.shard_map(device_fn, mesh=mesh, in_specs=in_specs, out_specs=seq_spec, check_vma=False)
```

profile of v0, /device:TPU:0, one launch (start us, length us, event | category | flops | bytes accessed | tf_op | source)
XLA Modules:
  0.0 348.9 jit_solution(4651953508705171121)
XLA Ops:
  0.0 3.3 slice.6
  3.3 3.3 collective-permute-start
  6.6 12.8 %shard_map.55.refs_1_.refs_2_ = bf16[512,2048]{1,0:T(8,128)(2,1)} custom-call(bf16[512,4096]{1,0:T(8,128)(2,1)S(1)} %copy-done, bf16[4096,2048]{1,0:T(8,128)(2,1)} %refs_0_.8), custom_call_target="tpu_custom_call" | custom-call | flops 8589934592 | bytes 16777216 | tf_op jit(solution)/shard_map/pallas_call | solution.py:142
  19.5 21.2 %shard_map.56 = (bf16[2048,512]{1,0:T(8,128)(2,1)}, bf16[512,2048]{1,0:T(8,128)(2,1)S(1)}) custom-call(bf16[512,4096]{1,0:T(8,128)(2,1)S(1)} %copy-done, bf16[4096,2048]{1,0:T(8,128)(2,1)} %refs_1_.5, bf16[4096,2048]{1,0:T(8,128)(2,1)} %refs_2_.3), custom_call_target="tpu_custom_call" | custom-call | flops 17179869184 | bytes 33554432 | tf_op jit(solution)/shard_map/pallas_call | solution.py:142
  44.5 3.9 %constant_dynamic-slice_fusion.1 = bf16[384,4096]{1,0:T(8,128)(2,1)} fusion(bf16[2048,4096]{1,0:T(8,128)(2,1)} %refs_0_.9, s32[]{:T(128)S(6)} %select_n.19), kind=kLoop, calls=%fused_computation.3 | loop fusion | bytes 6291460 | tf_op jit(solution)/shard_map/dynamic_slice | solution.py:216
  48.3 3.1 constant_dynamic-slice_fusion
  55.3 17.7 %shard_map.57 = (bf16[256,2048]{1,0:T(8,128)(2,1)S(1)}, bf16[2048,256]{1,0:T(8,128)(2,1)S(1)}, bf16[256,2048]{1,0:T(8,128)(2,1)S(1)}) custom-call(bf16[256,4096]{1,0:T(8,128)(2,1)S(1)} %collective-permute-done.x_ref, bf16[4096,2048]{1,0:T(8,128)(2,1)} %refs_0_.8, bf16[4096,2048]{1,0:T(8,128)(2,1)} %refs_1_.5, bf16[4096,2048]{1,0:T(8,128)(2,1)} %refs_2_.3), custom_call_target="tpu_custom_call" | custom-call | flops 12884901888 | bytes 50331648 | tf_op jit(solution)/shard_map/pallas_call | solution.py:142
  73.1 14.1 %shard_map.58 = (f32[16,1,512]{2,1,0:T(1,128)S(1)}, f32[16,1,512]{2,1,0:T(1,128)S(1)}, f32[2048,512]{1,0:T(8,128)}) custom-call(bf16[512,2048]{1,0:T(8,128)(2,1)S(1)} %copy-done.10, bf16[512,2048]{1,0:T(8,128)(2,1)} %shard_map.55.refs_1_.refs_2_, bf16[2048,512]{1,0:T(8,128)(2,1)} %get-tuple-element.50.refs_2_.refs_3_, ...), custom_call_target="tpu_custom_call" | custom-call | flops 8589934592 | bytes 10485760 | tf_op jit(solution)/shard_map/pallas_call | solution.py:88
  87.1 10.4 %collective-permute-done.1.x_ref = bf16[256,4096]{1,0:T(8,128)(2,1)} collective-permute-done((bf16[256,4096]{1,0:T(8,128)(2,1)}, bf16[256,4096]{1,0:T(8,128)(2,1)}, u32[]{:S(2)}, u32[]{:S(2)}) %collective-permute-start.1) | collective-permute-done | bytes 2097184 | tf_op jit(solution)/shard_map/ppermute | solution.py:203
  97.5 19.3 %shard_map.59 = (bf16[256,2048]{1,0:T(8,128)(2,1)S(1)}, bf16[2048,256]{1,0:T(8,128)(2,1)S(1)}, bf16[256,2048]{1,0:T(8,128)(2,1)S(1)}) custom-call(bf16[256,4096]{1,0:T(8,128)(2,1)} %collective-permute-done.1.x_ref, bf16[4096,2048]{1,0:T(8,128)(2,1)} %refs_0_.8, bf16[4096,2048]{1,0:T(8,128)(2,1)} %refs_1_.5, bf16[4096,2048]{1,0:T(8,128)(2,1)} %refs_2_.3), custom_call_target="tpu_custom_call" | custom-call | flops 12884901888 | bytes 50331648 | tf_op jit(solution)/shard_map/pallas_call | solution.py:142
  117.4 16.6 %collective-permute-done.9.refs_14_.refs_9_ = bf16[512,2048]{1,0:T(8,128)(2,1)} collective-permute-done((bf16[512,2048]{1,0:T(8,128)(2,1)}, bf16[512,2048]{1,0:T(8,128)(2,1)}, u32[]{:S(2)}, u32[]{:S(2)}) %collective-permute-start.9) | collective-permute-done | bytes 2097184 | tf_op jit(solution)/shard_map/ppermute | solution.py:204
  135.0 4.8 %collective-permute-done.8.refs_13_.refs_8_ = bf16[2048,256]{1,0:T(8,128)(2,1)S(1)} collective-permute-done((bf16[2048,256]{1,0:T(8,128)(2,1)S(1)}, bf16[2048,256]{1,0:T(8,128)(2,1)S(1)}, u32[]{:S(2)}, u32[]{:S(2)}) %collective-permute-start.8) | collective-permute-done | bytes 1048608 | tf_op jit(solution)/shard_map/ppermute | solution.py:205
  146.6 37.3 %shard_map.60 = (f32[16,1,512]{2,1,0:T(1,128)S(1)}, f32[16,1,512]{2,1,0:T(1,128)S(1)}, f32[2048,512]{1,0:T(8,128)}) custom-call(bf16[256,2048]{1,0:T(8,128)(2,1)S(1)} %get-tuple-element.71.refs_0_, bf16[256,2048]{1,0:T(8,128)(2,1)S(1)} %get-tuple-element.59.refs_1_, bf16[512,2048]{1,0:T(8,128)(2,1)} %shard_map.55.refs_1_.refs_2_, ...), custom_call_target="tpu_custom_call" | custom-call | flops 25769803776 | bytes 27262976 | tf_op jit(solution)/shard_map/pallas_call | solution.py:88
  183.9 5.9 %collective-permute-done.13.refs_2_.refs_1_ = bf16[256,2048]{1,0:T(8,128)(2,1)S(1)} collective-permute-done((bf16[256,2048]{1,0:T(8,128)(2,1)S(1)}, bf16[256,2048]{1,0:T(8,128)(2,1)S(1)}, u32[]{:S(2)}, u32[]{:S(2)}) %collective-permute-start.13) | collective-permute-done | bytes 1048608 | tf_op jit(solution)/shard_map/ppermute | solution.py:204
  192.3 30.7 %shard_map.61 = (f32[16,1,512]{2,1,0:T(1,128)S(1)}, f32[16,1,512]{2,1,0:T(1,128)S(1)}, f32[2048,512]{1,0:T(8,128)}) custom-call(bf16[512,2048]{1,0:T(8,128)(2,1)} %copy-done.9, bf16[256,2048]{1,0:T(8,128)(2,1)S(1)} %get-tuple-element.61.refs_6_.refs_1_, ...), custom_call_target="tpu_custom_call", output_to_operand_aliasing={{0}: (13, {}), {1}: (14, {}), {2}: (15, {})} | custom-call | flops 17179869184 | bytes 18874368 | tf_op jit(solution)/shard_map/pallas_call | solution.py:88
  224.6 10.0 %shard_map.62 = (f32[16,1,512]{2,1,0:T(1,128)S(1)}, f32[16,1,512]{2,1,0:T(1,128)S(1)}, f32[2048,512]{1,0:T(8,128)}) custom-call(bf16[256,2048]{1,0:T(8,128)(2,1)S(1)} %get-tuple-element.71.refs_0_, bf16[256,2048]{1,0:T(8,128)(2,1)S(1)} %get-tuple-element.59.refs_1_, ...), custom_call_target="tpu_custom_call", output_to_operand_aliasing={{0}: (6, {}), {1}: (7, {}), {2}: (8, {})} | custom-call | flops 4294967296 | bytes 6291456 | tf_op jit(solution)/shard_map/pallas_call | solution.py:88
  235.8 10.1 %shard_map.63 = (f32[16,1,512]{2,1,0:T(1,128)S(1)}, f32[16,1,512]{2,1,0:T(1,128)S(1)}, f32[2048,512]{1,0:T(8,128)}) custom-call(bf16[512,2048]{1,0:T(8,128)(2,1)} %copy-done.9, bf16[256,2048]{1,0:T(8,128)(2,1)S(1)} %collective-permute-done.13.refs_2_.refs_1_, ...), custom_call_target="tpu_custom_call", output_to_operand_aliasing={{0}: (5, {}), {1}: (6, {}), {2}: (7, {})} | custom-call | flops 4294967296 | bytes 6291456 | tf_op jit(solution)/shard_map/pallas_call | solution.py:88
  250.1 10.6 %shard_map.64 = bf16[512,2048]{1,0:T(8,128)(2,1)} custom-call(bf16[256,2048]{1,0:T(8,128)(2,1)S(1)} %get-tuple-element.71.refs_0_, bf16[256,2048]{1,0:T(8,128)(2,1)S(1)} %get-tuple-element.59.refs_1_, bf16[256,2048]{1,0:T(8,128)(2,1)S(1)} %collective-permute-done.4.refs_2_.refs_1_, bf16[256,2048]{1,0:T(8,128)(2,1)S(1)} %collective-permute-done.17.refs_3_.refs_2_, ...), custom_call_target="tpu_custom_call" | custom-call | flops 4294967296 | bytes 6291456 | tf_op jit(solution)/shard_map/pallas_call | solution.py:88
  263.4 10.6 %shard_map.65.lhs_ref = bf16[512,2048]{1,0:T(8,128)(2,1)} custom-call(bf16[512,2048]{1,0:T(8,128)(2,1)} %copy-done.9, bf16[256,2048]{1,0:T(8,128)(2,1)S(1)} %collective-permute-done.4.refs_2_.refs_1_, bf16[256,2048]{1,0:T(8,128)(2,1)S(1)} %collective-permute-done.17.refs_3_.refs_2_, bf16[2048,256]{1,0:T(8,128)(2,1)S(1)} %collective-permute-done.18.refs_4_.refs_3_, ...), custom_call_target="tpu_custom_call" | custom-call | flops 4294967296 | bytes 6291456 | tf_op jit(solution)/shard_map/pallas_call | solution.py:88
  275.7 15.2 %shard_map.66.refs_4_ = f32[512,4096]{1,0:T(8,128)} custom-call(s32[1]{0:T(128)} %constant.41.clone.1.first_unit, bf16[512,2048]{1,0:T(8,128)(2,1)S(1)} %copy-done.11, bf16[2048,4096]{1,0:T(8,128)(2,1)} %refs_0_.9), custom_call_target="tpu_custom_call" | custom-call | flops 8589934592 | bytes 16777216 | tf_op jit(solution)/shard_map/pallas_call | solution.py:170
  290.9 25.3 %collective-permute-done.20.lhs_ref = bf16[512,2048]{1,0:T(8,128)(2,1)S(1)} collective-permute-done((bf16[512,2048]{1,0:T(8,128)(2,1)}, bf16[512,2048]{1,0:T(8,128)(2,1)S(1)}, u32[]{:S(2)}, u32[]{:S(2)}) %collective-permute-start.20) | collective-permute-done | bytes 2097184 | tf_op jit(solution)/shard_map/ppermute | solution.py:203
  316.2 14.8 %shard_map.67.refs_2_ = f32[512,4096]{1,0:T(8,128)} custom-call(s32[4]{0:T(128)S(1)} %pad_add_fusion.1.first_unit, bf16[512,2048]{1,0:T(8,128)(2,1)S(1)} %collective-permute-done.20.lhs_ref, bf16[384,4096]{1,0:T(8,128)(2,1)} %collective-permute-done.21.refs_0_, bf16[384,4096]{1,0:T(8,128)(2,1)} %collective-permute-done.23.refs_1_, ...), custom_call_target="tpu_custom_call" | custom-call | flops 5368709120 | bytes 10485760 | tf_op jit(solution)/shard_map/pallas_call | solution.py:170
  331.2 5.9 %collective-permute-done.26.refs_1_ = bf16[384,4096]{1,0:T(8,128)(2,1)} collective-permute-done((bf16[384,4096]{1,0:T(8,128)(2,1)}, bf16[384,4096]{1,0:T(8,128)(2,1)}, u32[]{:S(2)}, u32[]{:S(2)}) %collective-permute-start.26) | collective-permute-done | bytes 3145760 | tf_op jit(solution)/shard_map/ppermute | solution.py:205
  337.1 11.8 %shard_map.68 = bf16[512,4096]{1,0:T(8,128)(2,1)} custom-call(s32[2]{0:T(128)S(1)} %pad_add_fusion.first_unit, bf16[512,2048]{1,0:T(8,128)(2,1)S(1)} %collective-permute-done.20.lhs_ref, bf16[384,4096]{1,0:T(8,128)(2,1)} %collective-permute-done.22.refs_0_, bf16[384,4096]{1,0:T(8,128)(2,1)} %collective-permute-done.26.refs_1_, f32[512,4096]{1,0:T(8,128)} %shard_map.67.refs_2_), custom_call_target="tpu_custom_call" | custom-call | flops 3221225472 | bytes 6291456 | tf_op jit(solution)/shard_map/pallas_call | solution.py:170
  (82 shorter events, 29.8 us)
Async XLA Ops:
  3.3 50.0 %collective-permute-start = (bf16[256,4096]{1,0:T(8,128)(2,1)}, bf16[256,4096]{1,0:T(8,128)(2,1)S(1)}, u32[]{:S(2)}, u32[]{:S(2)}) collective-permute-start(bf16[256,4096]{1,0:T(8,128)(2,1)} %slice.6), channel_id=1, source_target_pairs={{0,4},{4,0},{1,5},{5,1},{2,6},{6,2},{3,7},{7,3}} | collective-permute-start | bytes 6291464 | tf_op jit(solution)/shard_map/ppermute | solution.py:203
  40.7 32.4 %collective-permute-start.3 = (bf16[2048,512]{1,0:T(8,128)(2,1)}, bf16[2048,512]{1,0:T(8,128)(2,1)}, u32[]{:S(2)}, u32[]{:S(2)}) collective-permute-start(bf16[2048,512]{1,0:T(8,128)(2,1)} %get-tuple-element.50.refs_2_.refs_3_), channel_id=1, source_target_pairs={{0,1},{1,0},{2,3},{3,2},{4,5},{5,4},{6,7},{7,6}} | collective-permute-start | bytes 6291464 | tf_op jit(solution)/shard_map/ppermute | solution.py:205
  40.7 76.1 %collective-permute-start.10 = (bf16[2048,512]{1,0:T(8,128)(2,1)}, bf16[2048,512]{1,0:T(8,128)(2,1)}, u32[]{:S(2)}, u32[]{:S(2)}) collective-permute-start(bf16[2048,512]{1,0:T(8,128)(2,1)} %get-tuple-element.50.refs_2_.refs_3_), channel_id=1, source_target_pairs={{0,2},{1,3},{2,0},{3,1},{4,6},{5,7},{6,4},{7,5}} | collective-permute-start | bytes 6291464 | tf_op jit(solution)/shard_map/ppermute | solution.py:204
  42.2 30.8 %collective-permute-start.2 = (bf16[512,2048]{1,0:T(8,128)(2,1)}, bf16[512,2048]{1,0:T(8,128)(2,1)}, u32[]{:S(2)}, u32[]{:S(2)}) collective-permute-start(bf16[512,2048]{1,0:T(8,128)(2,1)} %shard_map.55.refs_1_.refs_2_), channel_id=1, source_target_pairs={{0,1},{1,0},{2,3},{3,2},{4,5},{5,4},{6,7},{7,6}} | collective-permute-start | bytes 6291464 | tf_op jit(solution)/shard_map/ppermute | solution.py:205
  44.0 53.5 %collective-permute-start.1 = (bf16[256,4096]{1,0:T(8,128)(2,1)}, bf16[256,4096]{1,0:T(8,128)(2,1)}, u32[]{:S(2)}, u32[]{:S(2)}) collective-permute-start(bf16[256,4096]{1,0:T(8,128)(2,1)} %slice.7), channel_id=1, source_target_pairs={{0,4},{4,0},{1,5},{5,1},{2,6},{6,2},{3,7},{7,3}} | collective-permute-start | bytes 6291464 | tf_op jit(solution)/shard_map/ppermute | solution.py:203
  53.3 80.7 %collective-permute-start.9 = (bf16[512,2048]{1,0:T(8,128)(2,1)}, bf16[512,2048]{1,0:T(8,128)(2,1)}, u32[]{:S(2)}, u32[]{:S(2)}) collective-permute-start(bf16[512,2048]{1,0:T(8,128)(2,1)} %shard_map.55.refs_1_.refs_2_), channel_id=1, source_target_pairs={{0,2},{1,3},{2,0},{3,1},{4,6},{5,7},{6,4},{7,5}} | collective-permute-start | bytes 6291464 | tf_op jit(solution)/shard_map/ppermute | solution.py:204
  116.8 17.7 %collective-permute-start.6 = (bf16[256,2048]{1,0:T(8,128)(2,1)S(1)}, bf16[256,2048]{1,0:T(8,128)(2,1)S(1)}, u32[]{:S(2)}, u32[]{:S(2)}) collective-permute-start(bf16[256,2048]{1,0:T(8,128)(2,1)S(1)} %get-tuple-element.60.refs_7_.refs_2_), channel_id=1, source_target_pairs={{0,1},{1,0},{2,3},{3,2},{4,5},{5,4},{6,7},{7,6}} | collective-permute-start | bytes 3145736 | tf_op jit(solution)/shard_map/ppermute | solution.py:205
  116.9 27.6 %collective-permute-start.12 = (bf16[2048,512]{1,0:T(8,128)(2,1)}, bf16[2048,512]{1,0:T(8,128)(2,1)S(1)}, u32[]{:S(2)}, u32[]{:S(2)}) collective-permute-start(bf16[2048,512]{1,0:T(8,128)(2,1)} %collective-permute-done.10.refs_15_.refs_10_), channel_id=1, source_target_pairs={{0,1},{1,0},{2,3},{3,2},{4,5},{5,4},{6,7},{7,6}} | collective-permute-start | bytes 6291464 | tf_op jit(solution)/shard_map/ppermute | solution.py:205
  134.0 11.1 %collective-permute-start.11 = (bf16[512,2048]{1,0:T(8,128)(2,1)}, bf16[512,2048]{1,0:T(8,128)(2,1)S(1)}, u32[]{:S(2)}, u32[]{:S(2)}) collective-permute-start(bf16[512,2048]{1,0:T(8,128)(2,1)} %collective-permute-done.9.refs_14_.refs_9_), channel_id=1, source_target_pairs={{0,1},{1,0},{2,3},{3,2},{4,5},{5,4},{6,7},{7,6}} | collective-permute-start | bytes 6291464 | tf_op jit(solution)/shard_map/ppermute | solution.py:205
  134.5 6.9 %collective-permute-start.5 = (bf16[256,2048]{1,0:T(8,128)(2,1)S(1)}, bf16[256,2048]{1,0:T(8,128)(2,1)S(1)}, u32[]{:S(2)}, u32[]{:S(2)}) collective-permute-start(bf16[256,2048]{1,0:T(8,128)(2,1)S(1)} %get-tuple-element.61.refs_6_.refs_1_), channel_id=1, source_target_pairs={{0,1},{1,0},{2,3},{3,2},{4,5},{5,4},{6,7},{7,6}} | collective-permute-start | bytes 3145736 | tf_op jit(solution)/shard_map/ppermute | solution.py:205
  134.5 8.5 %collective-permute-start.7 = (bf16[2048,256]{1,0:T(8,128)(2,1)S(1)}, bf16[2048,256]{1,0:T(8,128)(2,1)}, u32[]{:S(2)}, u32[]{:S(2)}) collective-permute-start(bf16[2048,256]{1,0:T(8,128)(2,1)S(1)} %get-tuple-element.62.refs_8_.refs_3_), channel_id=1, source_target_pairs={{0,1},{1,0},{2,3},{3,2},{4,5},{5,4},{6,7},{7,6}} | collective-permute-start | bytes 3145736 | tf_op jit(solution)/shard_map/ppermute | solution.py:205
  139.9 83.1 %collective-permute-start.21 = (bf16[384,4096]{1,0:T(8,128)(2,1)}, bf16[384,4096]{1,0:T(8,128)(2,1)}, u32[]{:S(2)}, u32[]{:S(2)}) collective-permute-start(bf16[384,4096]{1,0:T(8,128)(2,1)} %constant_dynamic-slice_fusion.1), channel_id=1, source_target_pairs={{0,4},{4,0},{1,5},{5,1},{2,6},{6,2},{3,7},{7,3}} | collective-permute-start | bytes 9437192 | tf_op jit(solution)/shard_map/ppermute | solution.py:203
  141.4 42.5 %collective-permute-start.15 = (bf16[2048,256]{1,0:T(8,128)(2,1)S(1)}, bf16[2048,256]{1,0:T(8,128)(2,1)S(1)}, u32[]{:S(2)}, u32[]{:S(2)}) collective-permute-start(bf16[2048,256]{1,0:T(8,128)(2,1)S(1)} %get-tuple-element.62.refs_8_.refs_3_), channel_id=1, source_target_pairs={{0,2},{1,3},{2,0},{3,1},{4,6},{5,7},{6,4},{7,5}} | collective-permute-start | bytes 3145736 | tf_op jit(solution)/shard_map/ppermute | solution.py:204
  143.0 46.9 %collective-permute-start.13 = (bf16[256,2048]{1,0:T(8,128)(2,1)S(1)}, bf16[256,2048]{1,0:T(8,128)(2,1)S(1)}, u32[]{:S(2)}, u32[]{:S(2)}) collective-permute-start(bf16[256,2048]{1,0:T(8,128)(2,1)S(1)} %get-tuple-element.61.refs_6_.refs_1_), channel_id=1, source_target_pairs={{0,2},{1,3},{2,0},{3,1},{4,6},{5,7},{6,4},{7,5}} | collective-permute-start | bytes 3145736 | tf_op jit(solution)/shard_map/ppermute | solution.py:204
  144.5 101.4 %collective-permute-start.18 = (bf16[2048,256]{1,0:T(8,128)(2,1)S(1)}, bf16[2048,256]{1,0:T(8,128)(2,1)S(1)}, u32[]{:S(2)}, u32[]{:S(2)}) collective-permute-start(bf16[2048,256]{1,0:T(8,128)(2,1)S(1)} %get-tuple-element.63.refs_9_.refs_4_), channel_id=1, source_target_pairs={{0,2},{1,3},{2,0},{3,1},{4,6},{5,7},{6,4},{7,5}} | collective-permute-start | bytes 3145736 | tf_op jit(solution)/shard_map/ppermute | solution.py:204
  145.0 101.1 %collective-permute-start.4 = (bf16[256,2048]{1,0:T(8,128)(2,1)S(1)}, bf16[256,2048]{1,0:T(8,128)(2,1)S(1)}, u32[]{:S(2)}, u32[]{:S(2)}) collective-permute-start(bf16[256,2048]{1,0:T(8,128)(2,1)S(1)} %get-tuple-element.60.refs_7_.refs_2_), channel_id=1, source_target_pairs={{0,2},{1,3},{2,0},{3,1},{4,6},{5,7},{6,4},{7,5}} | collective-permute-start | bytes 3145736 | tf_op jit(solution)/shard_map/ppermute | solution.py:204
  183.9 39.7 %collective-permute-start.16 = (bf16[2048,256]{1,0:T(8,128)(2,1)S(1)}, bf16[2048,256]{1,0:T(8,128)(2,1)S(1)}, u32[]{:S(2)}, u32[]{:S(2)}) collective-permute-start(bf16[2048,256]{1,0:T(8,128)(2,1)S(1)} %collective-permute-done.15.refs_4_.refs_3_), channel_id=1, source_target_pairs={{0,1},{1,0},{2,3},{3,2},{4,5},{5,4},{6,7},{7,6}} | collective-permute-start | bytes 3145736 | tf_op jit(solution)/shard_map/ppermute | solution.py:205
  189.9 33.7 %collective-permute-start.14 = (bf16[256,2048]{1,0:T(8,128)(2,1)S(1)}, bf16[256,2048]{1,0:T(8,128)(2,1)S(1)}, u32[]{:S(2)}, u32[]{:S(2)}) collective-permute-start(bf16[256,2048]{1,0:T(8,128)(2,1)S(1)} %collective-permute-done.13.refs_2_.refs_1_), channel_id=1, source_target_pairs={{0,1},{1,0},{2,3},{3,2},{4,5},{5,4},{6,7},{7,6}} | collective-permute-start | bytes 3145736 | tf_op jit(solution)/shard_map/ppermute | solution.py:205
  223.0 51.0 %collective-permute-start.24 = (bf16[256,4096]{1,0:T(8,128)(2,1)}, bf16[256,4096]{1,0:T(8,128)(2,1)}, u32[]{:S(2)}, u32[]{:S(2)}) collective-permute-start(bf16[256,4096]{1,0:T(8,128)(2,1)} %constant_dynamic-slice_fusion), channel_id=1, source_target_pairs={{0,4},{4,0},{1,5},{5,1},{2,6},{6,2},{3,7},{7,3}} | collective-permute-start | bytes 6291464 | tf_op jit(solution)/shard_map/ppermute | solution.py:203
  246.4 69.8 %collective-permute-start.23 = (bf16[384,4096]{1,0:T(8,128)(2,1)}, bf16[384,4096]{1,0:T(8,128)(2,1)}, u32[]{:S(2)}, u32[]{:S(2)}) collective-permute-start(bf16[384,4096]{1,0:T(8,128)(2,1)} %collective-permute-done.21.refs_0_), channel_id=1, source_target_pairs={{0,1},{1,0},{2,3},{3,2},{4,5},{5,4},{6,7},{7,6}} | collective-permute-start | bytes 9437192 | tf_op jit(solution)/shard_map/ppermute | solution.py:205
  246.7 84.4 %collective-permute-start.22 = (bf16[384,4096]{1,0:T(8,128)(2,1)}, bf16[384,4096]{1,0:T(8,128)(2,1)}, u32[]{:S(2)}, u32[]{:S(2)}) collective-permute-start(bf16[384,4096]{1,0:T(8,128)(2,1)} %collective-permute-done.21.refs_0_), channel_id=1, source_target_pairs={{0,2},{1,3},{2,0},{3,1},{4,6},{5,7},{6,4},{7,5}} | collective-permute-start | bytes 9437192 | tf_op jit(solution)/shard_map/ppermute | solution.py:204
  260.7 55.5 %collective-permute-start.20 = (bf16[512,2048]{1,0:T(8,128)(2,1)}, bf16[512,2048]{1,0:T(8,128)(2,1)S(1)}, u32[]{:S(2)}, u32[]{:S(2)}) collective-permute-start(bf16[512,2048]{1,0:T(8,128)(2,1)} %shard_map.64), channel_id=1, source_target_pairs={{0,4},{4,0},{1,5},{5,1},{2,6},{6,2},{3,7},{7,3}} | collective-permute-start | bytes 6291464 | tf_op jit(solution)/shard_map/ppermute | solution.py:203
  274.0 42.2 %collective-permute-start.25 = (bf16[256,4096]{1,0:T(8,128)(2,1)}, bf16[256,4096]{1,0:T(8,128)(2,1)}, u32[]{:S(2)}, u32[]{:S(2)}) collective-permute-start(bf16[256,4096]{1,0:T(8,128)(2,1)} %collective-permute-done.24.refs_2_), channel_id=1, source_target_pairs={{0,1},{1,0},{2,3},{3,2},{4,5},{5,4},{6,7},{7,6}} | collective-permute-start | bytes 6291464 | tf_op jit(solution)/shard_map/ppermute | solution.py:205
  331.1 6.0 %collective-permute-start.26 = (bf16[384,4096]{1,0:T(8,128)(2,1)}, bf16[384,4096]{1,0:T(8,128)(2,1)}, u32[]{:S(2)}, u32[]{:S(2)}) collective-permute-start(bf16[384,4096]{1,0:T(8,128)(2,1)} %collective-permute-done.22.refs_0_), channel_id=1, source_target_pairs={{0,1},{1,0},{2,3},{3,2},{4,5},{5,4},{6,7},{7,6}} | collective-permute-start | bytes 9437192 | tf_op jit(solution)/shard_map/ppermute | solution.py:205
  (19 other events, 106.7 us)
where the time goes:
time: 350 us; the launch traced here: 349 us
  Pallas kernels  236 us (67%)
  waiting for transfers between devices  74.1 us (21%)
  local copies, waits for them, and re-layouts  19.3 us (6%)
  starting transfers between devices  18.7 us (5%)
    pallas_call x7, Pallas kernels, attend(): pl.pallas_call(functools.partial(attend_kernel, tuple(shape), block, firs...  123 us
    pallas_call x4, Pallas kernels, project(): pl.pallas_call(functools.partial(project_kernel, tuple(flips), width), in...  71.1 us
    pallas_call x3, Pallas kernels, fold(): pl.pallas_call(functools.partial(fold_kernel, depths, base is not None),...  41.9 us
    ppermute x5, waiting for transfers between devices, device_fn(): over_y = lambda a: lax.ppermute(a, 'hp', hp_swap)  37.5 us
    ppermute x7, waiting for transfers between devices, device_fn(): over_x = lambda a: lax.ppermute(a, 'sp', x_swap)  22.5 us
    ppermute x15, waiting for transfers between devices, device_fn(): over_core = lambda a: lax.ppermute(a, 'sp', core_swap)  14.1 us
    ppermute x7, starting transfers between devices, device_fn(): over_x = lambda a: lax.ppermute(a, 'sp', x_swap)  10.1 us
    unnamed x32, local copies, waits for them, and re-layouts  7.52 us
  transfers between devices with their start and end apart: 27, of which 11 were waited for; matrix products, arithmetic and copies ran while one was open for 2% of the time, Pallas kernels for 64%

commit v1 on v0

v1 whole, which is shorter than its diff:
```python
import functools
import math

import jax
import jax.numpy as jnp
from jax import lax
from jax.experimental import pallas as pl
from jax.experimental.pallas import tpu as pltpu
from jax.sharding import PartitionSpec as P


HEAD_DIM = 128
EXP2_SCALE = math.log2(math.e) / math.sqrt(HEAD_DIM)


def attend_kernel(shape, heads, half, first, last, *refs):
    refs = list(refs)
    take = lambda n: [refs.pop(0) for _ in range(n)]
    q_refs = take(shape[0])
    groups = [([take(k) for k in widths], take(v)) for widths, v in shape[1:]]
    state_in = None if first else take(3)
    outs = refs
    at = lambda h: slice(h * HEAD_DIM, (h + 1) * HEAD_DIM)
    queries = [jnp.concatenate([r[:, at(h)] for r in q_refs], axis=0) for h in range(heads)]
    low = pl.program_id(0) < half

    def keys_of(piece, h):
        if len(piece) == 1:
            return piece[0][:, at(h)]
        return jnp.where(low, piece[0][:, at(h)], piece[1][:, at(h)])

    def scores_of(h, g):
        parts = [
            lax.dot_general(keys_of(k, h), queries[h], (((1,), (1,)), ((), ())), preferred_element_type=jnp.float32)
            for k in groups[g][0]
        ]
        return parts[0] if len(parts) == 1 else jnp.concatenate(parts, axis=0)

    items = [(h, g) for g in range(len(groups)) for h in range(heads)]
    depth = 2
    state = {} if first else {h: (state_in[0][h], state_in[1][h], state_in[2][at(h), :]) for h in range(heads)}
    ahead = [scores_of(*items[i]) for i in range(min(depth, len(items)))]
    for i, (h, g) in enumerate(items):
        if i + depth < len(items):
            ahead.append(scores_of(*items[i + depth]))
        scores = ahead.pop(0)
        new_max = jnp.max(scores, axis=0, keepdims=True) * EXP2_SCALE
        if h in state:
            new_max = jnp.maximum(state[h][0], new_max)
        probs = jnp.exp2(scores * EXP2_SCALE - new_max)
        part_sum = jnp.sum(probs, axis=0, keepdims=True)
        probs = probs.astype(jnp.bfloat16)
        part, row = None, 0
        for v in groups[g][1]:
            count = v.shape[1]
            piece = jnp.dot(v[at(h), :], probs[row:row + count], preferred_element_type=jnp.float32)
            part = piece if part is None else part + piece
            row += count
        if h in state:
            run_max, run_sum, acc = state[h]
            fade = jnp.exp2(run_max - new_max)
            state[h] = (new_max, run_sum * fade + part_sum, acc * fade + part)
        else:
            state[h] = (new_max, part_sum, part)
    for h in range(heads):
        run_max, run_sum, acc = state[h]
        if last:
            outs[0][:, at(h)] = (acc / run_sum).T.astype(jnp.bfloat16)
        else:
            outs[0][h], outs[1][h], outs[2][at(h), :] = run_max, run_sum, acc


def attend(queries, groups, state, last, block=1, part=(0, 1)):
    rows, all_heads = sum(q.shape[0] for q in queries), queries[0].shape[1] // HEAD_DIM
    heads = all_heads // part[1]
    width, steps = block * HEAD_DIM, heads // block
    half, base = all_heads // block // 2, part[0] * steps
    first = state is None
    state_specs = [
        pl.BlockSpec((block, 1, rows), lambda h: (h + base, 0, 0)),
        pl.BlockSpec((block, 1, rows), lambda h: (h + base, 0, 0)),
        pl.BlockSpec((width, rows), lambda h: (h + base, 0)),
    ]
    state_shapes = [jax.ShapeDtypeStruct((all_heads, 1, rows), jnp.float32)] * 2
    state_shapes.append(jax.ShapeDtypeStruct((all_heads * HEAD_DIM, rows), jnp.float32))
    tall = lambda a: pl.BlockSpec((a.shape[0], width), lambda h: (0, h + base))
    wide = lambda a: pl.BlockSpec((width, a.shape[1]), lambda h: (h + base, 0))
    operands, in_specs, shape, key_rows = list(queries), [tall(q) for q in queries], [len(queries)], 0
    for keys, values_t in groups:
        widths = []
        for k in keys:
            if not isinstance(k, tuple):
                operands.append(k)
                in_specs.append(tall(k))
                widths.append(1)
            elif part[1] == 2:
                operands.append(k[part[0]])
                in_specs.append(pl.BlockSpec((k[0].shape[0], width), lambda h: (0, h)))
                widths.append(1)
            else:
                operands += k
                in_specs.append(pl.BlockSpec((k[0].shape[0], width), lambda h: (0, jnp.minimum(h, half - 1))))
                in_specs.append(pl.BlockSpec((k[1].shape[0], width), lambda h: (0, jnp.maximum(h - half, 0))))
                widths.append(2)
        operands += values_t
        in_specs += [wide(v) for v in values_t]
        shape.append((tuple(widths), len(values_t)))
        key_rows += sum(v.shape[1] for v in values_t)
    count = len(operands)
    o_shape = jax.ShapeDtypeStruct((rows, heads * HEAD_DIM), jnp.bfloat16)
    return pl.pallas_call(
        functools.partial(attend_kernel, tuple(shape), block, half, first, last),
        grid=(steps,),
        in_specs=in_specs + ([] if first else state_specs),
        out_specs=pl.BlockSpec((rows, width), lambda h: (0, h)) if last else state_specs,
        out_shape=o_shape if last else state_shapes,
        input_output_aliases={} if first or last else {count + j: j for j in range(3)},
        cost_estimate=pl.CostEstimate(
            flops=8 * rows * key_rows * heads * HEAD_DIM,
            bytes_accessed=2 * heads * HEAD_DIM * (rows + 2 * key_rows),
            transcendentals=rows * key_rows * heads,
        ),
        compiler_params=pltpu.CompilerParams(vmem_limit_bytes=62 * 2**20),
    )(*operands, *(state or ()))


def project_kernel(flips, width, ranges, rows_of, x_ref, *refs):
    refs = list(refs)
    take = lambda n: [refs.pop(0) for _ in range(n)]
    count = len(flips)
    w_refs = take(count)
    source = take(1)[0] if rows_of and rows_of[0] is not None else None
    picks = rows_of[1] if rows_of else []
    o_refs, pick_refs = take(count), take(len(picks))
    ring, sems = take(2)
    stage = take(1)[0] if source is not None else None
    pick_sem = take(1)[0] if picks else None
    steps = [(stop - start) // width for start, stop in ranges]
    firsts = [sum(steps[:i]) for i in range(count)]

    def copy(i, step, slot):
        columns = pl.ds(pl.multiple_of(ranges[i][0] + step * width, width), width)
        return pltpu.make_async_copy(w_refs[i].at[:, columns], ring.at[slot], sems.at[slot])

    def fetch(n):
        for i in range(count):
            @pl.when(jnp.logical_and(n >= firsts[i], n < firsts[i] + steps[i]))
            def _():
                copy(i, n - firsts[i], lax.rem(n, 3)).start()

    def pick_copies(inward):
        copies, row = [], 0
        for j, (start, rows) in enumerate(picks):
            if source is None:
                copies.append(pltpu.make_async_copy(x_ref.at[pl.ds(start, rows)], pick_refs[j], pick_sem.at[j]))
                continue
            here = stage.at[pl.ds(row, rows)]
            row += rows
            if inward:
                there = source.at[pl.ds(pl.multiple_of(start(), 128), rows)]
                copies.append(pltpu.make_async_copy(there, here, pick_sem.at[j]))
            else:
                copies.append(pltpu.make_async_copy(here, pick_refs[j], pick_sem.at[j]))
        return copies

    fetch(jnp.int32(0))
    fetch(jnp.int32(1))
    for c in pick_copies(True):
        c.start()
    for i in range(count):
        def step(j, carry, i=i):
            n = firsts[i] + j
            slot = lax.rem(n, 3)
            fetch(n + 2)
            copy(i, j, slot).wait()
            block = jnp.dot(x_ref[...], ring[slot], preferred_element_type=jnp.float32)
            columns = pl.ds(pl.multiple_of(j * width, width), width)
            if flips[i]:
                o_refs[i][columns, :] = block.T.astype(jnp.bfloat16)
            else:
                o_refs[i][:, columns] = block.astype(jnp.bfloat16)
            return carry

        lax.fori_loop(0, steps[i], step, 0)
        if source is not None and i == 0:
            for inward, outward in zip(pick_copies(True), pick_copies(False)):
                inward.wait()
                outward.start()
    for c in pick_copies(False):
        c.wait()


def project(x, weights, flips, ranges=None, rows_of=None, width=512):
    rows, depth = x.shape
    ranges = ranges or [(0, w.shape[1]) for w in weights]
    counts = [stop - start for start, stop in ranges]
    shapes = [(c, rows) if f else (rows, c) for c, f in zip(counts, flips)]
    source, picks = rows_of or (None, [])
    any_spec, vmem_spec = pl.BlockSpec(memory_space=pl.ANY), pl.BlockSpec(memory_space=pltpu.VMEM)
    shapes += [(n, (x if source is None else source).shape[1]) for _, n in picks]
    scratch = [pltpu.VMEM((3, depth, width), jnp.bfloat16), pltpu.SemaphoreType.DMA((3,))]
    if source is not None:
        scratch.append(pltpu.VMEM((sum(n for _, n in picks), source.shape[1]), jnp.bfloat16))
    if picks:
        scratch.append(pltpu.SemaphoreType.DMA((len(picks),)))
    static = None if not picks else ('source' if source is not None else None, tuple(picks))
    return pl.pallas_call(
        functools.partial(project_kernel, tuple(flips), width, tuple(ranges), static),
        in_specs=[vmem_spec] + [any_spec] * (len(weights) + (source is not None)),
        out_specs=[vmem_spec] * len(weights) + [any_spec] * len(picks),
        out_shape=[jax.ShapeDtypeStruct(s, jnp.bfloat16) for s in shapes],
        scratch_shapes=scratch,
        cost_estimate=pl.CostEstimate(
            flops=2 * rows * depth * sum(counts),
            bytes_accessed=2 * depth * sum(counts),
            transcendentals=0,
        ),
        compiler_params=pltpu.CompilerParams(vmem_limit_bytes=62 * 2**20),
    )(x, *weights, *(() if source is None else (source,)))


def fold_kernel(depths, lhs_count, has_base, first_unit, *refs):
    lhs_refs, refs = refs[:lhs_count], refs[lhs_count:]
    lhs_ref, refs = refs[-1], refs[:-1]

    @pl.when(pl.program_id(0) == 0)
    def _():
        column = 0
        for ref in lhs_refs:
            lhs_ref[:, column:column + ref.shape[1]] = ref[...]
            column += ref.shape[1]

    if len(depths) == 1:
        left, right = lhs_ref[...], refs[0][...]
    else:
        starts = [pl.multiple_of(first_unit[i] * 128, 128) for i in range(len(depths))]
        left = jnp.concatenate([lhs_ref[:, pl.ds(s, d)] for s, d in zip(starts, depths)], axis=1)
        right = jnp.concatenate([refs[i][...] for i in range(len(depths))], axis=0)
    total = jnp.dot(left, right, preferred_element_type=jnp.float32)
    if has_base:
        total += refs[len(depths)][...]
    refs[-1][...] = total.astype(refs[-1].dtype)


def fold(lhs, pieces, units, base, dtype, part=(0, 1), width=512):
    rows, columns = lhs[0].shape[0], pieces[0].shape[1]
    depths = tuple(p.shape[0] for p in pieces)
    steps = columns // width // part[1]
    first = part[0] * steps
    here = lambda j, r: (0, j + first)
    out_spec = pl.BlockSpec((rows, width), here)
    inputs = [*lhs, *pieces] + ([] if base is None else [base])
    return pl.pallas_call(
        functools.partial(fold_kernel, depths, len(lhs), base is not None),
        grid_spec=pltpu.PrefetchScalarGridSpec(
            num_scalar_prefetch=1,
            grid=(steps,),
            in_specs=[pl.BlockSpec(a.shape, lambda j, r: (0, 0)) for a in lhs]
            + [pl.BlockSpec((d, width), here) for d in depths]
            + ([] if base is None else [pl.BlockSpec((rows, width), here)]),
            out_specs=out_spec,
            scratch_shapes=[pltpu.VMEM((rows, sum(a.shape[1] for a in lhs)), jnp.bfloat16)],
        ),
        out_shape=jax.ShapeDtypeStruct((rows, columns), dtype),
        input_output_aliases={len(inputs): 0} if part[1] > 1 else {},
        cost_estimate=pl.CostEstimate(
            flops=2 * rows * steps * width * sum(depths),
            bytes_accessed=2 * steps * width * sum(depths),
            transcendentals=0,
        ),
        compiler_params=pltpu.CompilerParams(vmem_limit_bytes=62 * 2**20),
    )(jnp.stack(units).astype(jnp.int32), *inputs)


def after(value, *tokens):
    return lax.optimization_barrier((value, *tokens))[0]


def solution(mesh):
    hp_swap = [(0, 1), (1, 0)]
    x_swap = [(0, 2), (1, 3), (2, 0), (3, 1)]
    core_swap = [(0, 1), (1, 0), (2, 3), (3, 2)]

    def device_fn(x_own, w_q, w_k, w_v, w_o):
        sp = lax.axis_index('sp')
        chip, core = sp // 2, sp % 2
        half = x_own.shape[0] // 2
        over_y = lambda a: lax.ppermute(a, 'hp', hp_swap)
        over_x = lambda a: lax.ppermute(a, 'sp', x_swap)
        over_core = lambda a: lax.ppermute(a, 'sp', core_swap)

        def proj(x, weights, flips, ranges=None, rows_of=None):
            return project(x, weights, flips, ranges, rows_of)

        unit_a = lambda chip_, core_: chip_ * 10 + core_ * 3
        unit_b = lambda core_: 6 + core_ * 2

        middle = w_k.shape[1] // 2
        x_f0 = over_y(x_own[:half])
        k_oa, x_half = proj(x_own, [w_k], [False], [(0, middle)], (None, [(half, half)]))
        k_xoa = over_x(k_oa)
        (k_ob,) = proj(after(x_own, k_oa), [w_k], [False], [(middle, 2 * middle)])
        k_xob = over_x(k_ob)
        x_f1 = over_y(x_half)
        first_a = lambda: unit_a(lax.axis_index('sp') // 2, lax.axis_index('sp') % 2) * 128
        first_b = lambda: unit_b(lax.axis_index('sp') % 2) * 128
        v_o, q_o, rows_a, rows_b = proj(
            after(x_own, k_ob), [w_v, w_q], [True, False], None, (w_o, [(first_a, 384), (first_b, 256)])
        )
        v_xo = over_x(v_o)
        wa = over_y(rows_a)
        wb = over_y(after(rows_b, rows_a))
        k_soa, k_sob, v_so = over_core(after(k_oa, v_o)), over_core(after(k_ob, v_o)), over_core(v_o)

        all_w, all_f = [w_k, w_v, w_q], [False, True, False]
        k_r0, v_r0, q_r0 = proj(after(x_f0, rows_a, rows_b), all_w, all_f)
        k_xr0, v_xr0 = over_x(k_r0), over_x(v_r0)
        k_sr0, v_sr0 = over_core(k_r0), over_core(v_r0)
        own, own_s = ([(k_oa, k_ob)], [v_o]), ([(k_soa, k_sob)], [v_so])
        state_o = attend([after(q_o, q_r0)], [own, own_s], None, False, 4)

        k_r1, v_r1, q_r1 = proj(after(x_f1, state_o[0]), all_w, all_f)
        k_xr1, v_xr1 = over_x(k_r1), over_x(v_r1)
        k_sr1, v_sr1 = over_core(k_r1), over_core(v_r1)
        k_sxoa, k_sxob = over_core(after(k_xoa, q_r0)), over_core(after(k_xob, q_r0))
        v_sxo = over_core(after(v_xo, v_r1))
        far, far_s = ([k_r0, k_r1], [v_r0, v_r1]), ([k_sr0, k_sr1], [v_sr0, v_sr1])
        xo, xo_s = ([(k_xoa, k_xob)], [v_xo]), ([(k_sxoa, k_sxob)], [v_sxo])
        state_r = attend([q_r0, q_r1], [own, own_s, far], None, False, 2)
        state_o = attend([after(q_o, state_r[0])], [far, far_s, xo, xo_s], state_o, False, 2)
        k_sxr0, v_sxr0 = over_core(after(k_xr0, state_o[0])), over_core(after(v_xr0, state_o[0]))
        late = ([k_xr0, k_sxr0], [v_xr0, v_sxr0])
        state_r = attend([after(q_r0, state_o[0]), q_r1], [far_s, xo, xo_s], state_r, False, 2)
        wx = over_x(after(wa, state_o[0]))
        wa_s = over_core(after(wa, state_o[0]))

        k_sxr1, v_sxr1 = over_core(after(k_xr1, state_r[0])), over_core(after(v_xr1, state_r[0]))
        latest = ([k_xr1, k_sxr1], [v_xr1, v_sxr1])
        o_ra = attend([q_r0, q_r1], [late, latest], state_r, True, 4, (0, 2))
        o_fa = over_y(o_ra)
        o_rb = attend([after(q_r0, o_ra), q_r1], [late, latest], state_r, True, 4, (1, 2))
        o_fb = over_y(o_rb)
        wb_s = over_core(after(wb, o_rb))
        o_own = attend([after(q_o, o_rb)], [late, latest], state_o, True, 4)
        total = fold([o_own], [w_o], [sp * 0], None, jnp.float32)
        wx_s = over_core(after(wx, total))
        units = [unit_a(chip, core), unit_a(chip, 1 - core), unit_b(core), unit_b(1 - core)]
        units += [unit_a(1 - chip, core), unit_a(1 - chip, 1 - core)]
        return fold([o_fa, after(o_fb, wx)], [wa, wa_s, wb, wb_s, wx, wx_s], units, total, jnp.bfloat16)

    seq_spec = P(('dp', 'sp', 'hp'), None)
    in_specs = (seq_spec, P(None, 'hp'), P(None, 'hp'), P(None, 'hp'), P('hp', None))
    return jax.shard_map(device_fn, mesh=mesh, in_specs=in_specs, out_specs=seq_spec, check_vma=False)
```

time: 350 us -> 401 us (1.15)
  waiting for transfers between devices: 74.1 us -> 123 us
  Pallas kernels: 236 us -> 251 us
  local copies, waits for them, and re-layouts: 19.3 us -> 5.8 us
    ppermute x7 -> x8, waiting for transfers between devices: 22.5 us -> 68.2 us  [device_fn(): over_x = lambda a: lax.ppermute(a, 'sp', x_swap)]
    ppermute x5 -> x6, waiting for transfers between devices: 37.5 us -> 53.9 us  [device_fn(): over_y = lambda a: lax.ppermute(a, 'hp', hp_swap)]
    pallas_call x14, Pallas kernels: 236 us -> 251 us  [the longest x7 130 us: attend(): pl.pallas_call(functools.partial(attend_kernel, tuple(shape), block, half...]
    ppermute x15 -> x17, waiting for transfers between devices: 14.1 us -> 0.89 us  [device_fn(): over_core = lambda a: lax.ppermute(a, 'sp', core_swap)]
    dynamic_slice x2 -> x0, local copies, waits for them, and re-layouts: 6.99 us -> none  [the longest x1 3.87 us: device_fn(): lax.dynamic_slice_in_dim(after(w_o, v_o), unit_a(chip, core) * 128, 384, 0)]
    unnamed x32 -> x16, local copies, waits for them, and re-layouts: 7.52 us -> 2.05 us
    ppermute x7 -> x8, starting transfers between devices: 10.1 us -> 9.6 us  [device_fn(): over_x = lambda a: lax.ppermute(a, 'sp', x_swap)]
  transfers between devices with their start and end apart: 27 -> 31, of which waited for: 11 -> 9; matrix products, arithmetic and copies ran while one was open for 2% -> 0% of each run, Pallas kernels for 64% -> 58%
where the time goes in v1:
time: 401 us
  Pallas kernels  251 us (63%)
  waiting for transfers between devices  123 us (31%)
  starting transfers between devices  20.4 us (5%)
  local copies, waits for them, and re-layouts  5.8 us (1%)
    pallas_call x7, Pallas kernels, attend(): pl.pallas_call(functools.partial(attend_kernel, tuple(shape), block, half...  130 us
    pallas_call x5, Pallas kernels, project(): pl.pallas_call(functools.partial(project_kernel, tuple(flips), width, tup...  87.2 us
    ppermute x8, waiting for transfers between devices, device_fn(): over_x = lambda a: lax.ppermute(a, 'sp', x_swap)  68.2 us
    ppermute x6, waiting for transfers between devices, device_fn(): over_y = lambda a: lax.ppermute(a, 'hp', hp_swap)  53.9 us
    pallas_call x2, Pallas kernels, fold(): pl.pallas_call(functools.partial(fold_kernel, depths, len(lhs), base is n...  33.7 us
    ppermute x8, starting transfers between devices, device_fn(): over_x = lambda a: lax.ppermute(a, 'sp', x_swap)  9.6 us
  transfers between devices with their start and end apart: 31, of which 9 were waited for; matrix products, arithmetic and copies ran while one was open for 0% of the time, Pallas kernels for 58%

profile of v1, /device:TPU:0, one launch (start us, length us, event | category | flops | bytes accessed | tf_op | source)
XLA Modules:
  0.0 400.5 jit_solution(9202170114559575244)
XLA Ops:
  0.0 3.1 slice.3
  3.1 3.3 collective-permute-start
  6.5 10.9 %shard_map.55 = (bf16[512,1024]{1,0:T(8,128)(2,1)}, bf16[256,4096]{1,0:T(8,128)(2,1)}) custom-call(bf16[512,4096]{1,0:T(8,128)(2,1)} %x_ref.3, bf16[4096,2048]{1,0:T(8,128)(2,1)} %refs_0_.9), custom_call_target="tpu_custom_call" | custom-call | flops 4294967296 | bytes 8388608 | tf_op jit(solution)/shard_map/pallas_call | solution.py:207
  17.3 10.0 %shard_map.56.refs_2_.refs_3_ = bf16[512,1024]{1,0:T(8,128)(2,1)} custom-call(bf16[512,4096]{1,0:T(8,128)(2,1)} %x_ref.3, bf16[4096,2048]{1,0:T(8,128)(2,1)} %refs_0_.9), custom_call_target="tpu_custom_call" | custom-call | flops 4294967296 | bytes 8388608 | tf_op jit(solution)/shard_map/pallas_call | solution.py:207
  27.4 25.5 %shard_map.57 = (bf16[2048,512]{1,0:T(8,128)(2,1)}, bf16[512,2048]{1,0:T(8,128)(2,1)}, bf16[384,4096]{1,0:T(8,128)(2,1)}, bf16[256,4096]{1,0:T(8,128)(2,1)}) custom-call(bf16[512,4096]{1,0:T(8,128)(2,1)} %x_ref.3, bf16[4096,2048]{1,0:T(8,128)(2,1)} %refs_1_.6, bf16[4096,2048]{1,0:T(8,128)(2,1)} %refs_2_.5, bf16[2048,4096]{1,0:T(8,128)(2,1)} %refs_1_.7), custom_call_target="tpu_custom_call" | custom-call | flops 17179869184 | bytes 33554432 | tf_op jit(solution)/shard_map/pallas_call | solution.py:207
  53.0 2.0 collective-permute-start.12
  55.5 20.3 %shard_map.58 = (bf16[256,2048]{1,0:T(8,128)(2,1)}, bf16[2048,256]{1,0:T(8,128)(2,1)}, bf16[256,2048]{1,0:T(8,128)(2,1)}) custom-call(bf16[256,4096]{1,0:T(8,128)(2,1)} %collective-permute-done.x_ref, bf16[4096,2048]{1,0:T(8,128)(2,1)} %refs_0_.9, bf16[4096,2048]{1,0:T(8,128)(2,1)} %refs_1_.6, bf16[4096,2048]{1,0:T(8,128)(2,1)} %refs_2_.5), custom_call_target="tpu_custom_call" | custom-call | flops 12884901888 | bytes 50331648 | tf_op jit(solution)/shard_map/pallas_call | solution.py:207
  77.9 14.8 %shard_map.59 = (f32[16,1,512]{2,1,0:T(1,128)}, f32[16,1,512]{2,1,0:T(1,128)}, f32[2048,512]{1,0:T(8,128)}) custom-call(bf16[512,2048]{1,0:T(8,128)(2,1)} %get-tuple-element.95.refs_0_, bf16[512,1024]{1,0:T(8,128)(2,1)} %get-tuple-element.63.refs_1_.refs_2_, bf16[512,1024]{1,0:T(8,128)(2,1)} %shard_map.56.refs_2_.refs_3_, ...), custom_call_target="tpu_custom_call" | custom-call | flops 8589934592 | bytes 10485760 | tf_op jit(solution)/shard_map/pallas_call | solution.py:111
  92.6 8.6 %collective-permute-done.1.x_ref = bf16[256,4096]{1,0:T(8,128)(2,1)} collective-permute-done((bf16[256,4096]{1,0:T(8,128)(2,1)}, bf16[256,4096]{1,0:T(8,128)(2,1)}, u32[]{:S(2)}, u32[]{:S(2)}) %collective-permute-start.1) | collective-permute-done | bytes 2097184 | tf_op jit(solution)/shard_map/ppermute | solution.py:288
  101.3 20.5 %shard_map.60 = (bf16[256,2048]{1,0:T(8,128)(2,1)}, bf16[2048,256]{1,0:T(8,128)(2,1)}, bf16[256,2048]{1,0:T(8,128)(2,1)}) custom-call(bf16[256,4096]{1,0:T(8,128)(2,1)} %collective-permute-done.1.x_ref, bf16[4096,2048]{1,0:T(8,128)(2,1)} %refs_0_.9, bf16[4096,2048]{1,0:T(8,128)(2,1)} %refs_1_.6, bf16[4096,2048]{1,0:T(8,128)(2,1)} %refs_2_.5), custom_call_target="tpu_custom_call" | custom-call | flops 12884901888 | bytes 50331648 | tf_op jit(solution)/shard_map/pallas_call | solution.py:207
  124.8 21.4 %collective-permute-done.10.refs_9_.refs_6_ = bf16[512,1024]{1,0:T(8,128)(2,1)} collective-permute-done((bf16[512,1024]{1,0:T(8,128)(2,1)}, bf16[512,1024]{1,0:T(8,128)(2,1)}, u32[]{:S(2)}, u32[]{:S(2)}) %collective-permute-start.10) | collective-permute-done | bytes 1048608 | tf_op jit(solution)/shard_map/ppermute | solution.py:289
  149.6 21.2 %shard_map.61 = (f32[16,1,512]{2,1,0:T(1,128)}, f32[16,1,512]{2,1,0:T(1,128)}, f32[2048,512]{1,0:T(8,128)}) custom-call(bf16[256,2048]{1,0:T(8,128)(2,1)} %get-tuple-element.90.refs_0_, bf16[256,2048]{1,0:T(8,128)(2,1)} %get-tuple-element.67.refs_1_, bf16[512,1024]{1,0:T(8,128)(2,1)} %get-tuple-element.63.refs_1_.refs_2_, ...), custom_call_target="tpu_custom_call" | custom-call | flops 12884901888 | bytes 14680064 | tf_op jit(solution)/shard_map/pallas_call | solution.py:111
  174.9 31.4 %shard_map.62 = (f32[16,1,512]{2,1,0:T(1,128)}, f32[16,1,512]{2,1,0:T(1,128)}, f32[2048,512]{1,0:T(8,128)}) custom-call(bf16[512,2048]{1,0:T(8,128)(2,1)} %get-tuple-element.95.refs_0_, bf16[256,2048]{1,0:T(8,128)(2,1)} %get-tuple-element.68.refs_8_.refs_1_, ...), custom_call_target="tpu_custom_call", output_to_operand_aliasing={{0}: (15, {}), {1}: (16, {}), {2}: (17, {})} | custom-call | flops 17179869184 | bytes 18874368 | tf_op jit(solution)/shard_map/pallas_call | solution.py:111
  206.4 24.4 %shard_map.63 = (f32[16,1,512]{2,1,0:T(1,128)}, f32[16,1,512]{2,1,0:T(1,128)}, f32[2048,512]{1,0:T(8,128)}) custom-call(bf16[256,2048]{1,0:T(8,128)(2,1)} %get-tuple-element.90.refs_0_, bf16[256,2048]{1,0:T(8,128)(2,1)} %get-tuple-element.67.refs_1_, ...), custom_call_target="tpu_custom_call", output_to_operand_aliasing={{0}: (12, {}), {1}: (13, {}), {2}: (14, {})} | custom-call | flops 12884901888 | bytes 14680064 | tf_op jit(solution)/shard_map/pallas_call | solution.py:111
  231.3 10.8 %collective-permute-done.17.refs_4_.refs_3_ = bf16[2048,256]{1,0:T(8,128)(2,1)} collective-permute-done((bf16[2048,256]{1,0:T(8,128)(2,1)}, bf16[2048,256]{1,0:T(8,128)(2,1)}, u32[]{:S(2)}, u32[]{:S(2)}) %collective-permute-start.17) | collective-permute-done | bytes 1048608 | tf_op jit(solution)/shard_map/ppermute | solution.py:289
  242.2 21.7 %collective-permute-done.5.refs_2_.refs_1_ = bf16[256,2048]{1,0:T(8,128)(2,1)} collective-permute-done((bf16[256,2048]{1,0:T(8,128)(2,1)S(1)}, bf16[256,2048]{1,0:T(8,128)(2,1)}, u32[]{:S(2)}, u32[]{:S(2)}) %collective-permute-start.5) | collective-permute-done | bytes 1048608 | tf_op jit(solution)/shard_map/ppermute | solution.py:289
  267.7 10.5 %shard_map.64 = bf16[512,1024]{1,0:T(8,128)(2,1)} custom-call(bf16[256,2048]{1,0:T(8,128)(2,1)} %get-tuple-element.90.refs_0_, bf16[256,2048]{1,0:T(8,128)(2,1)} %get-tuple-element.67.refs_1_, bf16[256,2048]{1,0:T(8,128)(2,1)} %collective-permute-done.5.refs_2_.refs_1_, bf16[256,2048]{1,0:T(8,128)(2,1)} %copy-done.7, ...), custom_call_target="tpu_custom_call" | custom-call | flops 4294967296 | bytes 5242880 | tf_op jit(solution)/shard_map/pallas_call | solution.py:111
  278.2 10.3 %shard_map.65 = bf16[512,1024]{1,0:T(8,128)(2,1)} custom-call(bf16[256,2048]{1,0:T(8,128)(2,1)} %get-tuple-element.90.refs_0_, bf16[256,2048]{1,0:T(8,128)(2,1)} %get-tuple-element.67.refs_1_, bf16[256,2048]{1,0:T(8,128)(2,1)} %collective-permute-done.5.refs_2_.refs_1_, bf16[256,2048]{1,0:T(8,128)(2,1)} %copy-done.7, ...), custom_call_target="tpu_custom_call" | custom-call | flops 4294967296 | bytes 5242880 | tf_op jit(solution)/shard_map/pallas_call | solution.py:111
  288.5 17.7 %shard_map.66.refs_0_ = bf16[512,2048]{1,0:T(8,128)(2,1)} custom-call(bf16[512,2048]{1,0:T(8,128)(2,1)} %get-tuple-element.95.refs_0_, bf16[256,2048]{1,0:T(8,128)(2,1)} %collective-permute-done.5.refs_2_.refs_1_, bf16[256,2048]{1,0:T(8,128)(2,1)} %copy-done.7, bf16[2048,256]{1,0:T(8,128)(2,1)} %collective-permute-done.17.refs_4_.refs_3_, ...), custom_call_target="tpu_custom_call" | custom-call | flops 8589934592 | bytes 10485760 | tf_op jit(solution)/shard_map/pallas_call | solution.py:111
  306.2 16.2 %shard_map.67.refs_8_ = f32[512,4096]{1,0:T(8,128)} custom-call(s32[1]{0:T(128)} %constant.36.clone.1.first_unit, bf16[512,2048]{1,0:T(8,128)(2,1)} %shard_map.66.refs_0_, bf16[2048,4096]{1,0:T(8,128)(2,1)} %refs_1_.7), custom_call_target="tpu_custom_call" | custom-call | flops 8589934592 | bytes 16777216 | tf_op jit(solution)/shard_map/pallas_call | solution.py:253
  322.4 12.3 %collective-permute-done.26.refs_6_ = bf16[384,4096]{1,0:T(8,128)(2,1)} collective-permute-done((bf16[384,4096]{1,0:T(8,128)(2,1)}, bf16[384,4096]{1,0:T(8,128)(2,1)}, u32[]{:S(2)}, u32[]{:S(2)}) %collective-permute-start.26) | collective-permute-done | bytes 3145760 | tf_op jit(solution)/shard_map/ppermute | solution.py:289
  337.8 23.6 %collective-permute-done.24.refs_1_ = bf16[512,1024]{1,0:T(8,128)(2,1)S(1)} collective-permute-done((bf16[512,1024]{1,0:T(8,128)(2,1)}, bf16[512,1024]{1,0:T(8,128)(2,1)S(1)}, u32[]{:S(2)}, u32[]{:S(2)}) %collective-permute-start.24) | collective-permute-done | bytes 1048608 | tf_op jit(solution)/shard_map/ppermute | solution.py:288
  361.4 21.6 %collective-permute-done.23.refs_0_ = bf16[512,1024]{1,0:T(8,128)(2,1)} collective-permute-done((bf16[512,1024]{1,0:T(8,128)(2,1)S(1)}, bf16[512,1024]{1,0:T(8,128)(2,1)}, u32[]{:S(2)}, u32[]{:S(2)}) %collective-permute-start.23) | collective-permute-done | bytes 1048608 | tf_op jit(solution)/shard_map/ppermute | solution.py:288
  383.1 17.5 %shard_map.68 = bf16[512,4096]{1,0:T(8,128)(2,1)} custom-call(s32[6]{0:T(128)} %stack.27.first_unit, bf16[512,1024]{1,0:T(8,128)(2,1)} %collective-permute-done.23.refs_0_, bf16[512,1024]{1,0:T(8,128)(2,1)} %copy-done.3, bf16[384,4096]{1,0:T(8,128)(2,1)} %collective-permute-done.25.refs_2_, bf16[384,4096]{1,0:T(8,128)(2,1)} %collective-permute-done.27.refs_3_, ...), custom_call_target="tpu_custom_call" | custom-call | flops 8589934592 | bytes 16777216 | tf_op jit(solution)/shard_map/pallas_call | solution.py:253
  (70 shorter events, 20.6 us)
Async XLA Ops:
  3.1 51.8 %collective-permute-start = (bf16[256,4096]{1,0:T(8,128)(2,1)}, bf16[256,4096]{1,0:T(8,128)(2,1)}, u32[]{:S(2)}, u32[]{:S(2)}) collective-permute-start(bf16[256,4096]{1,0:T(8,128)(2,1)} %slice.3), channel_id=1, source_target_pairs={{0,4},{4,0},{1,5},{5,1},{2,6},{6,2},{3,7},{7,3}} | collective-permute-start | bytes 6291464 | tf_op jit(solution)/shard_map/ppermute | solution.py:288
  52.9 25.0 %collective-permute-start.4 = (bf16[2048,512]{1,0:T(8,128)(2,1)}, bf16[2048,512]{1,0:T(8,128)(2,1)}, u32[]{:S(2)}, u32[]{:S(2)}) collective-permute-start(bf16[2048,512]{1,0:T(8,128)(2,1)} %get-tuple-element.62.refs_3_.refs_4_), channel_id=1, source_target_pairs={{0,1},{1,0},{2,3},{3,2},{4,5},{5,4},{6,7},{7,6}} | collective-permute-start | bytes 6291464 | tf_op jit(solution)/shard_map/ppermute | solution.py:290
  52.9 48.3 %collective-permute-start.1 = (bf16[256,4096]{1,0:T(8,128)(2,1)}, bf16[256,4096]{1,0:T(8,128)(2,1)}, u32[]{:S(2)}, u32[]{:S(2)}) collective-permute-start(bf16[256,4096]{1,0:T(8,128)(2,1)} %get-tuple-element.59), channel_id=1, source_target_pairs={{0,4},{4,0},{1,5},{5,1},{2,6},{6,2},{3,7},{7,3}} | collective-permute-start | bytes 6291464 | tf_op jit(solution)/shard_map/ppermute | solution.py:288
  53.0 71.3 %collective-permute-start.12 = (bf16[2048,512]{1,0:T(8,128)(2,1)}, bf16[2048,512]{1,0:T(8,128)(2,1)}, u32[]{:S(2)}, u32[]{:S(2)}) collective-permute-start(bf16[2048,512]{1,0:T(8,128)(2,1)} %get-tuple-element.62.refs_3_.refs_4_), channel_id=1, source_target_pairs={{0,2},{1,3},{2,0},{3,1},{4,6},{5,7},{6,4},{7,5}} | collective-permute-start | bytes 6291464 | tf_op jit(solution)/shard_map/ppermute | solution.py:289
  75.8 48.5 %collective-permute-start.11 = (bf16[512,1024]{1,0:T(8,128)(2,1)S(1)}, bf16[512,1024]{1,0:T(8,128)(2,1)}, u32[]{:S(2)}, u32[]{:S(2)}) collective-permute-start(bf16[512,1024]{1,0:T(8,128)(2,1)S(1)} %copy-done), channel_id=1, source_target_pairs={{0,2},{1,3},{2,0},{3,1},{4,6},{5,7},{6,4},{7,5}} | collective-permute-start | bytes 3145736 | tf_op jit(solution)/shard_map/ppermute | solution.py:289
  75.9 70.3 %collective-permute-start.10 = (bf16[512,1024]{1,0:T(8,128)(2,1)}, bf16[512,1024]{1,0:T(8,128)(2,1)}, u32[]{:S(2)}, u32[]{:S(2)}) collective-permute-start(bf16[512,1024]{1,0:T(8,128)(2,1)} %get-tuple-element.63.refs_1_.refs_2_), channel_id=1, source_target_pairs={{0,2},{1,3},{2,0},{3,1},{4,6},{5,7},{6,4},{7,5}} | collective-permute-start | bytes 3145736 | tf_op jit(solution)/shard_map/ppermute | solution.py:289
  121.8 26.2 %collective-permute-start.9 = (bf16[2048,256]{1,0:T(8,128)(2,1)}, bf16[2048,256]{1,0:T(8,128)(2,1)S(1)}, u32[]{:S(2)}, u32[]{:S(2)}) collective-permute-start(bf16[2048,256]{1,0:T(8,128)(2,1)} %get-tuple-element.71.refs_11_.refs_4_), channel_id=1, source_target_pairs={{0,1},{1,0},{2,3},{3,2},{4,5},{5,4},{6,7},{7,6}} | collective-permute-start | bytes 3145736 | tf_op jit(solution)/shard_map/ppermute | solution.py:290
  121.8 26.2 %collective-permute-start.7 = (bf16[256,2048]{1,0:T(8,128)(2,1)}, bf16[256,2048]{1,0:T(8,128)(2,1)S(1)}, u32[]{:S(2)}, u32[]{:S(2)}) collective-permute-start(bf16[256,2048]{1,0:T(8,128)(2,1)} %get-tuple-element.69.refs_9_.refs_2_), channel_id=1, source_target_pairs={{0,1},{1,0},{2,3},{3,2},{4,5},{5,4},{6,7},{7,6}} | collective-permute-start | bytes 3145736 | tf_op jit(solution)/shard_map/ppermute | solution.py:290
  124.3 50.1 %collective-permute-start.15 = (bf16[2048,512]{1,0:T(8,128)(2,1)}, bf16[2048,512]{1,0:T(8,128)(2,1)}, u32[]{:S(2)}, u32[]{:S(2)}) collective-permute-start(bf16[2048,512]{1,0:T(8,128)(2,1)} %collective-permute-done.12.refs_11_.refs_8_), channel_id=1, source_target_pairs={{0,1},{1,0},{2,3},{3,2},{4,5},{5,4},{6,7},{7,6}} | collective-permute-start | bytes 6291464 | tf_op jit(solution)/shard_map/ppermute | solution.py:290
  146.2 117.6 %collective-permute-start.25 = (bf16[384,4096]{1,0:T(8,128)(2,1)}, bf16[384,4096]{1,0:T(8,128)(2,1)}, u32[]{:S(2)}, u32[]{:S(2)}) collective-permute-start(bf16[384,4096]{1,0:T(8,128)(2,1)} %get-tuple-element.55), channel_id=1, source_target_pairs={{0,4},{4,0},{1,5},{5,1},{2,6},{6,2},{3,7},{7,3}} | collective-permute-start | bytes 9437192 | tf_op jit(solution)/shard_map/ppermute | solution.py:288
  148.5 24.4 %collective-permute-start.8 = (bf16[2048,256]{1,0:T(8,128)(2,1)}, bf16[2048,256]{1,0:T(8,128)(2,1)}, u32[]{:S(2)}, u32[]{:S(2)}) collective-permute-start(bf16[2048,256]{1,0:T(8,128)(2,1)} %get-tuple-element.70.refs_10_.refs_3_), channel_id=1, source_target_pairs={{0,1},{1,0},{2,3},{3,2},{4,5},{5,4},{6,7},{7,6}} | collective-permute-start | bytes 3145736 | tf_op jit(solution)/shard_map/ppermute | solution.py:290
  170.8 59.9 %collective-permute-start.21 = (bf16[2048,256]{1,0:T(8,128)(2,1)}, bf16[2048,256]{1,0:T(8,128)(2,1)}, u32[]{:S(2)}, u32[]{:S(2)}) collective-permute-start(bf16[2048,256]{1,0:T(8,128)(2,1)} %get-tuple-element.71.refs_11_.refs_4_), channel_id=1, source_target_pairs={{0,2},{1,3},{2,0},{3,1},{4,6},{5,7},{6,4},{7,5}} | collective-permute-start | bytes 3145736 | tf_op jit(solution)/shard_map/ppermute | solution.py:289
  172.4 58.5 %collective-permute-start.19 = (bf16[256,2048]{1,0:T(8,128)(2,1)}, bf16[256,2048]{1,0:T(8,128)(2,1)}, u32[]{:S(2)}, u32[]{:S(2)}) collective-permute-start(bf16[256,2048]{1,0:T(8,128)(2,1)} %get-tuple-element.69.refs_9_.refs_2_), channel_id=1, source_target_pairs={{0,2},{1,3},{2,0},{3,1},{4,6},{5,7},{6,4},{7,5}} | collective-permute-start | bytes 3145736 | tf_op jit(solution)/shard_map/ppermute | solution.py:289
  172.9 69.3 %collective-permute-start.17 = (bf16[2048,256]{1,0:T(8,128)(2,1)}, bf16[2048,256]{1,0:T(8,128)(2,1)}, u32[]{:S(2)}, u32[]{:S(2)}) collective-permute-start(bf16[2048,256]{1,0:T(8,128)(2,1)} %get-tuple-element.70.refs_10_.refs_3_), channel_id=1, source_target_pairs={{0,2},{1,3},{2,0},{3,1},{4,6},{5,7},{6,4},{7,5}} | collective-permute-start | bytes 3145736 | tf_op jit(solution)/shard_map/ppermute | solution.py:289
  174.4 89.5 %collective-permute-start.5 = (bf16[256,2048]{1,0:T(8,128)(2,1)S(1)}, bf16[256,2048]{1,0:T(8,128)(2,1)}, u32[]{:S(2)}, u32[]{:S(2)}) collective-permute-start(bf16[256,2048]{1,0:T(8,128)(2,1)S(1)} %copy-done.1), channel_id=1, source_target_pairs={{0,2},{1,3},{2,0},{3,1},{4,6},{5,7},{6,4},{7,5}} | collective-permute-start | bytes 3145736 | tf_op jit(solution)/shard_map/ppermute | solution.py:289
  230.8 34.5 %collective-permute-start.22 = (bf16[2048,256]{1,0:T(8,128)(2,1)}, bf16[2048,256]{1,0:T(8,128)(2,1)}, u32[]{:S(2)}, u32[]{:S(2)}) collective-permute-start(bf16[2048,256]{1,0:T(8,128)(2,1)} %collective-permute-done.21.refs_8_.refs_7_), channel_id=1, source_target_pairs={{0,1},{1,0},{2,3},{3,2},{4,5},{5,4},{6,7},{7,6}} | collective-permute-start | bytes 3145736 | tf_op jit(solution)/shard_map/ppermute | solution.py:290
  230.8 35.0 %collective-permute-start.20 = (bf16[256,2048]{1,0:T(8,128)(2,1)}, bf16[256,2048]{1,0:T(8,128)(2,1)}, u32[]{:S(2)}, u32[]{:S(2)}) collective-permute-start(bf16[256,2048]{1,0:T(8,128)(2,1)} %collective-permute-done.19.refs_6_.refs_5_), channel_id=1, source_target_pairs={{0,1},{1,0},{2,3},{3,2},{4,5},{5,4},{6,7},{7,6}} | collective-permute-start | bytes 3145736 | tf_op jit(solution)/shard_map/ppermute | solution.py:290
  263.8 70.8 %collective-permute-start.26 = (bf16[384,4096]{1,0:T(8,128)(2,1)}, bf16[384,4096]{1,0:T(8,128)(2,1)}, u32[]{:S(2)}, u32[]{:S(2)}) collective-permute-start(bf16[384,4096]{1,0:T(8,128)(2,1)} %collective-permute-done.25.refs_2_), channel_id=1, source_target_pairs={{0,2},{1,3},{2,0},{3,1},{4,6},{5,7},{6,4},{7,5}} | collective-permute-start | bytes 9437192 | tf_op jit(solution)/shard_map/ppermute | solution.py:289
  265.3 69.3 %collective-permute-start.28 = (bf16[256,4096]{1,0:T(8,128)(2,1)}, bf16[256,4096]{1,0:T(8,128)(2,1)}, u32[]{:S(2)}, u32[]{:S(2)}) collective-permute-start(bf16[256,4096]{1,0:T(8,128)(2,1)} %get-tuple-element.93), channel_id=1, source_target_pairs={{0,4},{4,0},{1,5},{5,1},{2,6},{6,2},{3,7},{7,3}} | collective-permute-start | bytes 6291464 | tf_op jit(solution)/shard_map/ppermute | solution.py:288
  265.9 117.2 %collective-permute-start.27 = (bf16[384,4096]{1,0:T(8,128)(2,1)}, bf16[384,4096]{1,0:T(8,128)(2,1)}, u32[]{:S(2)}, u32[]{:S(2)}) collective-permute-start(bf16[384,4096]{1,0:T(8,128)(2,1)} %collective-permute-done.25.refs_2_), channel_id=1, source_target_pairs={{0,1},{1,0},{2,3},{3,2},{4,5},{5,4},{6,7},{7,6}} | collective-permute-start | bytes 9437192 | tf_op jit(solution)/shard_map/ppermute | solution.py:290
  334.7 48.4 %collective-permute-start.30 = (bf16[384,4096]{1,0:T(8,128)(2,1)}, bf16[384,4096]{1,0:T(8,128)(2,1)}, u32[]{:S(2)}, u32[]{:S(2)}) collective-permute-start(bf16[384,4096]{1,0:T(8,128)(2,1)} %collective-permute-done.26.refs_6_), channel_id=1, source_target_pairs={{0,1},{1,0},{2,3},{3,2},{4,5},{5,4},{6,7},{7,6}} | collective-permute-start | bytes 9437192 | tf_op jit(solution)/shard_map/ppermute | solution.py:290
  334.7 48.4 %collective-permute-start.29 = (bf16[256,4096]{1,0:T(8,128)(2,1)}, bf16[256,4096]{1,0:T(8,128)(2,1)}, u32[]{:S(2)}, u32[]{:S(2)}) collective-permute-start(bf16[256,4096]{1,0:T(8,128)(2,1)} %collective-permute-done.28.refs_4_), channel_id=1, source_target_pairs={{0,1},{1,0},{2,3},{3,2},{4,5},{5,4},{6,7},{7,6}} | collective-permute-start | bytes 6291464 | tf_op jit(solution)/shard_map/ppermute | solution.py:290
  335.2 26.2 %collective-permute-start.24 = (bf16[512,1024]{1,0:T(8,128)(2,1)}, bf16[512,1024]{1,0:T(8,128)(2,1)S(1)}, u32[]{:S(2)}, u32[]{:S(2)}) collective-permute-start(bf16[512,1024]{1,0:T(8,128)(2,1)} %shard_map.65), channel_id=1, source_target_pairs={{0,4},{4,0},{1,5},{5,1},{2,6},{6,2},{3,7},{7,3}} | collective-permute-start | bytes 3145736 | tf_op jit(solution)/shard_map/ppermute | solution.py:288
  335.5 47.6 %collective-permute-start.23 = (bf16[512,1024]{1,0:T(8,128)(2,1)S(1)}, bf16[512,1024]{1,0:T(8,128)(2,1)}, u32[]{:S(2)}, u32[]{:S(2)}) collective-permute-start(bf16[512,1024]{1,0:T(8,128)(2,1)S(1)} %copy-done.2), channel_id=1, source_target_pairs={{0,4},{4,0},{1,5},{5,1},{2,6},{6,2},{3,7},{7,3}} | collective-permute-start | bytes 3145736 | tf_op jit(solution)/shard_map/ppermute | solution.py:288
  (15 other events, 247.5 us)

commit v2 on v1

--- a/solution.py
+++ b/solution.py
@@ -13,16 +13,17 @@
 EXP2_SCALE = math.log2(math.e) / math.sqrt(HEAD_DIM)
 
 
-def attend_kernel(shape, heads, half, first, last, *refs):
+def attend_kernel(shape, heads, split, first, last, scalars, *refs):
     refs = list(refs)
     take = lambda n: [refs.pop(0) for _ in range(n)]
+    take(scalars)
     q_refs = take(shape[0])
     groups = [([take(k) for k in widths], take(v)) for widths, v in shape[1:]]
     state_in = None if first else take(3)
     outs = refs
     at = lambda h: slice(h * HEAD_DIM, (h + 1) * HEAD_DIM)
     queries = [jnp.concatenate([r[:, at(h)] for r in q_refs], axis=0) for h in range(heads)]
-    low = pl.program_id(0) < half
+    low = pl.program_id(0) < split
 
     def keys_of(piece, h):
         if len(piece) == 1:
@@ -70,21 +71,23 @@
             outs[0][h], outs[1][h], outs[2][at(h), :] = run_max, run_sum, acc
 
 
-def attend(queries, groups, state, last, block=1, part=(0, 1)):
+def attend(queries, groups, state, last, block=1, part=None):
     rows, all_heads = sum(q.shape[0] for q in queries), queries[0].shape[1] // HEAD_DIM
-    heads = all_heads // part[1]
+    heads = all_heads if part is None else all_heads // 2
     width, steps = block * HEAD_DIM, heads // block
-    half, base = all_heads // block // 2, part[0] * steps
+    split, offset = 0, () if part is None else (jnp.full((1,), part * steps, jnp.int32),)
+    shift = lambda h, o: h + o[0][0] if o else h
+    spec = lambda block, index: pl.BlockSpec(block, lambda h, *o: index(h, shift(h, o)))
     first = state is None
     state_specs = [
-        pl.BlockSpec((block, 1, rows), lambda h: (h + base, 0, 0)),
-        pl.BlockSpec((block, 1, rows), lambda h: (h + base, 0, 0)),
-        pl.BlockSpec((width, rows), lambda h: (h + base, 0)),
+        spec((block, 1, rows), lambda h, g: (g, 0, 0)),
+        spec((block, 1, rows), lambda h, g: (g, 0, 0)),
+        spec((width, rows), lambda h, g: (g, 0)),
     ]
     state_shapes = [jax.ShapeDtypeStruct((all_heads, 1, rows), jnp.float32)] * 2
     state_shapes.append(jax.ShapeDtypeStruct((all_heads * HEAD_DIM, rows), jnp.float32))
-    tall = lambda a: pl.BlockSpec((a.shape[0], width), lambda h: (0, h + base))
-    wide = lambda a: pl.BlockSpec((width, a.shape[1]), lambda h: (h + base, 0))
+    tall = lambda a: spec((a.shape[0], width), lambda h, g: (0, g))
+    wide = lambda a: spec((width, a.shape[1]), lambda h, g: (g, 0))
     operands, in_specs, shape, key_rows = list(queries), [tall(q) for q in queries], [len(queries)], 0
     for keys, values_t in groups:
         widths = []
@@ -93,14 +96,11 @@
                 operands.append(k)
                 in_specs.append(tall(k))
                 widths.append(1)
-            elif part[1] == 2:
-                operands.append(k[part[0]])
-                in_specs.append(pl.BlockSpec((k[0].shape[0], width), lambda h: (0, h)))
-                widths.append(1)
             else:
+                split = k[0].shape[1] // width
                 operands += k
-                in_specs.append(pl.BlockSpec((k[0].shape[0], width), lambda h: (0, jnp.minimum(h, half - 1))))
-                in_specs.append(pl.BlockSpec((k[1].shape[0], width), lambda h: (0, jnp.maximum(h - half, 0))))
+                in_specs.append(spec((k[0].shape[0], width), lambda h, g, s=split: (0, jnp.minimum(h, s - 1))))
+                in_specs.append(spec((k[1].shape[0], width), lambda h, g, s=split: (0, jnp.maximum(h - s, 0))))
                 widths.append(2)
         operands += values_t
         in_specs += [wide(v) for v in values_t]
@@ -109,19 +109,22 @@
     count = len(operands)
     o_shape = jax.ShapeDtypeStruct((rows, heads * HEAD_DIM), jnp.bfloat16)
     return pl.pallas_call(
-        functools.partial(attend_kernel, tuple(shape), block, half, first, last),
-        grid=(steps,),
-        in_specs=in_specs + ([] if first else state_specs),
-        out_specs=pl.BlockSpec((rows, width), lambda h: (0, h)) if last else state_specs,
+        functools.partial(attend_kernel, tuple(shape), block, split, first, last, len(offset)),
+        grid_spec=pltpu.PrefetchScalarGridSpec(
+            num_scalar_prefetch=len(offset),
+            grid=(steps,),
+            in_specs=in_specs + ([] if first else state_specs),
+            out_specs=spec((rows, width), lambda h, g: (0, h)) if last else state_specs,
+        ),
         out_shape=o_shape if last else state_shapes,
-        input_output_aliases={} if first or last else {count + j: j for j in range(3)},
+        input_output_aliases={} if first or last else {len(offset) + count + j: j for j in range(3)},
         cost_estimate=pl.CostEstimate(
             flops=8 * rows * key_rows * heads * HEAD_DIM,
             bytes_accessed=2 * heads * HEAD_DIM * (rows + 2 * key_rows),
             transcendentals=rows * key_rows * heads,
         ),
         compiler_params=pltpu.CompilerParams(vmem_limit_bytes=62 * 2**20),
-    )(*operands, *(state or ()))
+    )(*offset, *operands, *(state or ()))
 
 
 def project_kernel(flips, width, ranges, rows_of, x_ref, *refs):
@@ -219,57 +222,104 @@
     )(x, *weights, *(() if source is None else (source,)))
 
 
-def fold_kernel(depths, lhs_count, has_base, first_unit, *refs):
-    lhs_refs, refs = refs[:lhs_count], refs[lhs_count:]
-    lhs_ref, refs = refs[-1], refs[:-1]
-
-    @pl.when(pl.program_id(0) == 0)
-    def _():
-        column = 0
-        for ref in lhs_refs:
-            lhs_ref[:, column:column + ref.shape[1]] = ref[...]
-            column += ref.shape[1]
-
-    if len(depths) == 1:
-        left, right = lhs_ref[...], refs[0][...]
-    else:
-        starts = [pl.multiple_of(first_unit[i] * 128, 128) for i in range(len(depths))]
-        left = jnp.concatenate([lhs_ref[:, pl.ds(s, d)] for s, d in zip(starts, depths)], axis=1)
-        right = jnp.concatenate([refs[i][...] for i in range(len(depths))], axis=0)
-    total = jnp.dot(left, right, preferred_element_type=jnp.float32)
-    if has_base:
-        total += refs[len(depths)][...]
-    refs[-1][...] = total.astype(refs[-1].dtype)
-
-
-def fold(lhs, pieces, units, base, dtype, part=(0, 1), width=512):
-    rows, columns = lhs[0].shape[0], pieces[0].shape[1]
-    depths = tuple(p.shape[0] for p in pieces)
-    steps = columns // width // part[1]
-    first = part[0] * steps
-    here = lambda j, r: (0, j + first)
-    out_spec = pl.BlockSpec((rows, width), here)
-    inputs = [*lhs, *pieces] + ([] if base is None else [base])
+def fold_kernel(plan, width, has_base, *refs):
+    refs = list(refs)
+    take = lambda n: [refs.pop(0) for _ in range(n)]
+    chip, core = lax.axis_index('sp') // 2, lax.axis_index('sp') % 2
+    lhs_refs = take(max(p[1] for p in plan) + 1)
+    piece_refs = [take(1 if p[3] is None else 2) for p in plan]
+    base_ref = take(1)[0] if has_base else None
+    out_ref, left, right, right_sem, outs, out_sem = take(6)
+    bases, base_sem = take(2) if has_base else (None, None)
+    steps = out_ref.shape[1] // width
+    columns = lambda j: pl.ds(pl.multiple_of(j * width, width), width)
+
+    def fetches(j, slot):
+        copies, row = [], 0
+        for i, (depth, _, _, choice) in enumerate(plan):
+            here = right.at[slot, pl.ds(row, depth)]
+            versions = [pltpu.make_async_copy(r.at[:, columns(j)], here, right_sem.at[slot, i]) for r in piece_refs[i]]
+            copies.append((versions, choice))
+            row += depth
+        if has_base:
+            versions = [pltpu.make_async_copy(base_ref.at[:, columns(j)], bases.at[slot], base_sem.at[slot])]
+            copies.append((versions, None))
+        return copies
+
+    def fetch(j):
+        for versions, choice in fetches(j, lax.rem(j, 3)):
+            if choice is None:
+                versions[0].start()
+                continue
+            pl.when(choice(chip, core))(versions[0].start)
+            pl.when(jnp.logical_not(choice(chip, core)))(versions[1].start)
+
+    def store(j):
+        slot = lax.rem(j, 2)
+        return pltpu.make_async_copy(outs.at[slot], out_ref.at[:, columns(j)], out_sem.at[slot])
+
+    fetch(jnp.int32(0))
+    fetch(jnp.int32(1))
+    column = 0
+    for depth, which, start, _ in plan:
+        source = lhs_refs[which]
+        picked = pl.ds(pl.multiple_of(start(chip, core), 128), depth)
+        left[:, column:column + depth] = source[...] if source.shape[1] == depth else source[:, picked]
+        column += depth
+
+    def step(j, carry):
+        slot = lax.rem(j, 3)
+
+        @pl.when(j + 2 < steps)
+        def _():
+            fetch(j + 2)
+
+        for versions, _ in fetches(j, slot):
+            versions[0].wait()
+
+        total = jnp.dot(left[...], right[slot], preferred_element_type=jnp.float32)
+        if has_base:
+            total += bases[slot]
+
+        @pl.when(j >= 2)
+        def _():
+            store(j - 2).wait()
+
+        outs[lax.rem(j, 2)] = total.astype(out_ref.dtype)
+        store(j).start()
+        return carry
+
+    lax.fori_loop(0, steps, step, 0)
+    store(jnp.int32(steps - 2)).wait()
+    store(jnp.int32(steps - 1)).wait()
+
+
+def fold(lhs, pieces, base, dtype, width=512):
+    plan, arrays = [], []
+    for piece, which, start, choice in pieces:
+        versions = piece if isinstance(piece, tuple) else (piece,)
+        plan.append((versions[0].shape[0], which, start, choice))
+        arrays += versions
+    rows, columns, depth = lhs[0].shape[0], arrays[0].shape[1], sum(p[0] for p in plan)
+    any_spec, vmem_spec = pl.BlockSpec(memory_space=pl.ANY), pl.BlockSpec(memory_space=pltpu.VMEM)
+    scratch = [
+        pltpu.VMEM((rows, depth), jnp.bfloat16),
+        pltpu.VMEM((3, depth, width), jnp.bfloat16),
+        pltpu.SemaphoreType.DMA((3, len(plan))),
+        pltpu.VMEM((2, rows, width), dtype),
+        pltpu.SemaphoreType.DMA((2,)),
+    ]
+    if base is not None:
+        scratch += [pltpu.VMEM((3, rows, width), jnp.float32), pltpu.SemaphoreType.DMA((3,))]
     return pl.pallas_call(
-        functools.partial(fold_kernel, depths, len(lhs), base is not None),
-        grid_spec=pltpu.PrefetchScalarGridSpec(
-            num_scalar_prefetch=1,
-            grid=(steps,),
-            in_specs=[pl.BlockSpec(a.shape, lambda j, r: (0, 0)) for a in lhs]
-            + [pl.BlockSpec((d, width), here) for d in depths]
-            + ([] if base is None else [pl.BlockSpec((rows, width), here)]),
-            out_specs=out_spec,
-            scratch_shapes=[pltpu.VMEM((rows, sum(a.shape[1] for a in lhs)), jnp.bfloat16)],
-        ),
+        functools.partial(fold_kernel, tuple(plan), width, base is not None),
+        in_specs=[vmem_spec] * len(lhs) + [any_spec] * (len(arrays) + (base is not None)),
+        out_specs=any_spec,
         out_shape=jax.ShapeDtypeStruct((rows, columns), dtype),
-        input_output_aliases={len(inputs): 0} if part[1] > 1 else {},
-        cost_estimate=pl.CostEstimate(
-            flops=2 * rows * steps * width * sum(depths),
-            bytes_accessed=2 * steps * width * sum(depths),
-            transcendentals=0,
-        ),
+        scratch_shapes=scratch,
+        cost_estimate=pl.CostEstimate(flops=2 * rows * columns * depth, bytes_accessed=2 * columns * depth, transcendentals=0),
         compiler_params=pltpu.CompilerParams(vmem_limit_bytes=62 * 2**20),
-    )(jnp.stack(units).astype(jnp.int32), *inputs)
+    )(*lhs, *arrays, *(() if base is None else (base,)))
 
 
 def after(value, *tokens):
@@ -283,7 +333,7 @@
 
     def device_fn(x_own, w_q, w_k, w_v, w_o):
         sp = lax.axis_index('sp')
-        chip, core = sp // 2, sp % 2
+        chip = sp // 2
         half = x_own.shape[0] // 2
         over_y = lambda a: lax.ppermute(a, 'hp', hp_swap)
         over_x = lambda a: lax.ppermute(a, 'sp', x_swap)
@@ -295,58 +345,66 @@
         unit_a = lambda chip_, core_: chip_ * 10 + core_ * 3
         unit_b = lambda core_: 6 + core_ * 2
 
-        middle = w_k.shape[1] // 2
+        middle = w_k.shape[1] // 4
         x_f0 = over_y(x_own[:half])
         k_oa, x_half = proj(x_own, [w_k], [False], [(0, middle)], (None, [(half, half)]))
         k_xoa = over_x(k_oa)
-        (k_ob,) = proj(after(x_own, k_oa), [w_k], [False], [(middle, 2 * middle)])
+        (k_ob,) = proj(after(x_own, k_oa), [w_k], [False], [(middle, 4 * middle)])
         k_xob = over_x(k_ob)
         x_f1 = over_y(x_half)
         first_a = lambda: unit_a(lax.axis_index('sp') // 2, lax.axis_index('sp') % 2) * 128
+        first_a1 = lambda: first_a() + 256
         first_b = lambda: unit_b(lax.axis_index('sp') % 2) * 128
-        v_o, q_o, rows_a, rows_b = proj(
-            after(x_own, k_ob), [w_v, w_q], [True, False], None, (w_o, [(first_a, 384), (first_b, 256)])
+        v_o, q_o, rows_a0, rows_a1, rows_b = proj(
+            after(x_own, k_ob), [w_v, w_q], [True, False], None, (w_o, [(first_a, 256), (first_a1, 128), (first_b, 256)])
         )
         v_xo = over_x(v_o)
-        wa = over_y(rows_a)
-        wb = over_y(after(rows_b, rows_a))
+        wa0, wa1, wb = over_y(rows_a0), over_y(rows_a1), over_y(rows_b)
         k_soa, k_sob, v_so = over_core(after(k_oa, v_o)), over_core(after(k_ob, v_o)), over_core(v_o)
 
         all_w, all_f = [w_k, w_v, w_q], [False, True, False]
-        k_r0, v_r0, q_r0 = proj(after(x_f0, rows_a, rows_b), all_w, all_f)
+        k_r0, v_r0, q_r0 = proj(after(x_f0, rows_b), all_w, all_f)
         k_xr0, v_xr0 = over_x(k_r0), over_x(v_r0)
         k_sr0, v_sr0 = over_core(k_r0), over_core(v_r0)
         own, own_s = ([(k_oa, k_ob)], [v_o]), ([(k_soa, k_sob)], [v_so])
         state_o = attend([after(q_o, q_r0)], [own, own_s], None, False, 4)
 
-        k_r1, v_r1, q_r1 = proj(after(x_f1, state_o[0]), all_w, all_f)
+        k_r1, v_r1 = proj(after(x_f1, state_o[0]), [w_k, w_v], [False, True])
         k_xr1, v_xr1 = over_x(k_r1), over_x(v_r1)
         k_sr1, v_sr1 = over_core(k_r1), over_core(v_r1)
+        v_sxo = over_core(after(v_xo, v_r1))
+        (q_r1,) = proj(after(x_f1, v_r1), [w_q], [False])
         k_sxoa, k_sxob = over_core(after(k_xoa, q_r0)), over_core(after(k_xob, q_r0))
-        v_sxo = over_core(after(v_xo, v_r1))
         far, far_s = ([k_r0, k_r1], [v_r0, v_r1]), ([k_sr0, k_sr1], [v_sr0, v_sr1])
         xo, xo_s = ([(k_xoa, k_xob)], [v_xo]), ([(k_sxoa, k_sxob)], [v_sxo])
-        state_r = attend([q_r0, q_r1], [own, own_s, far], None, False, 2)
+        state_r = attend([q_r0, q_r1], [own, own_s, far, far_s, xo, xo_s], None, False, 2)
+        k_sxr0, v_sxr0 = over_core(after(k_xr0, state_r[0])), over_core(after(v_xr0, state_r[0]))
+        late = ([k_xr0, k_sxr0], [v_xr0, v_sxr0])
         state_o = attend([after(q_o, state_r[0])], [far, far_s, xo, xo_s], state_o, False, 2)
-        k_sxr0, v_sxr0 = over_core(after(k_xr0, state_o[0])), over_core(after(v_xr0, state_o[0]))
-        late = ([k_xr0, k_sxr0], [v_xr0, v_sxr0])
-        state_r = attend([after(q_r0, state_o[0]), q_r1], [far_s, xo, xo_s], state_r, False, 2)
-        wx = over_x(after(wa, state_o[0]))
-        wa_s = over_core(after(wa, state_o[0]))
-
-        k_sxr1, v_sxr1 = over_core(after(k_xr1, state_r[0])), over_core(after(v_xr1, state_r[0]))
+        wx0, wx1 = over_x(after(wa0, state_r[0])), over_x(after(wa1, state_o[0]))
+        wa0_s, wa1_s = over_core(after(wa0, state_r[0])), over_core(after(wa1, state_o[0]))
+
+        k_sxr1, v_sxr1 = over_core(after(k_xr1, state_o[0])), over_core(after(v_xr1, state_o[0]))
         latest = ([k_xr1, k_sxr1], [v_xr1, v_sxr1])
-        o_ra = attend([q_r0, q_r1], [late, latest], state_r, True, 4, (0, 2))
+        o_ra = attend([after(q_r0, state_o[0]), q_r1], [late, latest], state_r, True, 4, chip)
         o_fa = over_y(o_ra)
-        o_rb = attend([after(q_r0, o_ra), q_r1], [late, latest], state_r, True, 4, (1, 2))
+        o_rb = attend([after(q_r0, o_ra), q_r1], [late, latest], state_r, True, 4, 1 - chip)
         o_fb = over_y(o_rb)
         wb_s = over_core(after(wb, o_rb))
         o_own = attend([after(q_o, o_rb)], [late, latest], state_o, True, 4)
-        total = fold([o_own], [w_o], [sp * 0], None, jnp.float32)
-        wx_s = over_core(after(wx, total))
-        units = [unit_a(chip, core), unit_a(chip, 1 - core), unit_b(core), unit_b(1 - core)]
-        units += [unit_a(1 - chip, core), unit_a(1 - chip, 1 - core)]
-        return fold([o_fa, after(o_fb, wx)], [wa, wa_s, wb, wb_s, wx, wx_s], units, total, jnp.bfloat16)
+        near = lambda core_of, more: lambda x, c: (x * 2 + core_of(c) * 3 + more) * 128
+        away = lambda core_of, more: lambda x, c: ((1 - x) * 2 + core_of(c) * 3 + more) * 128
+        same, other, zero = lambda c: c, lambda c: 1 - c, lambda x, c: 0
+        pieces = [(w_o, 0, zero, None), (wa0, 1, near(same, 0), None), (wa0_s, 1, near(other, 0), None)]
+        pieces += [(wa1, 1, near(same, 2), None), (wa1_s, 1, near(other, 2), None)]
+        pieces.append(((wb, wb_s), 1, lambda x, c: (1 - x) * 768, lambda x, c: c == x))
+        total = fold([o_own, o_fa], pieces, None, jnp.float32)
+        wx0_s = over_core(after(wx0, o_own))
+        wx1_s = over_core(after(wx1, total))
+        pieces = [((wb, wb_s), 0, lambda x, c: x * 768, lambda x, c: c != x)]
+        pieces += [(wx0, 0, away(same, 0), None), (wx0_s, 0, away(other, 0), None)]
+        pieces += [(wx1, 0, away(same, 2), None), (wx1_s, 0, away(other, 2), None)]
+        return fold([after(o_fb, wx1)], pieces, total, jnp.bfloat16)
 
     seq_spec = P(('dp', 'sp', 'hp'), None)
     in_specs = (seq_spec, P(None, 'hp'), P(None, 'hp'), P(None, 'hp'), P('hp', None))

time: 401 us -> 344 us (0.86)
  waiting for transfers between devices: 123 us -> 68 us
  Pallas kernels: 251 us -> 246 us
  starting transfers between devices: 20.4 us -> 25.2 us
    ppermute x6 -> x7, waiting for transfers between devices: 53.9 us -> 10.3 us  [device_fn(): over_y = lambda a: lax.ppermute(a, 'hp', hp_swap)]
    ppermute x8 -> x9, waiting for transfers between devices: 68.2 us -> 54.1 us  [device_fn(): over_x = lambda a: lax.ppermute(a, 'sp', x_swap)]
    pallas_call x9 -> x8, Pallas kernels: 164 us -> 154 us  [the longest x6 123 us: attend(): pl.pallas_call(functools.partial(attend_kernel, tuple(shape), block, spli...]
    pallas_call x5 -> x6, Pallas kernels: 87.2 us -> 91.9 us  [project(): pl.pallas_call(functools.partial(project_kernel, tuple(flips), width, tup...]
    ppermute x6 -> x7, starting transfers between devices: 7.64 us -> 10.2 us  [device_fn(): over_y = lambda a: lax.ppermute(a, 'hp', hp_swap)]
    ppermute x8 -> x9, starting transfers between devices: 9.6 us -> 11.5 us  [device_fn(): over_x = lambda a: lax.ppermute(a, 'sp', x_swap)]
  transfers between devices with their start and end apart: 31 -> 35, of which waited for: 9 -> 9; matrix products, arithmetic and copies ran while one was open for 0% -> 0% of each run, Pallas kernels for 58% -> 68%
where the time goes in v2:
time: 344 us
  Pallas kernels  246 us (72%)
  waiting for transfers between devices  68 us (20%)
  starting transfers between devices  25.2 us (7%)
  local copies, waits for them, and re-layouts  4.17 us (1%)
    pallas_call x6, Pallas kernels, attend(): pl.pallas_call(functools.partial(attend_kernel, tuple(shape), block, spli...  123 us
    pallas_call x6, Pallas kernels, project(): pl.pallas_call(functools.partial(project_kernel, tuple(flips), width, tup...  91.9 us
    ppermute x9, waiting for transfers between devices, device_fn(): over_x = lambda a: lax.ppermute(a, 'sp', x_swap)  54.1 us
    pallas_call x2, Pallas kernels, fold(): pl.pallas_call(functools.partial(fold_kernel, tuple(plan), width, base is...  31.1 us
    ppermute x9, starting transfers between devices, device_fn(): over_x = lambda a: lax.ppermute(a, 'sp', x_swap)  11.5 us
    ppermute x7, waiting for transfers between devices, device_fn(): over_y = lambda a: lax.ppermute(a, 'hp', hp_swap)  10.3 us
    ppermute x7, starting transfers between devices, device_fn(): over_y = lambda a: lax.ppermute(a, 'hp', hp_swap)  10.2 us
  transfers between devices with their start and end apart: 35, of which 9 were waited for; matrix products, arithmetic and copies ran while one was open for 0% of the time, Pallas kernels for 68%

profile of v2, /device:TPU:0, one launch (start us, length us, event | category | flops | bytes accessed | tf_op | source)
XLA Modules:
  0.0 344.0 jit_solution(11719955658389257411)
XLA Ops:
  0.0 3.1 slice.3
  3.1 3.3 collective-permute-start
  6.5 8.3 %shard_map.55 = (bf16[512,512]{1,0:T(8,128)(2,1)}, bf16[256,4096]{1,0:T(8,128)(2,1)}) custom-call(bf16[512,4096]{1,0:T(8,128)(2,1)} %x_ref.3, bf16[4096,2048]{1,0:T(8,128)(2,1)} %refs_0_.10), custom_call_target="tpu_custom_call" | custom-call | flops 2147483648 | bytes 4194304 | tf_op jit(solution)/shard_map/pallas_call | solution.py:210
  14.8 12.6 %shard_map.56.refs_2_.refs_3_ = bf16[512,1536]{1,0:T(8,128)(2,1)} custom-call(bf16[512,4096]{1,0:T(8,128)(2,1)} %x_ref.3, bf16[4096,2048]{1,0:T(8,128)(2,1)} %refs_0_.10), custom_call_target="tpu_custom_call" | custom-call | flops 6442450944 | bytes 12582912 | tf_op jit(solution)/shard_map/pallas_call | solution.py:210
  27.3 25.5 %shard_map.57 = (bf16[2048,512]{1,0:T(8,128)(2,1)}, bf16[512,2048]{1,0:T(8,128)(2,1)}, bf16[256,4096]{1,0:T(8,128)(2,1)}, bf16[128,4096]{1,0:T(8,128)(2,1)}, bf16[256,4096]{1,0:T(8,128)(2,1)}) custom-call(bf16[512,4096]{1,0:T(8,128)(2,1)} %x_ref.3, bf16[4096,2048]{1,0:T(8,128)(2,1)} %refs_1_.5, bf16[4096,2048]{1,0:T(8,128)(2,1)} %refs_0_.11, ...), custom_call_target="tpu_custom_call" | custom-call | flops 17179869184 | bytes 33554432 | tf_op jit(solution)/shard_map/pallas_call | solution.py:210
  53.4 2.0 collective-permute-start.11
  55.4 20.3 %shard_map.58 = (bf16[256,2048]{1,0:T(8,128)(2,1)}, bf16[2048,256]{1,0:T(8,128)(2,1)}, bf16[256,2048]{1,0:T(8,128)(2,1)}) custom-call(bf16[256,4096]{1,0:T(8,128)(2,1)} %collective-permute-done.x_ref, bf16[4096,2048]{1,0:T(8,128)(2,1)} %refs_0_.10, bf16[4096,2048]{1,0:T(8,128)(2,1)} %refs_1_.5, bf16[4096,2048]{1,0:T(8,128)(2,1)} %refs_0_.11), custom_call_target="tpu_custom_call" | custom-call | flops 12884901888 | bytes 50331648 | tf_op jit(solution)/shard_map/pallas_call | solution.py:210
  75.8 2.0 collective-permute-start.9
  77.8 14.8 %shard_map.59 = (f32[16,1,512]{2,1,0:T(1,128)}, f32[16,1,512]{2,1,0:T(1,128)}, f32[2048,512]{1,0:T(8,128)}) custom-call(bf16[512,2048]{1,0:T(8,128)(2,1)} %get-tuple-element.92.refs_0_, bf16[512,512]{1,0:T(8,128)(2,1)} %get-tuple-element.61.refs_1_.refs_2_, bf16[512,1536]{1,0:T(8,128)(2,1)} %shard_map.56.refs_2_.refs_3_, ...), custom_call_target="tpu_custom_call" | custom-call | flops 8589934592 | bytes 10485760 | tf_op jit(solution)/shard_map/pallas_call | solution.py:111
  92.5 8.8 %collective-permute-done.1.x_ref = bf16[256,4096]{1,0:T(8,128)(2,1)} collective-permute-done((bf16[256,4096]{1,0:T(8,128)(2,1)}, bf16[256,4096]{1,0:T(8,128)(2,1)}, u32[]{:S(2)}, u32[]{:S(2)}) %collective-permute-start.1) | collective-permute-done | bytes 2097184 | tf_op jit(solution)/shard_map/ppermute | solution.py:338
  101.3 15.3 %shard_map.60 = (bf16[256,2048]{1,0:T(8,128)(2,1)}, bf16[2048,256]{1,0:T(8,128)(2,1)}) custom-call(bf16[256,4096]{1,0:T(8,128)(2,1)} %collective-permute-done.1.x_ref, bf16[4096,2048]{1,0:T(8,128)(2,1)} %refs_0_.10, bf16[4096,2048]{1,0:T(8,128)(2,1)} %refs_1_.5), custom_call_target="tpu_custom_call" | custom-call | flops 8589934592 | bytes 33554432 | tf_op jit(solution)/shard_map/pallas_call | solution.py:210
  117.1 29.1 %collective-permute-done.9.refs_16_.refs_9_ = bf16[512,512]{1,0:T(8,128)(2,1)} collective-permute-done((bf16[512,512]{1,0:T(8,128)(2,1)}, bf16[512,512]{1,0:T(8,128)(2,1)}, u32[]{:S(2)}, u32[]{:S(2)}) %collective-permute-start.9) | collective-permute-done | bytes 524320 | tf_op jit(solution)/shard_map/ppermute | solution.py:339
  146.7 1.7 collective-permute-done.12.refs_19_.refs_12_
  149.0 10.0 %shard_map.61.refs_1_.refs_2_ = bf16[256,2048]{1,0:T(8,128)(2,1)} custom-call(bf16[256,4096]{1,0:T(8,128)(2,1)} %collective-permute-done.1.x_ref, bf16[4096,2048]{1,0:T(8,128)(2,1)} %refs_0_.11), custom_call_target="tpu_custom_call" | custom-call | flops 4294967296 | bytes 16777216 | tf_op jit(solution)/shard_map/pallas_call | solution.py:210
  159.0 1.8 collective-permute-start.26
  164.8 38.0 %shard_map.62 = (f32[16,1,512]{2,1,0:T(1,128)}, f32[16,1,512]{2,1,0:T(1,128)}, f32[2048,512]{1,0:T(8,128)}) custom-call(bf16[256,2048]{1,0:T(8,128)(2,1)} %get-tuple-element.85.refs_0_.refs_1_, bf16[256,2048]{1,0:T(8,128)(2,1)} %shard_map.61.refs_1_.refs_2_, bf16[512,512]{1,0:T(8,128)(2,1)} %get-tuple-element.61.refs_1_.refs_2_, ...), custom_call_target="tpu_custom_call" | custom-call | flops 25769803776 | bytes 27262976 | tf_op jit(solution)/shard_map/pallas_call | solution.py:111
  203.1 31.5 %shard_map.63 = (f32[16,1,512]{2,1,0:T(1,128)}, f32[16,1,512]{2,1,0:T(1,128)}, f32[2048,512]{1,0:T(8,128)}) custom-call(bf16[512,2048]{1,0:T(8,128)(2,1)} %get-tuple-element.92.refs_0_, bf16[256,2048]{1,0:T(8,128)(2,1)} %get-tuple-element.67.refs_8_.refs_1_, ...), custom_call_target="tpu_custom_call", output_to_operand_aliasing={{0}: (15, {}), {1}: (16, {}), {2}: (17, {})} | custom-call | flops 17179869184 | bytes 18874368 | tf_op jit(solution)/shard_map/pallas_call | solution.py:111
  235.2 18.3 %collective-permute-done.15.refs_3_.refs_1_ = bf16[256,2048]{1,0:T(8,128)(2,1)} collective-permute-done((bf16[256,2048]{1,0:T(8,128)(2,1)}, bf16[256,2048]{1,0:T(8,128)(2,1)}, u32[]{:S(2)}, u32[]{:S(2)}) %collective-permute-start.15) | collective-permute-done | bytes 1048608 | tf_op jit(solution)/shard_map/ppermute | solution.py:339
  258.1 10.5 %shard_map.64 = bf16[512,1024]{1,0:T(8,128)(2,1)} custom-call(s32[1]{0:T(128)} %bitcast.1.refs_0_, bf16[256,2048]{1,0:T(8,128)(2,1)} %get-tuple-element.85.refs_0_.refs_1_, bf16[256,2048]{1,0:T(8,128)(2,1)} %shard_map.61.refs_1_.refs_2_, bf16[256,2048]{1,0:T(8,128)(2,1)} %collective-permute-done.15.refs_3_.refs_1_, ...), custom_call_target="tpu_custom_call" | custom-call | flops 4294967296 | bytes 5242880 | tf_op jit(solution)/shard_map/pallas_call | solution.py:111
  268.6 10.7 %shard_map.65 = bf16[512,1024]{1,0:T(8,128)(2,1)} custom-call(s32[1]{0:T(128)} %bitcast.refs_0_, bf16[256,2048]{1,0:T(8,128)(2,1)} %get-tuple-element.85.refs_0_.refs_1_, bf16[256,2048]{1,0:T(8,128)(2,1)} %shard_map.61.refs_1_.refs_2_, bf16[256,2048]{1,0:T(8,128)(2,1)} %collective-permute-done.15.refs_3_.refs_1_, ...), custom_call_target="tpu_custom_call" | custom-call | flops 4294967296 | bytes 5242880 | tf_op jit(solution)/shard_map/pallas_call | solution.py:111
  281.4 17.7 %shard_map.66.refs_0_ = bf16[512,2048]{1,0:T(8,128)(2,1)} custom-call(bf16[512,2048]{1,0:T(8,128)(2,1)} %get-tuple-element.92.refs_0_, bf16[256,2048]{1,0:T(8,128)(2,1)} %collective-permute-done.15.refs_3_.refs_1_, bf16[256,2048]{1,0:T(8,128)(2,1)} %collective-permute-done.16.refs_4_.refs_2_, bf16[2048,256]{1,0:T(8,128)(2,1)} %collective-permute-done.17.refs_5_.refs_3_, ...), custom_call_target="tpu_custom_call" | custom-call | flops 8589934592 | bytes 10485760 | tf_op jit(solution)/shard_map/pallas_call | solution.py:111
  299.1 5.3 %collective-permute-done.29.refs_3_ = bf16[256,4096]{1,0:T(8,128)(2,1)} collective-permute-done((bf16[256,4096]{1,0:T(8,128)(2,1)}, bf16[256,4096]{1,0:T(8,128)(2,1)}, u32[]{:S(2)}, u32[]{:S(2)}) %collective-permute-start.29) | collective-permute-done | bytes 2097184 | tf_op jit(solution)/shard_map/ppermute | solution.py:339
  307.7 19.9 %shard_map.67.refs_7_ = f32[512,4096]{1,0:T(8,128)} custom-call(bf16[512,2048]{1,0:T(8,128)(2,1)} %shard_map.66.refs_0_, bf16[512,1024]{1,0:T(8,128)(2,1)} %collective-permute-done.31.refs_1_, bf16[2048,4096]{1,0:T(8,128)(2,1)} %refs_2_.5, bf16[256,4096]{1,0:T(8,128)(2,1)} %collective-permute-done.28.refs_3_, ...), custom_call_target="tpu_custom_call" | custom-call | flops 12884901888 | bytes 25165824 | tf_op jit(solution)/shard_map/pallas_call | solution.py:314
  332.7 11.1 %shard_map.68 = bf16[512,4096]{1,0:T(8,128)(2,1)} custom-call(bf16[512,1024]{1,0:T(8,128)(2,1)} %collective-permute-done.23.refs_0_, bf16[256,4096]{1,0:T(8,128)(2,1)} %collective-permute-done.26.refs_7_.refs_1_, bf16[256,4096]{1,0:T(8,128)(2,1)} %collective-permute-done.27.refs_8_.refs_2_, bf16[256,4096]{1,0:T(8,128)(2,1)} %collective-permute-done.29.refs_3_, ...), custom_call_target="tpu_custom_call" | custom-call | flops 4294967296 | bytes 8388608 | tf_op jit(solution)/shard_map/pallas_call | solution.py:314
  (73 shorter events, 22.0 us)
Async XLA Ops:
  3.1 52.3 %collective-permute-start = (bf16[256,4096]{1,0:T(8,128)(2,1)}, bf16[256,4096]{1,0:T(8,128)(2,1)}, u32[]{:S(2)}, u32[]{:S(2)}) collective-permute-start(bf16[256,4096]{1,0:T(8,128)(2,1)} %slice.3), channel_id=1, source_target_pairs={{0,4},{4,0},{1,5},{5,1},{2,6},{6,2},{3,7},{7,3}} | collective-permute-start | bytes 6291464 | tf_op jit(solution)/shard_map/ppermute | solution.py:338
  52.9 24.9 %collective-permute-start.4 = (bf16[2048,512]{1,0:T(8,128)(2,1)}, bf16[2048,512]{1,0:T(8,128)(2,1)}, u32[]{:S(2)}, u32[]{:S(2)}) collective-permute-start(bf16[2048,512]{1,0:T(8,128)(2,1)} %get-tuple-element.60.refs_3_.refs_4_), channel_id=1, source_target_pairs={{0,1},{1,0},{2,3},{3,2},{4,5},{5,4},{6,7},{7,6}} | collective-permute-start | bytes 6291464 | tf_op jit(solution)/shard_map/ppermute | solution.py:340
  52.9 22.9 %collective-permute-start.3 = (bf16[512,1536]{1,0:T(8,128)(2,1)S(1)}, bf16[512,1536]{1,0:T(8,128)(2,1)}, u32[]{:S(2)}, u32[]{:S(2)}) collective-permute-start(bf16[512,1536]{1,0:T(8,128)(2,1)S(1)} %copy-done.2), channel_id=1, source_target_pairs={{0,1},{1,0},{2,3},{3,2},{4,5},{5,4},{6,7},{7,6}} | collective-permute-start | bytes 4718600 | tf_op jit(solution)/shard_map/ppermute | solution.py:340
  53.4 47.9 %collective-permute-start.1 = (bf16[256,4096]{1,0:T(8,128)(2,1)}, bf16[256,4096]{1,0:T(8,128)(2,1)}, u32[]{:S(2)}, u32[]{:S(2)}) collective-permute-start(bf16[256,4096]{1,0:T(8,128)(2,1)} %get-tuple-element.58), channel_id=1, source_target_pairs={{0,4},{4,0},{1,5},{5,1},{2,6},{6,2},{3,7},{7,3}} | collective-permute-start | bytes 6291464 | tf_op jit(solution)/shard_map/ppermute | solution.py:338
  53.4 63.2 %collective-permute-start.11 = (bf16[2048,512]{1,0:T(8,128)(2,1)}, bf16[2048,512]{1,0:T(8,128)(2,1)}, u32[]{:S(2)}, u32[]{:S(2)}) collective-permute-start(bf16[2048,512]{1,0:T(8,128)(2,1)} %get-tuple-element.60.refs_3_.refs_4_), channel_id=1, source_target_pairs={{0,2},{1,3},{2,0},{3,1},{4,6},{5,7},{6,4},{7,5}} | collective-permute-start | bytes 6291464 | tf_op jit(solution)/shard_map/ppermute | solution.py:339
  75.7 70.5 %collective-permute-start.10 = (bf16[512,1536]{1,0:T(8,128)(2,1)S(1)}, bf16[512,1536]{1,0:T(8,128)(2,1)}, u32[]{:S(2)}, u32[]{:S(2)}) collective-permute-start(bf16[512,1536]{1,0:T(8,128)(2,1)S(1)} %copy-done.2), channel_id=1, source_target_pairs={{0,2},{1,3},{2,0},{3,1},{4,6},{5,7},{6,4},{7,5}} | collective-permute-start | bytes 4718600 | tf_op jit(solution)/shard_map/ppermute | solution.py:339
  75.8 70.5 %collective-permute-start.9 = (bf16[512,512]{1,0:T(8,128)(2,1)}, bf16[512,512]{1,0:T(8,128)(2,1)}, u32[]{:S(2)}, u32[]{:S(2)}) collective-permute-start(bf16[512,512]{1,0:T(8,128)(2,1)} %get-tuple-element.61.refs_1_.refs_2_), channel_id=1, source_target_pairs={{0,2},{1,3},{2,0},{3,1},{4,6},{5,7},{6,4},{7,5}} | collective-permute-start | bytes 1572872 | tf_op jit(solution)/shard_map/ppermute | solution.py:339
  116.6 32.0 %collective-permute-start.8 = (bf16[2048,256]{1,0:T(8,128)(2,1)}, bf16[2048,256]{1,0:T(8,128)(2,1)}, u32[]{:S(2)}, u32[]{:S(2)}) collective-permute-start(bf16[2048,256]{1,0:T(8,128)(2,1)} %get-tuple-element.65.refs_11_.refs_4_), channel_id=1, source_target_pairs={{0,1},{1,0},{2,3},{3,2},{4,5},{5,4},{6,7},{7,6}} | collective-permute-start | bytes 3145736 | tf_op jit(solution)/shard_map/ppermute | solution.py:340
  116.6 46.4 %collective-permute-start.14 = (bf16[2048,512]{1,0:T(8,128)(2,1)}, bf16[2048,512]{1,0:T(8,128)(2,1)}, u32[]{:S(2)}, u32[]{:S(2)}) collective-permute-start(bf16[2048,512]{1,0:T(8,128)(2,1)} %collective-permute-done.11.refs_18_.refs_11_), channel_id=1, source_target_pairs={{0,1},{1,0},{2,3},{3,2},{4,5},{5,4},{6,7},{7,6}} | collective-permute-start | bytes 6291464 | tf_op jit(solution)/shard_map/ppermute | solution.py:340
  159.0 120.4 %collective-permute-start.26 = (bf16[256,4096]{1,0:T(8,128)(2,1)}, bf16[256,4096]{1,0:T(8,128)(2,1)}, u32[]{:S(2)}, u32[]{:S(2)}) collective-permute-start(bf16[256,4096]{1,0:T(8,128)(2,1)} %get-tuple-element.54), channel_id=1, source_target_pairs={{0,4},{4,0},{1,5},{5,1},{2,6},{6,2},{3,7},{7,3}} | collective-permute-start | bytes 6291464 | tf_op jit(solution)/shard_map/ppermute | solution.py:338
  160.7 92.7 %collective-permute-start.28 = (bf16[256,4096]{1,0:T(8,128)(2,1)}, bf16[256,4096]{1,0:T(8,128)(2,1)}, u32[]{:S(2)}, u32[]{:S(2)}) collective-permute-start(bf16[256,4096]{1,0:T(8,128)(2,1)} %get-tuple-element.90), channel_id=1, source_target_pairs={{0,4},{4,0},{1,5},{5,1},{2,6},{6,2},{3,7},{7,3}} | collective-permute-start | bytes 6291464 | tf_op jit(solution)/shard_map/ppermute | solution.py:338
  161.0 41.8 %collective-permute-start.21 = (bf16[2048,256]{1,0:T(8,128)(2,1)}, bf16[2048,256]{1,0:T(8,128)(2,1)}, u32[]{:S(2)}, u32[]{:S(2)}) collective-permute-start(bf16[2048,256]{1,0:T(8,128)(2,1)} %get-tuple-element.65.refs_11_.refs_4_), channel_id=1, source_target_pairs={{0,2},{1,3},{2,0},{3,1},{4,6},{5,7},{6,4},{7,5}} | collective-permute-start | bytes 3145736 | tf_op jit(solution)/shard_map/ppermute | solution.py:339
  162.8 71.9 %collective-permute-start.19 = (bf16[256,2048]{1,0:T(8,128)(2,1)}, bf16[256,2048]{1,0:T(8,128)(2,1)}, u32[]{:S(2)}, u32[]{:S(2)}) collective-permute-start(bf16[256,2048]{1,0:T(8,128)(2,1)} %get-tuple-element.68.refs_9_.refs_2_), channel_id=1, source_target_pairs={{0,2},{1,3},{2,0},{3,1},{4,6},{5,7},{6,4},{7,5}} | collective-permute-start | bytes 3145736 | tf_op jit(solution)/shard_map/ppermute | solution.py:339
  163.1 71.6 %collective-permute-start.17 = (bf16[2048,256]{1,0:T(8,128)(2,1)}, bf16[2048,256]{1,0:T(8,128)(2,1)}, u32[]{:S(2)}, u32[]{:S(2)}) collective-permute-start(bf16[2048,256]{1,0:T(8,128)(2,1)} %get-tuple-element.69.refs_10_.refs_3_), channel_id=1, source_target_pairs={{0,2},{1,3},{2,0},{3,1},{4,6},{5,7},{6,4},{7,5}} | collective-permute-start | bytes 3145736 | tf_op jit(solution)/shard_map/ppermute | solution.py:339
  202.8 50.6 %collective-permute-start.15 = (bf16[256,2048]{1,0:T(8,128)(2,1)}, bf16[256,2048]{1,0:T(8,128)(2,1)}, u32[]{:S(2)}, u32[]{:S(2)}) collective-permute-start(bf16[256,2048]{1,0:T(8,128)(2,1)} %get-tuple-element.67.refs_8_.refs_1_), channel_id=1, source_target_pairs={{0,2},{1,3},{2,0},{3,1},{4,6},{5,7},{6,4},{7,5}} | collective-permute-start | bytes 3145736 | tf_op jit(solution)/shard_map/ppermute | solution.py:339
  254.0 25.5 %collective-permute-start.24 = (bf16[128,4096]{1,0:T(8,128)(2,1)S(1)}, bf16[128,4096]{1,0:T(8,128)(2,1)}, u32[]{:S(2)}, u32[]{:S(2)}) collective-permute-start(bf16[128,4096]{1,0:T(8,128)(2,1)S(1)} %copy-done.4), channel_id=1, source_target_pairs={{0,4},{4,0},{1,5},{5,1},{2,6},{6,2},{3,7},{7,3}} | collective-permute-start | bytes 3145736 | tf_op jit(solution)/shard_map/ppermute | solution.py:338
  255.7 51.9 %collective-permute-start.32 = (bf16[256,4096]{1,0:T(8,128)(2,1)}, bf16[256,4096]{1,0:T(8,128)(2,1)}, u32[]{:S(2)}, u32[]{:S(2)}) collective-permute-start(bf16[256,4096]{1,0:T(8,128)(2,1)} %collective-permute-done.28.refs_3_), channel_id=1, source_target_pairs={{0,1},{1,0},{2,3},{3,2},{4,5},{5,4},{6,7},{7,6}} | collective-permute-start | bytes 6291464 | tf_op jit(solution)/shard_map/ppermute | solution.py:340
  256.4 48.0 %collective-permute-start.29 = (bf16[256,4096]{1,0:T(8,128)(2,1)}, bf16[256,4096]{1,0:T(8,128)(2,1)}, u32[]{:S(2)}, u32[]{:S(2)}) collective-permute-start(bf16[256,4096]{1,0:T(8,128)(2,1)} %collective-permute-done.28.refs_3_), channel_id=1, source_target_pairs={{0,2},{1,3},{2,0},{3,1},{4,6},{5,7},{6,4},{7,5}} | collective-permute-start | bytes 6291464 | tf_op jit(solution)/shard_map/ppermute | solution.py:339
  279.4 28.3 %collective-permute-start.27 = (bf16[256,4096]{1,0:T(8,128)(2,1)}, bf16[256,4096]{1,0:T(8,128)(2,1)}, u32[]{:S(2)}, u32[]{:S(2)}) collective-permute-start(bf16[256,4096]{1,0:T(8,128)(2,1)} %collective-permute-done.26.refs_7_.refs_1_), channel_id=1, source_target_pairs={{0,1},{1,0},{2,3},{3,2},{4,5},{5,4},{6,7},{7,6}} | collective-permute-start | bytes 6291464 | tf_op jit(solution)/shard_map/ppermute | solution.py:340
  279.4 26.7 %collective-permute-start.33 = (bf16[128,4096]{1,0:T(8,128)(2,1)}, bf16[128,4096]{1,0:T(8,128)(2,1)}, u32[]{:S(2)}, u32[]{:S(2)}) collective-permute-start(bf16[128,4096]{1,0:T(8,128)(2,1)} %collective-permute-done.24.refs_5_), channel_id=1, source_target_pairs={{0,1},{1,0},{2,3},{3,2},{4,5},{5,4},{6,7},{7,6}} | collective-permute-start | bytes 3145736 | tf_op jit(solution)/shard_map/ppermute | solution.py:340
  279.9 27.7 %collective-permute-start.31 = (bf16[512,1024]{1,0:T(8,128)(2,1)}, bf16[512,1024]{1,0:T(8,128)(2,1)}, u32[]{:S(2)}, u32[]{:S(2)}) collective-permute-start(bf16[512,1024]{1,0:T(8,128)(2,1)} %shard_map.64), channel_id=1, source_target_pairs={{0,4},{4,0},{1,5},{5,1},{2,6},{6,2},{3,7},{7,3}} | collective-permute-start | bytes 3145736 | tf_op jit(solution)/shard_map/ppermute | solution.py:338
  304.4 24.6 %collective-permute-start.25 = (bf16[128,4096]{1,0:T(8,128)(2,1)}, bf16[128,4096]{1,0:T(8,128)(2,1)S(1)}, u32[]{:S(2)}, u32[]{:S(2)}) collective-permute-start(bf16[128,4096]{1,0:T(8,128)(2,1)} %collective-permute-done.24.refs_5_), channel_id=1, source_target_pairs={{0,2},{1,3},{2,0},{3,1},{4,6},{5,7},{6,4},{7,5}} | collective-permute-start | bytes 3145736 | tf_op jit(solution)/shard_map/ppermute | solution.py:339
  306.1 24.4 %collective-permute-start.23 = (bf16[512,1024]{1,0:T(8,128)(2,1)}, bf16[512,1024]{1,0:T(8,128)(2,1)}, u32[]{:S(2)}, u32[]{:S(2)}) collective-permute-start(bf16[512,1024]{1,0:T(8,128)(2,1)} %shard_map.65), channel_id=1, source_target_pairs={{0,4},{4,0},{1,5},{5,1},{2,6},{6,2},{3,7},{7,3}} | collective-permute-start | bytes 3145736 | tf_op jit(solution)/shard_map/ppermute | solution.py:338
  307.6 25.0 %collective-permute-start.30 = (bf16[256,4096]{1,0:T(8,128)(2,1)}, bf16[256,4096]{1,0:T(8,128)(2,1)}, u32[]{:S(2)}, u32[]{:S(2)}) collective-permute-start(bf16[256,4096]{1,0:T(8,128)(2,1)} %collective-permute-done.29.refs_3_), channel_id=1, source_target_pairs={{0,1},{1,0},{2,3},{3,2},{4,5},{5,4},{6,7},{7,6}} | collective-permute-start | bytes 6291464 | tf_op jit(solution)/shard_map/ppermute | solution.py:340
  (17 other events, 211.5 us)

commit v3 on v2

--- a/solution.py
+++ b/solution.py
@@ -11,6 +11,9 @@
 
 HEAD_DIM = 128
 EXP2_SCALE = math.log2(math.e) / math.sqrt(HEAD_DIM)
+CHUNK = 256
+SUM_LIMIT = 2.0**60
+ACC_LIMIT = 3.0e38
 
 
 def attend_kernel(shape, heads, split, first, last, scalars, *refs):
@@ -20,55 +23,84 @@
     q_refs = take(shape[0])
     groups = [([take(k) for k in widths], take(v)) for widths, v in shape[1:]]
     state_in = None if first else take(3)
-    outs = refs
-    at = lambda h: slice(h * HEAD_DIM, (h + 1) * HEAD_DIM)
-    queries = [jnp.concatenate([r[:, at(h)] for r in q_refs], axis=0) for h in range(heads)]
+    outs, q_copy = refs[:-1], refs[-1]
     low = pl.program_id(0) < split
-
-    def keys_of(piece, h):
-        if len(piece) == 1:
-            return piece[0][:, at(h)]
-        return jnp.where(low, piece[0][:, at(h)], piece[1][:, at(h)])
-
-    def scores_of(h, g):
-        parts = [
-            lax.dot_general(keys_of(k, h), queries[h], (((1,), (1,)), ((), ())), preferred_element_type=jnp.float32)
-            for k in groups[g][0]
-        ]
-        return parts[0] if len(parts) == 1 else jnp.concatenate(parts, axis=0)
-
-    items = [(h, g) for g in range(len(groups)) for h in range(heads)]
+    chunks = []
+    for pieces, values in groups:
+        k_parts = [(p, r) for p in pieces for r in range(0, p[0].shape[0], CHUNK)]
+        v_parts = [(v, c) for v in values for c in range(0, v.shape[1], CHUNK)]
+        chunks += [k + v for k, v in zip(k_parts, v_parts)]
+
+    def scores_of(chunk, at, query):
+        piece, row = chunk[:2]
+        keys = piece[0][row:row + CHUNK, at]
+        if len(piece) > 1:
+            keys = jnp.where(low, keys, piece[1][row:row + CHUNK, at])
+        return lax.dot_general(keys, query, (((1,), (1,)), ((), ())), preferred_element_type=jnp.float32)
+
+    def values_of(chunk, at, probs):
+        v, column = chunk[2:]
+        return jnp.dot(v[at, column:column + CHUNK], probs, preferred_element_type=jnp.float32)
+
+    fixed = [slice(h * HEAD_DIM, (h + 1) * HEAD_DIM) for h in range(heads)]
+    queries = [jnp.concatenate([r[:, at] for r in q_refs], axis=0) for at in fixed]
+    items = [(h, c) for c in range(len(chunks)) for h in range(heads)]
     depth = 2
-    state = {} if first else {h: (state_in[0][h], state_in[1][h], state_in[2][at(h), :]) for h in range(heads)}
-    ahead = [scores_of(*items[i]) for i in range(min(depth, len(items)))]
-    for i, (h, g) in enumerate(items):
+    state = {} if first else {h: (state_in[0][h], state_in[1][h], state_in[2][fixed[h], :]) for h in range(heads)}
+    score = lambda h, c: scores_of(chunks[c], fixed[h], queries[h])
+    ahead = [score(*item) for item in items[:depth]]
+    for i, (h, c) in enumerate(items):
         if i + depth < len(items):
-            ahead.append(scores_of(*items[i + depth]))
+            ahead.append(score(*items[i + depth]))
         scores = ahead.pop(0)
-        new_max = jnp.max(scores, axis=0, keepdims=True) * EXP2_SCALE
-        if h in state:
-            new_max = jnp.maximum(state[h][0], new_max)
-        probs = jnp.exp2(scores * EXP2_SCALE - new_max)
+        shift = state[h][0] if h in state else jnp.max(scores, axis=0, keepdims=True) * EXP2_SCALE
+        probs = jnp.exp2(scores * EXP2_SCALE - shift)
         part_sum = jnp.sum(probs, axis=0, keepdims=True)
-        probs = probs.astype(jnp.bfloat16)
-        part, row = None, 0
-        for v in groups[g][1]:
-            count = v.shape[1]
-            piece = jnp.dot(v[at(h), :], probs[row:row + count], preferred_element_type=jnp.float32)
-            part = piece if part is None else part + piece
-            row += count
-        if h in state:
-            run_max, run_sum, acc = state[h]
-            fade = jnp.exp2(run_max - new_max)
-            state[h] = (new_max, run_sum * fade + part_sum, acc * fade + part)
+        part = values_of(chunks[c], fixed[h], probs.astype(jnp.bfloat16))
+        state[h] = (shift, state[h][1] + part_sum, state[h][2] + part) if h in state else (shift, part_sum, part)
+
+    fine = None
+    for h in range(heads):
+        shift, run_sum, acc = state[h]
+        good = jnp.logical_and(jnp.max(run_sum) < SUM_LIMIT, jnp.max(jnp.abs(acc)) < ACC_LIMIT)
+        fine = good if fine is None else jnp.logical_and(fine, good)
+        if last:
+            outs[0][:, fixed[h]] = (acc / run_sum).T.astype(jnp.bfloat16)
         else:
-            state[h] = (new_max, part_sum, part)
-    for h in range(heads):
-        run_max, run_sum, acc = state[h]
-        if last:
-            outs[0][:, at(h)] = (acc / run_sum).T.astype(jnp.bfloat16)
-        else:
-            outs[0][h], outs[1][h], outs[2][at(h), :] = run_max, run_sum, acc
+            outs[0][h], outs[1][h], outs[2][fixed[h], :] = shift, run_sum, acc
+
+    @pl.when(jnp.logical_not(fine))
+    def _():
+        row = 0
+        for r in q_refs:
+            q_copy[row:row + r.shape[0], :] = r[...]
+            row += r.shape[0]
+
+        def redo(n, carry):
+            h = n // (row // HEAD_DIM)
+            at = pl.ds(pl.multiple_of(h * HEAD_DIM, HEAD_DIM), HEAD_DIM)
+            spot = pl.ds(pl.multiple_of((n % (row // HEAD_DIM)) * HEAD_DIM, HEAD_DIM), HEAD_DIM)
+            query = q_copy[spot, at]
+            if first:
+                run_max = jnp.full((1, HEAD_DIM), -jnp.inf, jnp.float32)
+                run_sum, acc = jnp.zeros((1, HEAD_DIM), jnp.float32), jnp.zeros((HEAD_DIM, HEAD_DIM), jnp.float32)
+            else:
+                run_max, run_sum, acc = state_in[0][h, :, spot], state_in[1][h, :, spot], state_in[2][at, spot]
+            for chunk in chunks:
+                scaled = scores_of(chunk, at, query) * EXP2_SCALE
+                new_max = jnp.maximum(run_max, jnp.max(scaled, axis=0, keepdims=True))
+                fade = jnp.exp2(run_max - new_max)
+                probs = jnp.exp2(scaled - new_max)
+                run_sum = run_sum * fade + jnp.sum(probs, axis=0, keepdims=True)
+                acc = acc * fade + values_of(chunk, at, probs.astype(jnp.bfloat16))
+                run_max = new_max
+            if last:
+                outs[0][spot, at] = (acc / run_sum).T.astype(jnp.bfloat16)
+            else:
+                outs[0][h, :, spot], outs[1][h, :, spot], outs[2][at, spot] = run_max, run_sum, acc
+            return carry
+
+        lax.fori_loop(0, heads * (row // HEAD_DIM), redo, 0)
 
 
 def attend(queries, groups, state, last, block=1, part=None):
@@ -115,6 +147,7 @@
             grid=(steps,),
             in_specs=in_specs + ([] if first else state_specs),
             out_specs=spec((rows, width), lambda h, g: (0, h)) if last else state_specs,
+            scratch_shapes=[pltpu.VMEM((rows, width), jnp.bfloat16)],
         ),
         out_shape=o_shape if last else state_shapes,
         input_output_aliases={} if first or last else {len(offset) + count + j: j for j in range(3)},
@@ -339,17 +372,17 @@
         over_x = lambda a: lax.ppermute(a, 'sp', x_swap)
         over_core = lambda a: lax.ppermute(a, 'sp', core_swap)
 
-        def proj(x, weights, flips, ranges=None, rows_of=None):
-            return project(x, weights, flips, ranges, rows_of)
+        def proj(x, weights, flips, ranges=None, rows_of=None, width=512):
+            return project(x, weights, flips, ranges, rows_of, width)
 
         unit_a = lambda chip_, core_: chip_ * 10 + core_ * 3
         unit_b = lambda core_: 6 + core_ * 2
 
-        middle = w_k.shape[1] // 4
-        x_f0 = over_y(x_own[:half])
-        k_oa, x_half = proj(x_own, [w_k], [False], [(0, middle)], (None, [(half, half)]))
+        middle = w_k.shape[1] // 2
+        k_oa, x_half0, x_half = proj(x_own, [w_k], [False], [(0, middle)], (None, [(0, half), (half, half)]), 256)
         k_xoa = over_x(k_oa)
-        (k_ob,) = proj(after(x_own, k_oa), [w_k], [False], [(middle, 4 * middle)])
+        x_f0 = over_y(x_half0)
+        (k_ob,) = proj(after(x_own, k_oa), [w_k], [False], [(middle, 2 * middle)])
         k_xob = over_x(k_ob)
         x_f1 = over_y(x_half)
         first_a = lambda: unit_a(lax.axis_index('sp') // 2, lax.axis_index('sp') % 2) * 128
@@ -380,15 +413,16 @@
         state_r = attend([q_r0, q_r1], [own, own_s, far, far_s, xo, xo_s], None, False, 2)
         k_sxr0, v_sxr0 = over_core(after(k_xr0, state_r[0])), over_core(after(v_xr0, state_r[0]))
         late = ([k_xr0, k_sxr0], [v_xr0, v_sxr0])
-        state_o = attend([after(q_o, state_r[0])], [far, far_s, xo, xo_s], state_o, False, 2)
+        state_o = attend([after(q_o, state_r[0])], [far, far_s, xo, xo_s], state_o, False, 1)
         wx0, wx1 = over_x(after(wa0, state_r[0])), over_x(after(wa1, state_o[0]))
         wa0_s, wa1_s = over_core(after(wa0, state_r[0])), over_core(after(wa1, state_o[0]))
-
-        k_sxr1, v_sxr1 = over_core(after(k_xr1, state_o[0])), over_core(after(v_xr1, state_o[0]))
+        state_r = attend([after(q_r0, state_o[0]), q_r1], [late], state_r, False, 4)
+
+        k_sxr1, v_sxr1 = over_core(after(k_xr1, state_r[0])), over_core(after(v_xr1, state_r[0]))
         latest = ([k_xr1, k_sxr1], [v_xr1, v_sxr1])
-        o_ra = attend([after(q_r0, state_o[0]), q_r1], [late, latest], state_r, True, 4, chip)
+        o_ra = attend([after(q_r0, state_r[0]), q_r1], [latest], state_r, True, 4, chip)
         o_fa = over_y(o_ra)
-        o_rb = attend([after(q_r0, o_ra), q_r1], [late, latest], state_r, True, 4, 1 - chip)
+        o_rb = attend([after(q_r0, o_ra), q_r1], [latest], state_r, True, 4, 1 - chip)
         o_fb = over_y(o_rb)
         wb_s = over_core(after(wb, o_rb))
         o_own = attend([after(q_o, o_rb)], [late, latest], state_o, True, 4)
@@ -399,7 +433,7 @@
         pieces += [(wa1, 1, near(same, 2), None), (wa1_s, 1, near(other, 2), None)]
         pieces.append(((wb, wb_s), 1, lambda x, c: (1 - x) * 768, lambda x, c: c == x))
         total = fold([o_own, o_fa], pieces, None, jnp.float32)
-        wx0_s = over_core(after(wx0, o_own))
+        wx0_s = over_core(after(wx0, total))
         wx1_s = over_core(after(wx1, total))
         pieces = [((wb, wb_s), 0, lambda x, c: x * 768, lambda x, c: c != x)]
         pieces += [(wx0, 0, away(same, 0), None), (wx0_s, 0, away(other, 0), None)]

time: 344 us -> 397 us (1.15)
  waiting for transfers between devices: 68 us -> 144 us
  Pallas kernels: 246 us -> 227 us
    ppermute x7, waiting for transfers between devices: 10.3 us -> 84 us  [device_fn(): over_y = lambda a: lax.ppermute(a, 'hp', hp_swap)]
    pallas_call x6 -> x7, Pallas kernels: 123 us -> 103 us  [attend(): pl.pallas_call(functools.partial(attend_kernel, tuple(shape), block, spli...]
    ppermute x9, waiting for transfers between devices: 54.1 us -> 58.9 us  [device_fn(): over_x = lambda a: lax.ppermute(a, 'sp', x_swap)]
  transfers between devices with their start and end apart: 35 -> 35, of which waited for: 9 -> 13; matrix products, arithmetic and copies ran while one was open for 0% -> 0% of each run, Pallas kernels for 68% -> 52%
where the time goes in v3:
time: 397 us; the launch traced here: 396 us
  Pallas kernels  227 us (57%)
  waiting for transfers between devices  144 us (36%)
  starting transfers between devices  22 us (6%)
    pallas_call x7, Pallas kernels, attend(): pl.pallas_call(functools.partial(attend_kernel, tuple(shape), block, spli...  103 us
    pallas_call x6, Pallas kernels, project(): pl.pallas_call(functools.partial(project_kernel, tuple(flips), width, tup...  92.5 us
    ppermute x7, waiting for transfers between devices, device_fn(): over_y = lambda a: lax.ppermute(a, 'hp', hp_swap)  84 us
    ppermute x9, waiting for transfers between devices, device_fn(): over_x = lambda a: lax.ppermute(a, 'sp', x_swap)  58.9 us
    pallas_call x2, Pallas kernels, fold(): pl.pallas_call(functools.partial(fold_kernel, tuple(plan), width, base is...  31 us
    ppermute x9, starting transfers between devices, device_fn(): over_x = lambda a: lax.ppermute(a, 'sp', x_swap)  10.1 us
    ppermute x7, starting transfers between devices, device_fn(): over_y = lambda a: lax.ppermute(a, 'hp', hp_swap)  9.21 us
  transfers between devices with their start and end apart: 35, of which 13 were waited for; matrix products, arithmetic and copies ran while one was open for 0% of the time, Pallas kernels for 52%

profile of v3, /device:TPU:0, one launch (start us, length us, event | category | flops | bytes accessed | tf_op | source)
XLA Modules:
  0.0 396.1 jit_solution(11805348613789331533)
XLA Ops:
  0.0 11.4 %shard_map.55 = (bf16[512,1024]{1,0:T(8,128)(2,1)}, bf16[256,4096]{1,0:T(8,128)(2,1)}, bf16[256,4096]{1,0:T(8,128)(2,1)}) custom-call(bf16[512,4096]{1,0:T(8,128)(2,1)} %x_ref.3, bf16[4096,2048]{1,0:T(8,128)(2,1)} %refs_0_.10), custom_call_target="tpu_custom_call" | custom-call | flops 4294967296 | bytes 8388608 | tf_op jit(solution)/shard_map/pallas_call | solution.py:243
  14.8 10.0 %shard_map.56.refs_2_.refs_3_ = bf16[512,1024]{1,0:T(8,128)(2,1)} custom-call(bf16[512,4096]{1,0:T(8,128)(2,1)} %x_ref.3, bf16[4096,2048]{1,0:T(8,128)(2,1)} %refs_0_.10), custom_call_target="tpu_custom_call" | custom-call | flops 4294967296 | bytes 8388608 | tf_op jit(solution)/shard_map/pallas_call | solution.py:243
  24.8 25.5 %shard_map.57 = (bf16[2048,512]{1,0:T(8,128)(2,1)}, bf16[512,2048]{1,0:T(8,128)(2,1)}, bf16[256,4096]{1,0:T(8,128)(2,1)}, bf16[128,4096]{1,0:T(8,128)(2,1)}, bf16[256,4096]{1,0:T(8,128)(2,1)}) custom-call(bf16[512,4096]{1,0:T(8,128)(2,1)} %x_ref.3, bf16[4096,2048]{1,0:T(8,128)(2,1)} %refs_1_.5, bf16[4096,2048]{1,0:T(8,128)(2,1)} %refs_0_.11, ...), custom_call_target="tpu_custom_call" | custom-call | flops 17179869184 | bytes 33554432 | tf_op jit(solution)/shard_map/pallas_call | solution.py:243
  52.3 9.2 %collective-permute-done.x_ref = bf16[256,4096]{1,0:T(8,128)(2,1)} collective-permute-done((bf16[256,4096]{1,0:T(8,128)(2,1)}, bf16[256,4096]{1,0:T(8,128)(2,1)}, u32[]{:S(2)}, u32[]{:S(2)}) %collective-permute-start) | collective-permute-done | bytes 2097184 | tf_op jit(solution)/shard_map/ppermute | solution.py:371
  61.6 20.4 %shard_map.58 = (bf16[256,2048]{1,0:T(8,128)(2,1)}, bf16[2048,256]{1,0:T(8,128)(2,1)}, bf16[256,2048]{1,0:T(8,128)(2,1)}) custom-call(bf16[256,4096]{1,0:T(8,128)(2,1)} %collective-permute-done.x_ref, bf16[4096,2048]{1,0:T(8,128)(2,1)} %refs_0_.10, bf16[4096,2048]{1,0:T(8,128)(2,1)} %refs_1_.5, bf16[4096,2048]{1,0:T(8,128)(2,1)} %refs_0_.11), custom_call_target="tpu_custom_call" | custom-call | flops 12884901888 | bytes 50331648 | tf_op jit(solution)/shard_map/pallas_call | solution.py:243
  84.0 14.6 %shard_map.59 = (f32[16,1,512]{2,1,0:T(1,128)}, f32[16,1,512]{2,1,0:T(1,128)}, f32[2048,512]{1,0:T(8,128)}) custom-call(bf16[512,2048]{1,0:T(8,128)(2,1)} %get-tuple-element.102.refs_0_, bf16[512,1024]{1,0:T(8,128)(2,1)} %get-tuple-element.67.refs_1_.refs_2_, bf16[512,1024]{1,0:T(8,128)(2,1)} %shard_map.56.refs_2_.refs_3_, ...), custom_call_target="tpu_custom_call" | custom-call | flops 8589934592 | bytes 10485760 | tf_op jit(solution)/shard_map/pallas_call | solution.py:143
  98.5 7.1 %collective-permute-done.1.x_ref = bf16[256,4096]{1,0:T(8,128)(2,1)} collective-permute-done((bf16[256,4096]{1,0:T(8,128)(2,1)}, bf16[256,4096]{1,0:T(8,128)(2,1)}, u32[]{:S(2)}, u32[]{:S(2)}) %collective-permute-start.1) | collective-permute-done | bytes 2097184 | tf_op jit(solution)/shard_map/ppermute | solution.py:371
  105.6 15.3 %shard_map.60 = (bf16[256,2048]{1,0:T(8,128)(2,1)}, bf16[2048,256]{1,0:T(8,128)(2,1)}) custom-call(bf16[256,4096]{1,0:T(8,128)(2,1)} %collective-permute-done.1.x_ref, bf16[4096,2048]{1,0:T(8,128)(2,1)} %refs_0_.10, bf16[4096,2048]{1,0:T(8,128)(2,1)} %refs_1_.5), custom_call_target="tpu_custom_call" | custom-call | flops 8589934592 | bytes 33554432 | tf_op jit(solution)/shard_map/pallas_call | solution.py:243
  122.0 21.6 %collective-permute-done.10.refs_17_.refs_10_ = bf16[512,1024]{1,0:T(8,128)(2,1)} collective-permute-done((bf16[512,1024]{1,0:T(8,128)(2,1)S(1)}, bf16[512,1024]{1,0:T(8,128)(2,1)}, u32[]{:S(2)}, u32[]{:S(2)}) %collective-permute-start.10) | collective-permute-done | bytes 1048608 | tf_op jit(solution)/shard_map/ppermute | solution.py:372
  144.1 10.0 %shard_map.61.refs_1_.refs_2_ = bf16[256,2048]{1,0:T(8,128)(2,1)} custom-call(bf16[256,4096]{1,0:T(8,128)(2,1)} %collective-permute-done.1.x_ref, bf16[4096,2048]{1,0:T(8,128)(2,1)} %refs_0_.11), custom_call_target="tpu_custom_call" | custom-call | flops 4294967296 | bytes 16777216 | tf_op jit(solution)/shard_map/pallas_call | solution.py:243
  159.9 33.8 %shard_map.62 = (f32[16,1,512]{2,1,0:T(1,128)}, f32[16,1,512]{2,1,0:T(1,128)}, f32[2048,512]{1,0:T(8,128)}) custom-call(bf16[256,2048]{1,0:T(8,128)(2,1)} %get-tuple-element.95.refs_0_.refs_1_, bf16[256,2048]{1,0:T(8,128)(2,1)} %shard_map.61.refs_1_.refs_2_, bf16[512,1024]{1,0:T(8,128)(2,1)} %get-tuple-element.67.refs_1_.refs_2_, ...), custom_call_target="tpu_custom_call" | custom-call | flops 25769803776 | bytes 27262976 | tf_op jit(solution)/shard_map/pallas_call | solution.py:143
  194.1 10.9 %collective-permute-done.17.refs_4_.refs_3_ = bf16[2048,256]{1,0:T(8,128)(2,1)} collective-permute-done((bf16[2048,256]{1,0:T(8,128)(2,1)}, bf16[2048,256]{1,0:T(8,128)(2,1)}, u32[]{:S(2)}, u32[]{:S(2)}) %collective-permute-start.17) | collective-permute-done | bytes 1048608 | tf_op jit(solution)/shard_map/ppermute | solution.py:372
  205.0 42.4 %collective-permute-done.28.refs_3_ = bf16[256,4096]{1,0:T(8,128)(2,1)} collective-permute-done((bf16[256,4096]{1,0:T(8,128)(2,1)}, bf16[256,4096]{1,0:T(8,128)(2,1)}, u32[]{:S(2)}, u32[]{:S(2)}) %collective-permute-start.28) | collective-permute-done | bytes 2097184 | tf_op jit(solution)/shard_map/ppermute | solution.py:371
  247.4 24.0 %shard_map.63 = (f32[16,1,512]{2,1,0:T(1,128)}, f32[16,1,512]{2,1,0:T(1,128)}, f32[2048,512]{1,0:T(8,128)}) custom-call(bf16[512,2048]{1,0:T(8,128)(2,1)} %get-tuple-element.102.refs_0_, bf16[256,2048]{1,0:T(8,128)(2,1)} %get-tuple-element.73.refs_8_.refs_1_, ...), custom_call_target="tpu_custom_call", output_to_operand_aliasing={{0}: (15, {}), {1}: (16, {}), {2}: (17, {})} | custom-call | flops 17179869184 | bytes 18874368 | tf_op jit(solution)/shard_map/pallas_call | solution.py:143
  271.4 8.8 %shard_map.64 = (f32[16,1,512]{2,1,0:T(1,128)}, f32[16,1,512]{2,1,0:T(1,128)}, f32[2048,512]{1,0:T(8,128)}) custom-call(bf16[256,2048]{1,0:T(8,128)(2,1)} %get-tuple-element.95.refs_0_.refs_1_, bf16[256,2048]{1,0:T(8,128)(2,1)} %shard_map.61.refs_1_.refs_2_, ...), custom_call_target="tpu_custom_call", output_to_operand_aliasing={{0}: (6, {}), {1}: (7, {}), {2}: (8, {})} | custom-call | flops 4294967296 | bytes 6291456 | tf_op jit(solution)/shard_map/pallas_call | solution.py:143
  284.7 5.3 %shard_map.65 = bf16[512,1024]{1,0:T(8,128)(2,1)} custom-call(s32[1]{0:T(128)} %bitcast.1.refs_0_, bf16[256,2048]{1,0:T(8,128)(2,1)} %get-tuple-element.95.refs_0_.refs_1_, bf16[256,2048]{1,0:T(8,128)(2,1)} %shard_map.61.refs_1_.refs_2_, bf16[256,2048]{1,0:T(8,128)(2,1)} %copy-done, bf16[256,2048]{1,0:T(8,128)(2,1)} %copy-done.1, ...), custom_call_target="tpu_custom_call" | custom-call | flops 2147483648 | bytes 3145728 | tf_op jit(solution)/shard_map/pallas_call | solution.py:143
  290.0 5.3 %shard_map.66 = bf16[512,1024]{1,0:T(8,128)(2,1)} custom-call(s32[1]{0:T(128)} %bitcast.refs_0_, bf16[256,2048]{1,0:T(8,128)(2,1)} %get-tuple-element.95.refs_0_.refs_1_, bf16[256,2048]{1,0:T(8,128)(2,1)} %shard_map.61.refs_1_.refs_2_, bf16[256,2048]{1,0:T(8,128)(2,1)} %copy-done, bf16[256,2048]{1,0:T(8,128)(2,1)} %copy-done.1, ...), custom_call_target="tpu_custom_call" | custom-call | flops 2147483648 | bytes 3145728 | tf_op jit(solution)/shard_map/pallas_call | solution.py:143
  295.8 10.9 %collective-permute-done.24.refs_5_ = bf16[128,4096]{1,0:T(8,128)(2,1)} collective-permute-done((bf16[128,4096]{1,0:T(8,128)(2,1)}, bf16[128,4096]{1,0:T(8,128)(2,1)}, u32[]{:S(2)}, u32[]{:S(2)}) %collective-permute-start.24) | collective-permute-done | bytes 1048608 | tf_op jit(solution)/shard_map/ppermute | solution.py:371
  310.0 11.6 %shard_map.67.refs_0_ = bf16[512,2048]{1,0:T(8,128)(2,1)} custom-call(bf16[512,2048]{1,0:T(8,128)(2,1)} %get-tuple-element.102.refs_0_, bf16[256,2048]{1,0:T(8,128)(2,1)} %collective-permute-done.15.refs_2_.refs_1_, bf16[256,2048]{1,0:T(8,128)(2,1)} %collective-permute-done.16.refs_3_.refs_2_, bf16[2048,256]{1,0:T(8,128)(2,1)} %collective-permute-done.17.refs_4_.refs_3_, ...), custom_call_target="tpu_custom_call" | custom-call | flops 8589934592 | bytes 10485760 | tf_op jit(solution)/shard_map/pallas_call | solution.py:143
  322.1 10.5 %collective-permute-done.30.refs_1_ = bf16[512,1024]{1,0:T(8,128)(2,1)} collective-permute-done((bf16[512,1024]{1,0:T(8,128)(2,1)}, bf16[512,1024]{1,0:T(8,128)(2,1)}, u32[]{:S(2)}, u32[]{:S(2)}) %collective-permute-start.30) | collective-permute-done | bytes 1048608 | tf_op jit(solution)/shard_map/ppermute | solution.py:371
  332.6 19.9 %shard_map.68.refs_7_ = f32[512,4096]{1,0:T(8,128)} custom-call(bf16[512,2048]{1,0:T(8,128)(2,1)} %shard_map.67.refs_0_, bf16[512,1024]{1,0:T(8,128)(2,1)} %collective-permute-done.30.refs_1_, bf16[2048,4096]{1,0:T(8,128)(2,1)} %refs_2_.5, bf16[256,4096]{1,0:T(8,128)(2,1)} %collective-permute-done.28.refs_3_, ...), custom_call_target="tpu_custom_call" | custom-call | flops 12884901888 | bytes 25165824 | tf_op jit(solution)/shard_map/pallas_call | solution.py:347
  352.5 4.7 %collective-permute-done.29.refs_3_ = bf16[256,4096]{1,0:T(8,128)(2,1)} collective-permute-done((bf16[256,4096]{1,0:T(8,128)(2,1)}, bf16[256,4096]{1,0:T(8,128)(2,1)}, u32[]{:S(2)}, u32[]{:S(2)}) %collective-permute-start.29) | collective-permute-done | bytes 2097184 | tf_op jit(solution)/shard_map/ppermute | solution.py:372
  357.5 21.4 %collective-permute-done.25.refs_5_ = bf16[128,4096]{1,0:T(8,128)(2,1)} collective-permute-done((bf16[128,4096]{1,0:T(8,128)(2,1)}, bf16[128,4096]{1,0:T(8,128)(2,1)}, u32[]{:S(2)}, u32[]{:S(2)}) %collective-permute-start.25) | collective-permute-done | bytes 1048608 | tf_op jit(solution)/shard_map/ppermute | solution.py:372
  384.8 11.1 %shard_map.69 = bf16[512,4096]{1,0:T(8,128)(2,1)} custom-call(bf16[512,1024]{1,0:T(8,128)(2,1)} %copy-done.3, bf16[256,4096]{1,0:T(8,128)(2,1)} %collective-permute-done.26.refs_7_.refs_1_, bf16[256,4096]{1,0:T(8,128)(2,1)} %collective-permute-done.27.refs_8_.refs_2_, bf16[256,4096]{1,0:T(8,128)(2,1)} %collective-permute-done.29.refs_3_, ...), custom_call_target="tpu_custom_call" | custom-call | flops 4294967296 | bytes 8388608 | tf_op jit(solution)/shard_map/pallas_call | solution.py:347
  (75 shorter events, 29.9 us)
Async XLA Ops:
  11.4 50.2 %collective-permute-start = (bf16[256,4096]{1,0:T(8,128)(2,1)}, bf16[256,4096]{1,0:T(8,128)(2,1)}, u32[]{:S(2)}, u32[]{:S(2)}) collective-permute-start(bf16[256,4096]{1,0:T(8,128)(2,1)} %get-tuple-element.56), channel_id=1, source_target_pairs={{0,4},{4,0},{1,5},{5,1},{2,6},{6,2},{3,7},{7,3}} | collective-permute-start | bytes 6291464 | tf_op jit(solution)/shard_map/ppermute | solution.py:371
  50.3 33.7 %collective-permute-start.4 = (bf16[2048,512]{1,0:T(8,128)(2,1)}, bf16[2048,512]{1,0:T(8,128)(2,1)}, u32[]{:S(2)}, u32[]{:S(2)}) collective-permute-start(bf16[2048,512]{1,0:T(8,128)(2,1)} %get-tuple-element.66.refs_3_.refs_4_), channel_id=1, source_target_pairs={{0,1},{1,0},{2,3},{3,2},{4,5},{5,4},{6,7},{7,6}} | collective-permute-start | bytes 6291464 | tf_op jit(solution)/shard_map/ppermute | solution.py:373
  50.3 55.3 %collective-permute-start.1 = (bf16[256,4096]{1,0:T(8,128)(2,1)}, bf16[256,4096]{1,0:T(8,128)(2,1)}, u32[]{:S(2)}, u32[]{:S(2)}) collective-permute-start(bf16[256,4096]{1,0:T(8,128)(2,1)} %get-tuple-element.64), channel_id=1, source_target_pairs={{0,4},{4,0},{1,5},{5,1},{2,6},{6,2},{3,7},{7,3}} | collective-permute-start | bytes 6291464 | tf_op jit(solution)/shard_map/ppermute | solution.py:371
  50.3 71.1 %collective-permute-start.11 = (bf16[2048,512]{1,0:T(8,128)(2,1)}, bf16[2048,512]{1,0:T(8,128)(2,1)}, u32[]{:S(2)}, u32[]{:S(2)}) collective-permute-start(bf16[2048,512]{1,0:T(8,128)(2,1)} %get-tuple-element.66.refs_3_.refs_4_), channel_id=1, source_target_pairs={{0,2},{1,3},{2,0},{3,1},{4,6},{5,7},{6,4},{7,5}} | collective-permute-start | bytes 6291464 | tf_op jit(solution)/shard_map/ppermute | solution.py:372
  52.3 29.6 %collective-permute-start.2 = (bf16[512,1024]{1,0:T(8,128)(2,1)}, bf16[512,1024]{1,0:T(8,128)(2,1)}, u32[]{:S(2)}, u32[]{:S(2)}) collective-permute-start(bf16[512,1024]{1,0:T(8,128)(2,1)} %get-tuple-element.67.refs_1_.refs_2_), channel_id=1, source_target_pairs={{0,1},{1,0},{2,3},{3,2},{4,5},{5,4},{6,7},{7,6}} | collective-permute-start | bytes 3145736 | tf_op jit(solution)/shard_map/ppermute | solution.py:373
  81.9 39.7 %collective-permute-start.9 = (bf16[512,1024]{1,0:T(8,128)(2,1)}, bf16[512,1024]{1,0:T(8,128)(2,1)}, u32[]{:S(2)}, u32[]{:S(2)}) collective-permute-start(bf16[512,1024]{1,0:T(8,128)(2,1)} %get-tuple-element.67.refs_1_.refs_2_), channel_id=1, source_target_pairs={{0,2},{1,3},{2,0},{3,1},{4,6},{5,7},{6,4},{7,5}} | collective-permute-start | bytes 3145736 | tf_op jit(solution)/shard_map/ppermute | solution.py:372
  83.9 59.7 %collective-permute-start.10 = (bf16[512,1024]{1,0:T(8,128)(2,1)S(1)}, bf16[512,1024]{1,0:T(8,128)(2,1)}, u32[]{:S(2)}, u32[]{:S(2)}) collective-permute-start(bf16[512,1024]{1,0:T(8,128)(2,1)S(1)} %copy-done.5), channel_id=1, source_target_pairs={{0,2},{1,3},{2,0},{3,1},{4,6},{5,7},{6,4},{7,5}} | collective-permute-start | bytes 3145736 | tf_op jit(solution)/shard_map/ppermute | solution.py:372
  121.5 36.8 %collective-permute-start.14 = (bf16[2048,512]{1,0:T(8,128)(2,1)}, bf16[2048,512]{1,0:T(8,128)(2,1)}, u32[]{:S(2)}, u32[]{:S(2)}) collective-permute-start(bf16[2048,512]{1,0:T(8,128)(2,1)} %collective-permute-done.11.refs_18_.refs_11_), channel_id=1, source_target_pairs={{0,1},{1,0},{2,3},{3,2},{4,5},{5,4},{6,7},{7,6}} | collective-permute-start | bytes 6291464 | tf_op jit(solution)/shard_map/ppermute | solution.py:373
  121.7 34.2 %collective-permute-start.8 = (bf16[2048,256]{1,0:T(8,128)(2,1)}, bf16[2048,256]{1,0:T(8,128)(2,1)}, u32[]{:S(2)}, u32[]{:S(2)}) collective-permute-start(bf16[2048,256]{1,0:T(8,128)(2,1)} %get-tuple-element.71.refs_11_.refs_4_), channel_id=1, source_target_pairs={{0,1},{1,0},{2,3},{3,2},{4,5},{5,4},{6,7},{7,6}} | collective-permute-start | bytes 3145736 | tf_op jit(solution)/shard_map/ppermute | solution.py:373
  154.1 141.2 %collective-permute-start.26 = (bf16[256,4096]{1,0:T(8,128)(2,1)}, bf16[256,4096]{1,0:T(8,128)(2,1)}, u32[]{:S(2)}, u32[]{:S(2)}) collective-permute-start(bf16[256,4096]{1,0:T(8,128)(2,1)} %get-tuple-element.60), channel_id=1, source_target_pairs={{0,4},{4,0},{1,5},{5,1},{2,6},{6,2},{3,7},{7,3}} | collective-permute-start | bytes 6291464 | tf_op jit(solution)/shard_map/ppermute | solution.py:371
  155.9 91.5 %collective-permute-start.28 = (bf16[256,4096]{1,0:T(8,128)(2,1)}, bf16[256,4096]{1,0:T(8,128)(2,1)}, u32[]{:S(2)}, u32[]{:S(2)}) collective-permute-start(bf16[256,4096]{1,0:T(8,128)(2,1)} %get-tuple-element.100), channel_id=1, source_target_pairs={{0,4},{4,0},{1,5},{5,1},{2,6},{6,2},{3,7},{7,3}} | collective-permute-start | bytes 6291464 | tf_op jit(solution)/shard_map/ppermute | solution.py:371
  156.2 37.6 %collective-permute-start.15 = (bf16[256,2048]{1,0:T(8,128)(2,1)}, bf16[256,2048]{1,0:T(8,128)(2,1)}, u32[]{:S(2)}, u32[]{:S(2)}) collective-permute-start(bf16[256,2048]{1,0:T(8,128)(2,1)} %get-tuple-element.73.refs_8_.refs_1_), channel_id=1, source_target_pairs={{0,2},{1,3},{2,0},{3,1},{4,6},{5,7},{6,4},{7,5}} | collective-permute-start | bytes 3145736 | tf_op jit(solution)/shard_map/ppermute | solution.py:372
  157.9 47.1 %collective-permute-start.17 = (bf16[2048,256]{1,0:T(8,128)(2,1)}, bf16[2048,256]{1,0:T(8,128)(2,1)}, u32[]{:S(2)}, u32[]{:S(2)}) collective-permute-start(bf16[2048,256]{1,0:T(8,128)(2,1)} %get-tuple-element.75.refs_10_.refs_3_), channel_id=1, source_target_pairs={{0,2},{1,3},{2,0},{3,1},{4,6},{5,7},{6,4},{7,5}} | collective-permute-start | bytes 3145736 | tf_op jit(solution)/shard_map/ppermute | solution.py:372
  158.2 122.0 %collective-permute-start.19 = (bf16[256,2048]{1,0:T(8,128)(2,1)}, bf16[256,2048]{1,0:T(8,128)(2,1)S(1)}, u32[]{:S(2)}, u32[]{:S(2)}) collective-permute-start(bf16[256,2048]{1,0:T(8,128)(2,1)} %get-tuple-element.74.refs_9_.refs_2_), channel_id=1, source_target_pairs={{0,2},{1,3},{2,0},{3,1},{4,6},{5,7},{6,4},{7,5}} | collective-permute-start | bytes 3145736 | tf_op jit(solution)/shard_map/ppermute | solution.py:372
  193.8 87.0 %collective-permute-start.21 = (bf16[2048,256]{1,0:T(8,128)(2,1)}, bf16[2048,256]{1,0:T(8,128)(2,1)}, u32[]{:S(2)}, u32[]{:S(2)}) collective-permute-start(bf16[2048,256]{1,0:T(8,128)(2,1)} %get-tuple-element.71.refs_11_.refs_4_), channel_id=1, source_target_pairs={{0,2},{1,3},{2,0},{3,1},{4,6},{5,7},{6,4},{7,5}} | collective-permute-start | bytes 3145736 | tf_op jit(solution)/shard_map/ppermute | solution.py:372
  205.0 66.4 %collective-permute-start.16 = (bf16[256,2048]{1,0:T(8,128)(2,1)}, bf16[256,2048]{1,0:T(8,128)(2,1)}, u32[]{:S(2)}, u32[]{:S(2)}) collective-permute-start(bf16[256,2048]{1,0:T(8,128)(2,1)} %collective-permute-done.15.refs_2_.refs_1_), channel_id=1, source_target_pairs={{0,1},{1,0},{2,3},{3,2},{4,5},{5,4},{6,7},{7,6}} | collective-permute-start | bytes 3145736 | tf_op jit(solution)/shard_map/ppermute | solution.py:373
  280.8 25.8 %collective-permute-start.24 = (bf16[128,4096]{1,0:T(8,128)(2,1)}, bf16[128,4096]{1,0:T(8,128)(2,1)}, u32[]{:S(2)}, u32[]{:S(2)}) collective-permute-start(bf16[128,4096]{1,0:T(8,128)(2,1)} %get-tuple-element.96), channel_id=1, source_target_pairs={{0,4},{4,0},{1,5},{5,1},{2,6},{6,2},{3,7},{7,3}} | collective-permute-start | bytes 3145736 | tf_op jit(solution)/shard_map/ppermute | solution.py:371
  282.6 39.5 %collective-permute-start.31 = (bf16[256,4096]{1,0:T(8,128)(2,1)}, bf16[256,4096]{1,0:T(8,128)(2,1)}, u32[]{:S(2)}, u32[]{:S(2)}) collective-permute-start(bf16[256,4096]{1,0:T(8,128)(2,1)} %collective-permute-done.28.refs_3_), channel_id=1, source_target_pairs={{0,1},{1,0},{2,3},{3,2},{4,5},{5,4},{6,7},{7,6}} | collective-permute-start | bytes 6291464 | tf_op jit(solution)/shard_map/ppermute | solution.py:373
  295.4 37.2 %collective-permute-start.27 = (bf16[256,4096]{1,0:T(8,128)(2,1)}, bf16[256,4096]{1,0:T(8,128)(2,1)}, u32[]{:S(2)}, u32[]{:S(2)}) collective-permute-start(bf16[256,4096]{1,0:T(8,128)(2,1)} %collective-permute-done.26.refs_7_.refs_1_), channel_id=1, source_target_pairs={{0,1},{1,0},{2,3},{3,2},{4,5},{5,4},{6,7},{7,6}} | collective-permute-start | bytes 6291464 | tf_op jit(solution)/shard_map/ppermute | solution.py:373
  306.7 25.9 %collective-permute-start.30 = (bf16[512,1024]{1,0:T(8,128)(2,1)}, bf16[512,1024]{1,0:T(8,128)(2,1)}, u32[]{:S(2)}, u32[]{:S(2)}) collective-permute-start(bf16[512,1024]{1,0:T(8,128)(2,1)} %shard_map.65), channel_id=1, source_target_pairs={{0,4},{4,0},{1,5},{5,1},{2,6},{6,2},{3,7},{7,3}} | collective-permute-start | bytes 3145736 | tf_op jit(solution)/shard_map/ppermute | solution.py:371
  308.4 48.8 %collective-permute-start.29 = (bf16[256,4096]{1,0:T(8,128)(2,1)}, bf16[256,4096]{1,0:T(8,128)(2,1)}, u32[]{:S(2)}, u32[]{:S(2)}) collective-permute-start(bf16[256,4096]{1,0:T(8,128)(2,1)} %collective-permute-done.28.refs_3_), channel_id=1, source_target_pairs={{0,2},{1,3},{2,0},{3,1},{4,6},{5,7},{6,4},{7,5}} | collective-permute-start | bytes 6291464 | tf_op jit(solution)/shard_map/ppermute | solution.py:372
  321.6 57.4 %collective-permute-start.25 = (bf16[128,4096]{1,0:T(8,128)(2,1)}, bf16[128,4096]{1,0:T(8,128)(2,1)}, u32[]{:S(2)}, u32[]{:S(2)}) collective-permute-start(bf16[128,4096]{1,0:T(8,128)(2,1)} %collective-permute-done.24.refs_5_), channel_id=1, source_target_pairs={{0,2},{1,3},{2,0},{3,1},{4,6},{5,7},{6,4},{7,5}} | collective-permute-start | bytes 3145736 | tf_op jit(solution)/shard_map/ppermute | solution.py:372
  357.2 27.5 %collective-permute-start.33 = (bf16[256,4096]{1,0:T(8,128)(2,1)}, bf16[256,4096]{1,0:T(8,128)(2,1)}, u32[]{:S(2)}, u32[]{:S(2)}) collective-permute-start(bf16[256,4096]{1,0:T(8,128)(2,1)} %collective-permute-done.29.refs_3_), channel_id=1, source_target_pairs={{0,1},{1,0},{2,3},{3,2},{4,5},{5,4},{6,7},{7,6}} | collective-permute-start | bytes 6291464 | tf_op jit(solution)/shard_map/ppermute | solution.py:373
  357.2 25.6 %collective-permute-start.23 = (bf16[512,1024]{1,0:T(8,128)(2,1)S(1)}, bf16[512,1024]{1,0:T(8,128)(2,1)S(1)}, u32[]{:S(2)}, u32[]{:S(2)}) collective-permute-start(bf16[512,1024]{1,0:T(8,128)(2,1)S(1)} %copy-done.2), channel_id=1, source_target_pairs={{0,4},{4,0},{1,5},{5,1},{2,6},{6,2},{3,7},{7,3}} | collective-permute-start | bytes 3145736 | tf_op jit(solution)/shard_map/ppermute | solution.py:371
  (18 other events, 239.5 us)

commit v4 on v3

--- a/solution.py
+++ b/solution.py
@@ -160,7 +160,7 @@
     )(*offset, *operands, *(state or ()))
 
 
-def project_kernel(flips, width, ranges, rows_of, x_ref, *refs):
+def project_kernel(flips, width, ranges, rows_of, x_hbm, *refs):
     refs = list(refs)
     take = lambda n: [refs.pop(0) for _ in range(n)]
     count = len(flips)
@@ -168,7 +168,7 @@
     source = take(1)[0] if rows_of and rows_of[0] is not None else None
     picks = rows_of[1] if rows_of else []
     o_refs, pick_refs = take(count), take(len(picks))
-    ring, sems = take(2)
+    x_ref, x_sem, ring, sems = take(4)
     stage = take(1)[0] if source is not None else None
     pick_sem = take(1)[0] if picks else None
     steps = [(stop - start) // width for start, stop in ranges]
@@ -199,8 +199,11 @@
                 copies.append(pltpu.make_async_copy(here, pick_refs[j], pick_sem.at[j]))
         return copies
 
+    x_copy = pltpu.make_async_copy(x_hbm, x_ref, x_sem)
+    x_copy.start()
     fetch(jnp.int32(0))
     fetch(jnp.int32(1))
+    x_copy.wait()
     for c in pick_copies(True):
         c.start()
     for i in range(count):
@@ -234,7 +237,8 @@
     source, picks = rows_of or (None, [])
     any_spec, vmem_spec = pl.BlockSpec(memory_space=pl.ANY), pl.BlockSpec(memory_space=pltpu.VMEM)
     shapes += [(n, (x if source is None else source).shape[1]) for _, n in picks]
-    scratch = [pltpu.VMEM((3, depth, width), jnp.bfloat16), pltpu.SemaphoreType.DMA((3,))]
+    scratch = [pltpu.VMEM(x.shape, jnp.bfloat16), pltpu.SemaphoreType.DMA(())]
+    scratch += [pltpu.VMEM((3, depth, width), jnp.bfloat16), pltpu.SemaphoreType.DMA((3,))]
     if source is not None:
         scratch.append(pltpu.VMEM((sum(n for _, n in picks), source.shape[1]), jnp.bfloat16))
     if picks:
@@ -242,7 +246,7 @@
     static = None if not picks else ('source' if source is not None else None, tuple(picks))
     return pl.pallas_call(
         functools.partial(project_kernel, tuple(flips), width, tuple(ranges), static),
-        in_specs=[vmem_spec] + [any_spec] * (len(weights) + (source is not None)),
+        in_specs=[any_spec] * (1 + len(weights) + (source is not None)),
         out_specs=[vmem_spec] * len(weights) + [any_spec] * len(picks),
         out_shape=[jax.ShapeDtypeStruct(s, jnp.bfloat16) for s in shapes],
         scratch_shapes=scratch,
@@ -262,7 +266,7 @@
     lhs_refs = take(max(p[1] for p in plan) + 1)
     piece_refs = [take(1 if p[3] is None else 2) for p in plan]
     base_ref = take(1)[0] if has_base else None
-    out_ref, left, right, right_sem, outs, out_sem = take(6)
+    out_ref, left, left_sem, right, right_sem, outs, out_sem = take(7)
     bases, base_sem = take(2) if has_base else (None, None)
     steps = out_ref.shape[1] // width
     columns = lambda j: pl.ds(pl.multiple_of(j * width, width), width)
@@ -291,14 +295,17 @@
         slot = lax.rem(j, 2)
         return pltpu.make_async_copy(outs.at[slot], out_ref.at[:, columns(j)], out_sem.at[slot])
 
+    lhs_copies, column = [], 0
+    for i, (depth, which, start, _) in enumerate(plan):
+        picked = pl.ds(pl.multiple_of(start(chip, core), 128), depth)
+        source, here = lhs_refs[which].at[:, picked], left.at[:, column:column + depth]
+        lhs_copies.append(pltpu.make_async_copy(source, here, left_sem.at[i]))
+        lhs_copies[-1].start()
+        column += depth
     fetch(jnp.int32(0))
     fetch(jnp.int32(1))
-    column = 0
-    for depth, which, start, _ in plan:
-        source = lhs_refs[which]
-        picked = pl.ds(pl.multiple_of(start(chip, core), 128), depth)
-        left[:, column:column + depth] = source[...] if source.shape[1] == depth else source[:, picked]
-        column += depth
+    for c in lhs_copies:
+        c.wait()
 
     def step(j, carry):
         slot = lax.rem(j, 3)
@@ -334,9 +341,10 @@
         plan.append((versions[0].shape[0], which, start, choice))
         arrays += versions
     rows, columns, depth = lhs[0].shape[0], arrays[0].shape[1], sum(p[0] for p in plan)
-    any_spec, vmem_spec = pl.BlockSpec(memory_space=pl.ANY), pl.BlockSpec(memory_space=pltpu.VMEM)
+    any_spec = pl.BlockSpec(memory_space=pl.ANY)
     scratch = [
         pltpu.VMEM((rows, depth), jnp.bfloat16),
+        pltpu.SemaphoreType.DMA((len(plan),)),
         pltpu.VMEM((3, depth, width), jnp.bfloat16),
         pltpu.SemaphoreType.DMA((3, len(plan))),
         pltpu.VMEM((2, rows, width), dtype),
@@ -346,7 +354,7 @@
         scratch += [pltpu.VMEM((3, rows, width), jnp.float32), pltpu.SemaphoreType.DMA((3,))]
     return pl.pallas_call(
         functools.partial(fold_kernel, tuple(plan), width, base is not None),
-        in_specs=[vmem_spec] * len(lhs) + [any_spec] * (len(arrays) + (base is not None)),
+        in_specs=[any_spec] * (len(lhs) + len(arrays) + (base is not None)),
         out_specs=any_spec,
         out_shape=jax.ShapeDtypeStruct((rows, columns), dtype),
         scratch_shapes=scratch,
@@ -379,10 +387,10 @@
         unit_b = lambda core_: 6 + core_ * 2
 
         middle = w_k.shape[1] // 2
-        k_oa, x_half0, x_half = proj(x_own, [w_k], [False], [(0, middle)], (None, [(0, half), (half, half)]), 256)
+        k_oa, x_half0 = proj(x_own, [w_k], [False], [(0, middle)], (None, [(0, half)]), 256)
         k_xoa = over_x(k_oa)
         x_f0 = over_y(x_half0)
-        (k_ob,) = proj(after(x_own, k_oa), [w_k], [False], [(middle, 2 * middle)])
+        k_ob, x_half = proj(after(x_own, k_oa), [w_k], [False], [(middle, 2 * middle)], (None, [(half, half)]))
         k_xob = over_x(k_ob)
         x_f1 = over_y(x_half)
         first_a = lambda: unit_a(lax.axis_index('sp') // 2, lax.axis_index('sp') % 2) * 128

time: 397 us -> 391 us (0.985)
  Pallas kernels: 227 us -> 219 us
    pallas_call x6, Pallas kernels: 92.5 us -> 85.4 us  [project(): pl.pallas_call(functools.partial(project_kernel, tuple(flips), width, tup...]
  transfers between devices with their start and end apart: 35 -> 35, of which waited for: 13 -> 12; matrix products, arithmetic and copies ran while one was open for 0% -> 0% of each run, Pallas kernels for 52% -> 51%
where the time goes in v4:
time: 391 us; the launch traced here: 390 us
  Pallas kernels  219 us (56%)
  waiting for transfers between devices  146 us (37%)
  starting transfers between devices  22.1 us (6%)
    pallas_call x7, Pallas kernels, attend(): pl.pallas_call(functools.partial(attend_kernel, tuple(shape), block, spli...  103 us
    ppermute x7, waiting for transfers between devices, device_fn(): over_y = lambda a: lax.ppermute(a, 'hp', hp_swap)  86.7 us
    pallas_call x6, Pallas kernels, project(): pl.pallas_call(functools.partial(project_kernel, tuple(flips), width, tup...  85.4 us
    ppermute x9, waiting for transfers between devices, device_fn(): over_x = lambda a: lax.ppermute(a, 'sp', x_swap)  57.8 us
    pallas_call x2, Pallas kernels, fold(): pl.pallas_call(functools.partial(fold_kernel, tuple(plan), width, base is...  30.1 us
    ppermute x9, starting transfers between devices, device_fn(): over_x = lambda a: lax.ppermute(a, 'sp', x_swap)  10.1 us
    ppermute x7, starting transfers between devices, device_fn(): over_y = lambda a: lax.ppermute(a, 'hp', hp_swap)  9.17 us
  transfers between devices with their start and end apart: 35, of which 12 were waited for; matrix products, arithmetic and copies ran while one was open for 0% of the time, Pallas kernels for 51%

profile of v4, /device:TPU:0, one launch (start us, length us, event | category | flops | bytes accessed | tf_op | source)
XLA Modules:
  0.0 390.0 jit_solution(11424262873761535717)
XLA Ops:
  0.0 9.0 %shard_map.55 = (bf16[512,1024]{1,0:T(8,128)(2,1)}, bf16[256,4096]{1,0:T(8,128)(2,1)}) custom-call(bf16[512,4096]{1,0:T(8,128)(2,1)} %x_hbm.3, bf16[4096,2048]{1,0:T(8,128)(2,1)} %refs_0_.10), custom_call_target="tpu_custom_call" | custom-call | flops 4294967296 | bytes 8388608 | tf_op jit(solution)/shard_map/pallas_call | solution.py:247
  12.3 9.2 %shard_map.56 = (bf16[512,1024]{1,0:T(8,128)(2,1)}, bf16[256,4096]{1,0:T(8,128)(2,1)}) custom-call(bf16[512,4096]{1,0:T(8,128)(2,1)} %x_hbm.3, bf16[4096,2048]{1,0:T(8,128)(2,1)} %refs_0_.10), custom_call_target="tpu_custom_call" | custom-call | flops 4294967296 | bytes 8388608 | tf_op jit(solution)/shard_map/pallas_call | solution.py:247
  21.5 24.6 %shard_map.57 = (bf16[2048,512]{1,0:T(8,128)(2,1)}, bf16[512,2048]{1,0:T(8,128)(2,1)}, bf16[256,4096]{1,0:T(8,128)(2,1)}, bf16[128,4096]{1,0:T(8,128)(2,1)}, bf16[256,4096]{1,0:T(8,128)(2,1)}) custom-call(bf16[512,4096]{1,0:T(8,128)(2,1)} %x_hbm.3, bf16[4096,2048]{1,0:T(8,128)(2,1)} %refs_1_.5, bf16[4096,2048]{1,0:T(8,128)(2,1)} %refs_0_.11, ...), custom_call_target="tpu_custom_call" | custom-call | flops 17179869184 | bytes 33554432 | tf_op jit(solution)/shard_map/pallas_call | solution.py:247
  48.1 11.0 %collective-permute-done.x_hbm = bf16[256,4096]{1,0:T(8,128)(2,1)} collective-permute-done((bf16[256,4096]{1,0:T(8,128)(2,1)}, bf16[256,4096]{1,0:T(8,128)(2,1)}, u32[]{:S(2)}, u32[]{:S(2)}) %collective-permute-start) | collective-permute-done | bytes 2097184 | tf_op jit(solution)/shard_map/ppermute | solution.py:379
  59.1 19.4 %shard_map.58 = (bf16[256,2048]{1,0:T(8,128)(2,1)}, bf16[2048,256]{1,0:T(8,128)(2,1)}, bf16[256,2048]{1,0:T(8,128)(2,1)}) custom-call(bf16[256,4096]{1,0:T(8,128)(2,1)} %collective-permute-done.x_hbm, bf16[4096,2048]{1,0:T(8,128)(2,1)} %refs_0_.10, bf16[4096,2048]{1,0:T(8,128)(2,1)} %refs_1_.5, bf16[4096,2048]{1,0:T(8,128)(2,1)} %refs_0_.11), custom_call_target="tpu_custom_call" | custom-call | flops 12884901888 | bytes 50331648 | tf_op jit(solution)/shard_map/pallas_call | solution.py:247
  80.6 14.6 %shard_map.59 = (f32[16,1,512]{2,1,0:T(1,128)}, f32[16,1,512]{2,1,0:T(1,128)}, f32[2048,512]{1,0:T(8,128)}) custom-call(bf16[512,2048]{1,0:T(8,128)(2,1)} %get-tuple-element.104.refs_0_, bf16[512,1024]{1,0:T(8,128)(2,1)} %get-tuple-element.69.refs_1_.refs_2_, bf16[512,1024]{1,0:T(8,128)(2,1)} %get-tuple-element.70.refs_2_.refs_3_, ...), custom_call_target="tpu_custom_call" | custom-call | flops 8589934592 | bytes 10485760 | tf_op jit(solution)/shard_map/pallas_call | solution.py:143
  95.2 8.0 %collective-permute-done.1.x_hbm = bf16[256,4096]{1,0:T(8,128)(2,1)} collective-permute-done((bf16[256,4096]{1,0:T(8,128)(2,1)}, bf16[256,4096]{1,0:T(8,128)(2,1)}, u32[]{:S(2)}, u32[]{:S(2)}) %collective-permute-start.1) | collective-permute-done | bytes 2097184 | tf_op jit(solution)/shard_map/ppermute | solution.py:379
  103.2 14.3 %shard_map.60 = (bf16[256,2048]{1,0:T(8,128)(2,1)}, bf16[2048,256]{1,0:T(8,128)(2,1)}) custom-call(bf16[256,4096]{1,0:T(8,128)(2,1)} %collective-permute-done.1.x_hbm, bf16[4096,2048]{1,0:T(8,128)(2,1)} %refs_0_.10, bf16[4096,2048]{1,0:T(8,128)(2,1)} %refs_1_.5), custom_call_target="tpu_custom_call" | custom-call | flops 8589934592 | bytes 33554432 | tf_op jit(solution)/shard_map/pallas_call | solution.py:247
  118.6 20.8 %collective-permute-done.10.refs_17_.refs_10_ = bf16[512,1024]{1,0:T(8,128)(2,1)} collective-permute-done((bf16[512,1024]{1,0:T(8,128)(2,1)}, bf16[512,1024]{1,0:T(8,128)(2,1)}, u32[]{:S(2)}, u32[]{:S(2)}) %collective-permute-start.10) | collective-permute-done | bytes 1048608 | tf_op jit(solution)/shard_map/ppermute | solution.py:380
  139.9 9.0 %shard_map.61.refs_1_.refs_2_ = bf16[256,2048]{1,0:T(8,128)(2,1)} custom-call(bf16[256,4096]{1,0:T(8,128)(2,1)} %collective-permute-done.1.x_hbm, bf16[4096,2048]{1,0:T(8,128)(2,1)} %refs_0_.11), custom_call_target="tpu_custom_call" | custom-call | flops 4294967296 | bytes 16777216 | tf_op jit(solution)/shard_map/pallas_call | solution.py:247
  154.8 33.8 %shard_map.62 = (f32[16,1,512]{2,1,0:T(1,128)}, f32[16,1,512]{2,1,0:T(1,128)}, f32[2048,512]{1,0:T(8,128)}) custom-call(bf16[256,2048]{1,0:T(8,128)(2,1)} %get-tuple-element.97.refs_0_.refs_1_, bf16[256,2048]{1,0:T(8,128)(2,1)} %shard_map.61.refs_1_.refs_2_, bf16[512,1024]{1,0:T(8,128)(2,1)} %get-tuple-element.69.refs_1_.refs_2_, ...), custom_call_target="tpu_custom_call" | custom-call | flops 25769803776 | bytes 27262976 | tf_op jit(solution)/shard_map/pallas_call | solution.py:143
  188.9 10.9 %collective-permute-done.17.refs_4_.refs_3_ = bf16[2048,256]{1,0:T(8,128)(2,1)} collective-permute-done((bf16[2048,256]{1,0:T(8,128)(2,1)}, bf16[2048,256]{1,0:T(8,128)(2,1)}, u32[]{:S(2)}, u32[]{:S(2)}) %collective-permute-start.17) | collective-permute-done | bytes 1048608 | tf_op jit(solution)/shard_map/ppermute | solution.py:380
  199.9 42.4 %collective-permute-done.28.refs_3_ = bf16[256,4096]{1,0:T(8,128)(2,1)} collective-permute-done((bf16[256,4096]{1,0:T(8,128)(2,1)}, bf16[256,4096]{1,0:T(8,128)(2,1)}, u32[]{:S(2)}, u32[]{:S(2)}) %collective-permute-start.28) | collective-permute-done | bytes 2097184 | tf_op jit(solution)/shard_map/ppermute | solution.py:379
  242.3 24.0 %shard_map.63 = (f32[16,1,512]{2,1,0:T(1,128)}, f32[16,1,512]{2,1,0:T(1,128)}, f32[2048,512]{1,0:T(8,128)}) custom-call(bf16[512,2048]{1,0:T(8,128)(2,1)} %get-tuple-element.104.refs_0_, bf16[256,2048]{1,0:T(8,128)(2,1)} %get-tuple-element.75.refs_8_.refs_1_, ...), custom_call_target="tpu_custom_call", output_to_operand_aliasing={{0}: (15, {}), {1}: (16, {}), {2}: (17, {})} | custom-call | flops 17179869184 | bytes 18874368 | tf_op jit(solution)/shard_map/pallas_call | solution.py:143
  266.3 8.8 %shard_map.64 = (f32[16,1,512]{2,1,0:T(1,128)}, f32[16,1,512]{2,1,0:T(1,128)}, f32[2048,512]{1,0:T(8,128)}) custom-call(bf16[256,2048]{1,0:T(8,128)(2,1)} %get-tuple-element.97.refs_0_.refs_1_, bf16[256,2048]{1,0:T(8,128)(2,1)} %shard_map.61.refs_1_.refs_2_, ...), custom_call_target="tpu_custom_call", output_to_operand_aliasing={{0}: (6, {}), {1}: (7, {}), {2}: (8, {})} | custom-call | flops 4294967296 | bytes 6291456 | tf_op jit(solution)/shard_map/pallas_call | solution.py:143
  279.6 5.3 %shard_map.65 = bf16[512,1024]{1,0:T(8,128)(2,1)} custom-call(s32[1]{0:T(128)} %bitcast.1.refs_0_, bf16[256,2048]{1,0:T(8,128)(2,1)} %get-tuple-element.97.refs_0_.refs_1_, bf16[256,2048]{1,0:T(8,128)(2,1)} %shard_map.61.refs_1_.refs_2_, bf16[256,2048]{1,0:T(8,128)(2,1)} %copy-done, bf16[256,2048]{1,0:T(8,128)(2,1)} %copy-done.1, ...), custom_call_target="tpu_custom_call" | custom-call | flops 2147483648 | bytes 3145728 | tf_op jit(solution)/shard_map/pallas_call | solution.py:143
  284.9 5.3 %shard_map.66 = bf16[512,1024]{1,0:T(8,128)(2,1)} custom-call(s32[1]{0:T(128)} %bitcast.refs_0_, bf16[256,2048]{1,0:T(8,128)(2,1)} %get-tuple-element.97.refs_0_.refs_1_, bf16[256,2048]{1,0:T(8,128)(2,1)} %shard_map.61.refs_1_.refs_2_, bf16[256,2048]{1,0:T(8,128)(2,1)} %copy-done, bf16[256,2048]{1,0:T(8,128)(2,1)} %copy-done.1, ...), custom_call_target="tpu_custom_call" | custom-call | flops 2147483648 | bytes 3145728 | tf_op jit(solution)/shard_map/pallas_call | solution.py:143
  290.7 10.9 %collective-permute-done.24.refs_5_ = bf16[128,4096]{1,0:T(8,128)(2,1)} collective-permute-done((bf16[128,4096]{1,0:T(8,128)(2,1)}, bf16[128,4096]{1,0:T(8,128)(2,1)}, u32[]{:S(2)}, u32[]{:S(2)}) %collective-permute-start.24) | collective-permute-done | bytes 1048608 | tf_op jit(solution)/shard_map/ppermute | solution.py:379
  304.7 11.6 %shard_map.67.refs_0_ = bf16[512,2048]{1,0:T(8,128)(2,1)} custom-call(bf16[512,2048]{1,0:T(8,128)(2,1)} %get-tuple-element.104.refs_0_, bf16[256,2048]{1,0:T(8,128)(2,1)} %collective-permute-done.15.refs_2_.refs_1_, bf16[256,2048]{1,0:T(8,128)(2,1)} %collective-permute-done.16.refs_3_.refs_2_, bf16[2048,256]{1,0:T(8,128)(2,1)} %collective-permute-done.17.refs_4_.refs_3_, ...), custom_call_target="tpu_custom_call" | custom-call | flops 8589934592 | bytes 10485760 | tf_op jit(solution)/shard_map/pallas_call | solution.py:143
  316.9 10.5 %collective-permute-done.30.refs_1_ = bf16[512,1024]{1,0:T(8,128)(2,1)} collective-permute-done((bf16[512,1024]{1,0:T(8,128)(2,1)}, bf16[512,1024]{1,0:T(8,128)(2,1)}, u32[]{:S(2)}, u32[]{:S(2)}) %collective-permute-start.30) | collective-permute-done | bytes 1048608 | tf_op jit(solution)/shard_map/ppermute | solution.py:379
  327.4 19.9 %shard_map.68.refs_7_ = f32[512,4096]{1,0:T(8,128)} custom-call(bf16[512,2048]{1,0:T(8,128)(2,1)} %shard_map.67.refs_0_, bf16[512,1024]{1,0:T(8,128)(2,1)} %collective-permute-done.30.refs_1_, bf16[2048,4096]{1,0:T(8,128)(2,1)} %refs_2_.5, bf16[256,4096]{1,0:T(8,128)(2,1)} %collective-permute-done.28.refs_3_, ...), custom_call_target="tpu_custom_call" | custom-call | flops 12884901888 | bytes 25165824 | tf_op jit(solution)/shard_map/pallas_call | solution.py:355
  347.4 4.7 %collective-permute-done.29.refs_3_ = bf16[256,4096]{1,0:T(8,128)(2,1)} collective-permute-done((bf16[256,4096]{1,0:T(8,128)(2,1)}, bf16[256,4096]{1,0:T(8,128)(2,1)}, u32[]{:S(2)}, u32[]{:S(2)}) %collective-permute-start.29) | collective-permute-done | bytes 2097184 | tf_op jit(solution)/shard_map/ppermute | solution.py:380
  352.4 21.4 %collective-permute-done.25.refs_5_ = bf16[128,4096]{1,0:T(8,128)(2,1)} collective-permute-done((bf16[128,4096]{1,0:T(8,128)(2,1)}, bf16[128,4096]{1,0:T(8,128)(2,1)}, u32[]{:S(2)}, u32[]{:S(2)}) %collective-permute-start.25) | collective-permute-done | bytes 1048608 | tf_op jit(solution)/shard_map/ppermute | solution.py:380
  379.6 10.2 %shard_map.69 = bf16[512,4096]{1,0:T(8,128)(2,1)} custom-call(bf16[512,1024]{1,0:T(8,128)(2,1)} %copy-done.3, bf16[256,4096]{1,0:T(8,128)(2,1)} %collective-permute-done.26.refs_7_.refs_1_, bf16[256,4096]{1,0:T(8,128)(2,1)} %collective-permute-done.27.refs_8_.refs_2_, bf16[256,4096]{1,0:T(8,128)(2,1)} %collective-permute-done.29.refs_3_, ...), custom_call_target="tpu_custom_call" | custom-call | flops 4294967296 | bytes 8388608 | tf_op jit(solution)/shard_map/pallas_call | solution.py:355
  (75 shorter events, 30.0 us)
Async XLA Ops:
  9.0 50.2 %collective-permute-start = (bf16[256,4096]{1,0:T(8,128)(2,1)}, bf16[256,4096]{1,0:T(8,128)(2,1)}, u32[]{:S(2)}, u32[]{:S(2)}) collective-permute-start(bf16[256,4096]{1,0:T(8,128)(2,1)} %get-tuple-element.57), channel_id=1, source_target_pairs={{0,4},{4,0},{1,5},{5,1},{2,6},{6,2},{3,7},{7,3}} | collective-permute-start | bytes 6291464 | tf_op jit(solution)/shard_map/ppermute | solution.py:379
  46.1 34.6 %collective-permute-start.4 = (bf16[2048,512]{1,0:T(8,128)(2,1)}, bf16[2048,512]{1,0:T(8,128)(2,1)}, u32[]{:S(2)}, u32[]{:S(2)}) collective-permute-start(bf16[2048,512]{1,0:T(8,128)(2,1)} %get-tuple-element.68.refs_3_.refs_4_), channel_id=1, source_target_pairs={{0,1},{1,0},{2,3},{3,2},{4,5},{5,4},{6,7},{7,6}} | collective-permute-start | bytes 6291464 | tf_op jit(solution)/shard_map/ppermute | solution.py:381
  46.1 57.1 %collective-permute-start.1 = (bf16[256,4096]{1,0:T(8,128)(2,1)}, bf16[256,4096]{1,0:T(8,128)(2,1)}, u32[]{:S(2)}, u32[]{:S(2)}) collective-permute-start(bf16[256,4096]{1,0:T(8,128)(2,1)} %get-tuple-element.66), channel_id=1, source_target_pairs={{0,4},{4,0},{1,5},{5,1},{2,6},{6,2},{3,7},{7,3}} | collective-permute-start | bytes 6291464 | tf_op jit(solution)/shard_map/ppermute | solution.py:379
  46.1 72.0 %collective-permute-start.11 = (bf16[2048,512]{1,0:T(8,128)(2,1)}, bf16[2048,512]{1,0:T(8,128)(2,1)}, u32[]{:S(2)}, u32[]{:S(2)}) collective-permute-start(bf16[2048,512]{1,0:T(8,128)(2,1)} %get-tuple-element.68.refs_3_.refs_4_), channel_id=1, source_target_pairs={{0,2},{1,3},{2,0},{3,1},{4,6},{5,7},{6,4},{7,5}} | collective-permute-start | bytes 6291464 | tf_op jit(solution)/shard_map/ppermute | solution.py:380
  48.1 30.4 %collective-permute-start.2 = (bf16[512,1024]{1,0:T(8,128)(2,1)S(1)}, bf16[512,1024]{1,0:T(8,128)(2,1)}, u32[]{:S(2)}, u32[]{:S(2)}) collective-permute-start(bf16[512,1024]{1,0:T(8,128)(2,1)S(1)} %copy-done.5), channel_id=1, source_target_pairs={{0,1},{1,0},{2,3},{3,2},{4,5},{5,4},{6,7},{7,6}} | collective-permute-start | bytes 3145736 | tf_op jit(solution)/shard_map/ppermute | solution.py:381
  78.6 39.6 %collective-permute-start.9 = (bf16[512,1024]{1,0:T(8,128)(2,1)S(1)}, bf16[512,1024]{1,0:T(8,128)(2,1)}, u32[]{:S(2)}, u32[]{:S(2)}) collective-permute-start(bf16[512,1024]{1,0:T(8,128)(2,1)S(1)} %copy-done.5), channel_id=1, source_target_pairs={{0,2},{1,3},{2,0},{3,1},{4,6},{5,7},{6,4},{7,5}} | collective-permute-start | bytes 3145736 | tf_op jit(solution)/shard_map/ppermute | solution.py:380
  80.6 58.8 %collective-permute-start.10 = (bf16[512,1024]{1,0:T(8,128)(2,1)}, bf16[512,1024]{1,0:T(8,128)(2,1)}, u32[]{:S(2)}, u32[]{:S(2)}) collective-permute-start(bf16[512,1024]{1,0:T(8,128)(2,1)} %get-tuple-element.70.refs_2_.refs_3_), channel_id=1, source_target_pairs={{0,2},{1,3},{2,0},{3,1},{4,6},{5,7},{6,4},{7,5}} | collective-permute-start | bytes 3145736 | tf_op jit(solution)/shard_map/ppermute | solution.py:380
  118.1 35.0 %collective-permute-start.14 = (bf16[2048,512]{1,0:T(8,128)(2,1)}, bf16[2048,512]{1,0:T(8,128)(2,1)}, u32[]{:S(2)}, u32[]{:S(2)}) collective-permute-start(bf16[2048,512]{1,0:T(8,128)(2,1)} %collective-permute-done.11.refs_18_.refs_11_), channel_id=1, source_target_pairs={{0,1},{1,0},{2,3},{3,2},{4,5},{5,4},{6,7},{7,6}} | collective-permute-start | bytes 6291464 | tf_op jit(solution)/shard_map/ppermute | solution.py:381
  118.1 32.6 %collective-permute-start.8 = (bf16[2048,256]{1,0:T(8,128)(2,1)}, bf16[2048,256]{1,0:T(8,128)(2,1)S(1)}, u32[]{:S(2)}, u32[]{:S(2)}) collective-permute-start(bf16[2048,256]{1,0:T(8,128)(2,1)} %get-tuple-element.73.refs_11_.refs_4_), channel_id=1, source_target_pairs={{0,1},{1,0},{2,3},{3,2},{4,5},{5,4},{6,7},{7,6}} | collective-permute-start | bytes 3145736 | tf_op jit(solution)/shard_map/ppermute | solution.py:381
  149.0 141.3 %collective-permute-start.26 = (bf16[256,4096]{1,0:T(8,128)(2,1)}, bf16[256,4096]{1,0:T(8,128)(2,1)}, u32[]{:S(2)}, u32[]{:S(2)}) collective-permute-start(bf16[256,4096]{1,0:T(8,128)(2,1)} %get-tuple-element.62), channel_id=1, source_target_pairs={{0,4},{4,0},{1,5},{5,1},{2,6},{6,2},{3,7},{7,3}} | collective-permute-start | bytes 6291464 | tf_op jit(solution)/shard_map/ppermute | solution.py:379
  150.7 91.5 %collective-permute-start.28 = (bf16[256,4096]{1,0:T(8,128)(2,1)}, bf16[256,4096]{1,0:T(8,128)(2,1)}, u32[]{:S(2)}, u32[]{:S(2)}) collective-permute-start(bf16[256,4096]{1,0:T(8,128)(2,1)} %get-tuple-element.102), channel_id=1, source_target_pairs={{0,4},{4,0},{1,5},{5,1},{2,6},{6,2},{3,7},{7,3}} | collective-permute-start | bytes 6291464 | tf_op jit(solution)/shard_map/ppermute | solution.py:379
  151.0 37.6 %collective-permute-start.15 = (bf16[256,2048]{1,0:T(8,128)(2,1)}, bf16[256,2048]{1,0:T(8,128)(2,1)}, u32[]{:S(2)}, u32[]{:S(2)}) collective-permute-start(bf16[256,2048]{1,0:T(8,128)(2,1)} %get-tuple-element.75.refs_8_.refs_1_), channel_id=1, source_target_pairs={{0,2},{1,3},{2,0},{3,1},{4,6},{5,7},{6,4},{7,5}} | collective-permute-start | bytes 3145736 | tf_op jit(solution)/shard_map/ppermute | solution.py:380
  152.7 47.1 %collective-permute-start.17 = (bf16[2048,256]{1,0:T(8,128)(2,1)}, bf16[2048,256]{1,0:T(8,128)(2,1)}, u32[]{:S(2)}, u32[]{:S(2)}) collective-permute-start(bf16[2048,256]{1,0:T(8,128)(2,1)} %get-tuple-element.77.refs_10_.refs_3_), channel_id=1, source_target_pairs={{0,2},{1,3},{2,0},{3,1},{4,6},{5,7},{6,4},{7,5}} | collective-permute-start | bytes 3145736 | tf_op jit(solution)/shard_map/ppermute | solution.py:380
  153.1 122.0 %collective-permute-start.19 = (bf16[256,2048]{1,0:T(8,128)(2,1)}, bf16[256,2048]{1,0:T(8,128)(2,1)S(1)}, u32[]{:S(2)}, u32[]{:S(2)}) collective-permute-start(bf16[256,2048]{1,0:T(8,128)(2,1)} %get-tuple-element.76.refs_9_.refs_2_), channel_id=1, source_target_pairs={{0,2},{1,3},{2,0},{3,1},{4,6},{5,7},{6,4},{7,5}} | collective-permute-start | bytes 3145736 | tf_op jit(solution)/shard_map/ppermute | solution.py:380
  188.6 87.0 %collective-permute-start.21 = (bf16[2048,256]{1,0:T(8,128)(2,1)}, bf16[2048,256]{1,0:T(8,128)(2,1)}, u32[]{:S(2)}, u32[]{:S(2)}) collective-permute-start(bf16[2048,256]{1,0:T(8,128)(2,1)} %get-tuple-element.73.refs_11_.refs_4_), channel_id=1, source_target_pairs={{0,2},{1,3},{2,0},{3,1},{4,6},{5,7},{6,4},{7,5}} | collective-permute-start | bytes 3145736 | tf_op jit(solution)/shard_map/ppermute | solution.py:380
  199.9 66.4 %collective-permute-start.16 = (bf16[256,2048]{1,0:T(8,128)(2,1)}, bf16[256,2048]{1,0:T(8,128)(2,1)}, u32[]{:S(2)}, u32[]{:S(2)}) collective-permute-start(bf16[256,2048]{1,0:T(8,128)(2,1)} %collective-permute-done.15.refs_2_.refs_1_), channel_id=1, source_target_pairs={{0,1},{1,0},{2,3},{3,2},{4,5},{5,4},{6,7},{7,6}} | collective-permute-start | bytes 3145736 | tf_op jit(solution)/shard_map/ppermute | solution.py:381
  275.7 25.8 %collective-permute-start.24 = (bf16[128,4096]{1,0:T(8,128)(2,1)}, bf16[128,4096]{1,0:T(8,128)(2,1)}, u32[]{:S(2)}, u32[]{:S(2)}) collective-permute-start(bf16[128,4096]{1,0:T(8,128)(2,1)} %get-tuple-element.98), channel_id=1, source_target_pairs={{0,4},{4,0},{1,5},{5,1},{2,6},{6,2},{3,7},{7,3}} | collective-permute-start | bytes 3145736 | tf_op jit(solution)/shard_map/ppermute | solution.py:379
  277.4 39.5 %collective-permute-start.31 = (bf16[256,4096]{1,0:T(8,128)(2,1)}, bf16[256,4096]{1,0:T(8,128)(2,1)}, u32[]{:S(2)}, u32[]{:S(2)}) collective-permute-start(bf16[256,4096]{1,0:T(8,128)(2,1)} %collective-permute-done.28.refs_3_), channel_id=1, source_target_pairs={{0,1},{1,0},{2,3},{3,2},{4,5},{5,4},{6,7},{7,6}} | collective-permute-start | bytes 6291464 | tf_op jit(solution)/shard_map/ppermute | solution.py:381
  290.3 37.2 %collective-permute-start.27 = (bf16[256,4096]{1,0:T(8,128)(2,1)}, bf16[256,4096]{1,0:T(8,128)(2,1)}, u32[]{:S(2)}, u32[]{:S(2)}) collective-permute-start(bf16[256,4096]{1,0:T(8,128)(2,1)} %collective-permute-done.26.refs_7_.refs_1_), channel_id=1, source_target_pairs={{0,1},{1,0},{2,3},{3,2},{4,5},{5,4},{6,7},{7,6}} | collective-permute-start | bytes 6291464 | tf_op jit(solution)/shard_map/ppermute | solution.py:381
  301.6 25.9 %collective-permute-start.30 = (bf16[512,1024]{1,0:T(8,128)(2,1)}, bf16[512,1024]{1,0:T(8,128)(2,1)}, u32[]{:S(2)}, u32[]{:S(2)}) collective-permute-start(bf16[512,1024]{1,0:T(8,128)(2,1)} %shard_map.65), channel_id=1, source_target_pairs={{0,4},{4,0},{1,5},{5,1},{2,6},{6,2},{3,7},{7,3}} | collective-permute-start | bytes 3145736 | tf_op jit(solution)/shard_map/ppermute | solution.py:379
  303.3 48.8 %collective-permute-start.29 = (bf16[256,4096]{1,0:T(8,128)(2,1)}, bf16[256,4096]{1,0:T(8,128)(2,1)}, u32[]{:S(2)}, u32[]{:S(2)}) collective-permute-start(bf16[256,4096]{1,0:T(8,128)(2,1)} %collective-permute-done.28.refs_3_), channel_id=1, source_target_pairs={{0,2},{1,3},{2,0},{3,1},{4,6},{5,7},{6,4},{7,5}} | collective-permute-start | bytes 6291464 | tf_op jit(solution)/shard_map/ppermute | solution.py:380
  316.4 57.4 %collective-permute-start.25 = (bf16[128,4096]{1,0:T(8,128)(2,1)}, bf16[128,4096]{1,0:T(8,128)(2,1)}, u32[]{:S(2)}, u32[]{:S(2)}) collective-permute-start(bf16[128,4096]{1,0:T(8,128)(2,1)} %collective-permute-done.24.refs_5_), channel_id=1, source_target_pairs={{0,2},{1,3},{2,0},{3,1},{4,6},{5,7},{6,4},{7,5}} | collective-permute-start | bytes 3145736 | tf_op jit(solution)/shard_map/ppermute | solution.py:380
  352.1 27.5 %collective-permute-start.33 = (bf16[256,4096]{1,0:T(8,128)(2,1)}, bf16[256,4096]{1,0:T(8,128)(2,1)}, u32[]{:S(2)}, u32[]{:S(2)}) collective-permute-start(bf16[256,4096]{1,0:T(8,128)(2,1)} %collective-permute-done.29.refs_3_), channel_id=1, source_target_pairs={{0,1},{1,0},{2,3},{3,2},{4,5},{5,4},{6,7},{7,6}} | collective-permute-start | bytes 6291464 | tf_op jit(solution)/shard_map/ppermute | solution.py:381
  352.1 25.6 %collective-permute-start.23 = (bf16[512,1024]{1,0:T(8,128)(2,1)S(1)}, bf16[512,1024]{1,0:T(8,128)(2,1)S(1)}, u32[]{:S(2)}, u32[]{:S(2)}) collective-permute-start(bf16[512,1024]{1,0:T(8,128)(2,1)S(1)} %copy-done.2), channel_id=1, source_target_pairs={{0,4},{4,0},{1,5},{5,1},{2,6},{6,2},{3,7},{7,3}} | collective-permute-start | bytes 3145736 | tf_op jit(solution)/shard_map/ppermute | solution.py:379
  (18 other events, 222.2 us)

commit v5 on v4

--- a/solution.py
+++ b/solution.py
@@ -386,11 +386,11 @@
         unit_a = lambda chip_, core_: chip_ * 10 + core_ * 3
         unit_b = lambda core_: 6 + core_ * 2
 
-        middle = w_k.shape[1] // 2
+        middle = w_k.shape[1] * 3 // 8
         k_oa, x_half0 = proj(x_own, [w_k], [False], [(0, middle)], (None, [(0, half)]), 256)
         k_xoa = over_x(k_oa)
         x_f0 = over_y(x_half0)
-        k_ob, x_half = proj(after(x_own, k_oa), [w_k], [False], [(middle, 2 * middle)], (None, [(half, half)]))
+        k_ob, x_half = proj(after(x_own, k_oa), [w_k], [False], [(middle, w_k.shape[1])], (None, [(half, half)]), 256)
         k_xob = over_x(k_ob)
         x_f1 = over_y(x_half)
         first_a = lambda: unit_a(lax.axis_index('sp') // 2, lax.axis_index('sp') % 2) * 128
@@ -408,7 +408,7 @@
         k_xr0, v_xr0 = over_x(k_r0), over_x(v_r0)
         k_sr0, v_sr0 = over_core(k_r0), over_core(v_r0)
         own, own_s = ([(k_oa, k_ob)], [v_o]), ([(k_soa, k_sob)], [v_so])
-        state_o = attend([after(q_o, q_r0)], [own, own_s], None, False, 4)
+        state_o = attend([after(q_o, q_r0)], [own, own_s], None, False, 2)
 
         k_r1, v_r1 = proj(after(x_f1, state_o[0]), [w_k, w_v], [False, True])
         k_xr1, v_xr1 = over_x(k_r1), over_x(v_r1)
@@ -446,7 +446,7 @@
         pieces = [((wb, wb_s), 0, lambda x, c: x * 768, lambda x, c: c != x)]
         pieces += [(wx0, 0, away(same, 0), None), (wx0_s, 0, away(other, 0), None)]
         pieces += [(wx1, 0, away(same, 2), None), (wx1_s, 0, away(other, 2), None)]
-        return fold([after(o_fb, wx1)], pieces, total, jnp.bfloat16)
+        return fold([after(o_fb, wx1)], pieces, total, jnp.bfloat16, 1024)
 
     seq_spec = P(('dp', 'sp', 'hp'), None)
     in_specs = (seq_spec, P(None, 'hp'), P(None, 'hp'), P(None, 'hp'), P('hp', None))

time: 391 us -> 390 us (level)
  transfers between devices with their start and end apart: 35 -> 35, of which waited for: 12 -> 12; matrix products, arithmetic and copies ran while one was open for 0% -> 0% of each run, Pallas kernels for 51% -> 52%
where the time goes in v5:
time: 390 us
  Pallas kernels  220 us (56%)
  waiting for transfers between devices  143 us (37%)
  starting transfers between devices  22.6 us (6%)
    pallas_call x7, Pallas kernels, attend(): pl.pallas_call(functools.partial(attend_kernel, tuple(shape), block, spli...  105 us
    pallas_call x6, Pallas kernels, project(): pl.pallas_call(functools.partial(project_kernel, tuple(flips), width, tup...  85.1 us
    ppermute x7, waiting for transfers between devices, device_fn(): over_y = lambda a: lax.ppermute(a, 'hp', hp_swap)  83.2 us
    ppermute x9, waiting for transfers between devices, device_fn(): over_x = lambda a: lax.ppermute(a, 'sp', x_swap)  58.6 us
    pallas_call x2, Pallas kernels, fold(): pl.pallas_call(functools.partial(fold_kernel, tuple(plan), width, base is...  30.1 us
    ppermute x9, starting transfers between devices, device_fn(): over_x = lambda a: lax.ppermute(a, 'sp', x_swap)  10.1 us
    ppermute x7, starting transfers between devices, device_fn(): over_y = lambda a: lax.ppermute(a, 'hp', hp_swap)  9.2 us
  transfers between devices with their start and end apart: 35, of which 12 were waited for; matrix products, arithmetic and copies ran while one was open for 0% of the time, Pallas kernels for 52%

profile of v5, /device:TPU:0, one launch (start us, length us, event | category | flops | bytes accessed | tf_op | source)
XLA Modules:
  0.0 389.7 jit_solution(1335195093742422441)
XLA Ops:
  0.0 7.6 %shard_map.55 = (bf16[512,768]{1,0:T(8,128)(2,1)}, bf16[256,4096]{1,0:T(8,128)(2,1)}) custom-call(bf16[512,4096]{1,0:T(8,128)(2,1)} %x_hbm.3, bf16[4096,2048]{1,0:T(8,128)(2,1)} %refs_0_.10), custom_call_target="tpu_custom_call" | custom-call | flops 3221225472 | bytes 6291456 | tf_op jit(solution)/shard_map/pallas_call | solution.py:247
  10.9 10.2 %shard_map.56 = (bf16[512,1280]{1,0:T(8,128)(2,1)}, bf16[256,4096]{1,0:T(8,128)(2,1)}) custom-call(bf16[512,4096]{1,0:T(8,128)(2,1)} %x_hbm.3, bf16[4096,2048]{1,0:T(8,128)(2,1)} %refs_0_.10), custom_call_target="tpu_custom_call" | custom-call | flops 5368709120 | bytes 10485760 | tf_op jit(solution)/shard_map/pallas_call | solution.py:247
  21.2 24.6 %shard_map.57 = (bf16[2048,512]{1,0:T(8,128)(2,1)}, bf16[512,2048]{1,0:T(8,128)(2,1)}, bf16[256,4096]{1,0:T(8,128)(2,1)}, bf16[128,4096]{1,0:T(8,128)(2,1)}, bf16[256,4096]{1,0:T(8,128)(2,1)}) custom-call(bf16[512,4096]{1,0:T(8,128)(2,1)} %x_hbm.3, bf16[4096,2048]{1,0:T(8,128)(2,1)} %refs_1_.5, bf16[4096,2048]{1,0:T(8,128)(2,1)} %refs_0_.11, ...), custom_call_target="tpu_custom_call" | custom-call | flops 17179869184 | bytes 33554432 | tf_op jit(solution)/shard_map/pallas_call | solution.py:247
  48.3 9.4 %collective-permute-done.x_hbm = bf16[256,4096]{1,0:T(8,128)(2,1)} collective-permute-done((bf16[256,4096]{1,0:T(8,128)(2,1)}, bf16[256,4096]{1,0:T(8,128)(2,1)}, u32[]{:S(2)}, u32[]{:S(2)}) %collective-permute-start) | collective-permute-done | bytes 2097184 | tf_op jit(solution)/shard_map/ppermute | solution.py:379
  57.7 19.4 %shard_map.58 = (bf16[256,2048]{1,0:T(8,128)(2,1)}, bf16[2048,256]{1,0:T(8,128)(2,1)}, bf16[256,2048]{1,0:T(8,128)(2,1)}) custom-call(bf16[256,4096]{1,0:T(8,128)(2,1)} %collective-permute-done.x_hbm, bf16[4096,2048]{1,0:T(8,128)(2,1)} %refs_0_.10, bf16[4096,2048]{1,0:T(8,128)(2,1)} %refs_1_.5, bf16[4096,2048]{1,0:T(8,128)(2,1)} %refs_0_.11), custom_call_target="tpu_custom_call" | custom-call | flops 12884901888 | bytes 50331648 | tf_op jit(solution)/shard_map/pallas_call | solution.py:247
  79.2 15.9 %shard_map.59 = (f32[16,1,512]{2,1,0:T(1,128)}, f32[16,1,512]{2,1,0:T(1,128)}, f32[2048,512]{1,0:T(8,128)}) custom-call(bf16[512,2048]{1,0:T(8,128)(2,1)} %get-tuple-element.104.refs_0_, bf16[512,768]{1,0:T(8,128)(2,1)} %get-tuple-element.69.refs_1_.refs_2_, bf16[512,1280]{1,0:T(8,128)(2,1)} %get-tuple-element.70.refs_2_.refs_3_, ...), custom_call_target="tpu_custom_call" | custom-call | flops 8589934592 | bytes 10485760 | tf_op jit(solution)/shard_map/pallas_call | solution.py:143
  95.1 6.8 %collective-permute-done.1.x_hbm = bf16[256,4096]{1,0:T(8,128)(2,1)} collective-permute-done((bf16[256,4096]{1,0:T(8,128)(2,1)}, bf16[256,4096]{1,0:T(8,128)(2,1)}, u32[]{:S(2)}, u32[]{:S(2)}) %collective-permute-start.1) | collective-permute-done | bytes 2097184 | tf_op jit(solution)/shard_map/ppermute | solution.py:379
  101.8 14.3 %shard_map.60 = (bf16[256,2048]{1,0:T(8,128)(2,1)}, bf16[2048,256]{1,0:T(8,128)(2,1)}) custom-call(bf16[256,4096]{1,0:T(8,128)(2,1)} %collective-permute-done.1.x_hbm, bf16[4096,2048]{1,0:T(8,128)(2,1)} %refs_0_.10, bf16[4096,2048]{1,0:T(8,128)(2,1)} %refs_1_.5), custom_call_target="tpu_custom_call" | custom-call | flops 8589934592 | bytes 33554432 | tf_op jit(solution)/shard_map/pallas_call | solution.py:247
  116.7 22.4 %collective-permute-done.10.refs_17_.refs_10_ = bf16[512,1280]{1,0:T(8,128)(2,1)} collective-permute-done((bf16[512,1280]{1,0:T(8,128)(2,1)S(1)}, bf16[512,1280]{1,0:T(8,128)(2,1)}, u32[]{:S(2)}, u32[]{:S(2)}) %collective-permute-start.10) | collective-permute-done | bytes 1310752 | tf_op jit(solution)/shard_map/ppermute | solution.py:380
  140.2 9.1 %shard_map.61.refs_1_.refs_2_ = bf16[256,2048]{1,0:T(8,128)(2,1)} custom-call(bf16[256,4096]{1,0:T(8,128)(2,1)} %collective-permute-done.1.x_hbm, bf16[4096,2048]{1,0:T(8,128)(2,1)} %refs_0_.11), custom_call_target="tpu_custom_call" | custom-call | flops 4294967296 | bytes 16777216 | tf_op jit(solution)/shard_map/pallas_call | solution.py:247
  155.0 34.0 %shard_map.62 = (f32[16,1,512]{2,1,0:T(1,128)}, f32[16,1,512]{2,1,0:T(1,128)}, f32[2048,512]{1,0:T(8,128)}) custom-call(bf16[256,2048]{1,0:T(8,128)(2,1)} %get-tuple-element.97.refs_0_.refs_1_, bf16[256,2048]{1,0:T(8,128)(2,1)} %shard_map.61.refs_1_.refs_2_, bf16[512,768]{1,0:T(8,128)(2,1)} %get-tuple-element.69.refs_1_.refs_2_, ...), custom_call_target="tpu_custom_call" | custom-call | flops 25769803776 | bytes 27262976 | tf_op jit(solution)/shard_map/pallas_call | solution.py:143
  190.1 10.0 %collective-permute-done.17.refs_4_.refs_3_ = bf16[2048,256]{1,0:T(8,128)(2,1)} collective-permute-done((bf16[2048,256]{1,0:T(8,128)(2,1)}, bf16[2048,256]{1,0:T(8,128)(2,1)}, u32[]{:S(2)}, u32[]{:S(2)}) %collective-permute-start.17) | collective-permute-done | bytes 1048608 | tf_op jit(solution)/shard_map/ppermute | solution.py:380
  200.1 42.0 %collective-permute-done.28.refs_3_ = bf16[256,4096]{1,0:T(8,128)(2,1)} collective-permute-done((bf16[256,4096]{1,0:T(8,128)(2,1)}, bf16[256,4096]{1,0:T(8,128)(2,1)}, u32[]{:S(2)}, u32[]{:S(2)}) %collective-permute-start.28) | collective-permute-done | bytes 2097184 | tf_op jit(solution)/shard_map/ppermute | solution.py:379
  242.1 24.0 %shard_map.63 = (f32[16,1,512]{2,1,0:T(1,128)}, f32[16,1,512]{2,1,0:T(1,128)}, f32[2048,512]{1,0:T(8,128)}) custom-call(bf16[512,2048]{1,0:T(8,128)(2,1)} %get-tuple-element.104.refs_0_, bf16[256,2048]{1,0:T(8,128)(2,1)} %get-tuple-element.75.refs_8_.refs_1_, ...), custom_call_target="tpu_custom_call", output_to_operand_aliasing={{0}: (15, {}), {1}: (16, {}), {2}: (17, {})} | custom-call | flops 17179869184 | bytes 18874368 | tf_op jit(solution)/shard_map/pallas_call | solution.py:143
  266.1 8.8 %shard_map.64 = (f32[16,1,512]{2,1,0:T(1,128)}, f32[16,1,512]{2,1,0:T(1,128)}, f32[2048,512]{1,0:T(8,128)}) custom-call(bf16[256,2048]{1,0:T(8,128)(2,1)} %get-tuple-element.97.refs_0_.refs_1_, bf16[256,2048]{1,0:T(8,128)(2,1)} %shard_map.61.refs_1_.refs_2_, ...), custom_call_target="tpu_custom_call", output_to_operand_aliasing={{0}: (6, {}), {1}: (7, {}), {2}: (8, {})} | custom-call | flops 4294967296 | bytes 6291456 | tf_op jit(solution)/shard_map/pallas_call | solution.py:143
  279.3 5.4 %shard_map.65 = bf16[512,1024]{1,0:T(8,128)(2,1)} custom-call(s32[1]{0:T(128)} %bitcast.1.refs_0_, bf16[256,2048]{1,0:T(8,128)(2,1)} %get-tuple-element.97.refs_0_.refs_1_, bf16[256,2048]{1,0:T(8,128)(2,1)} %shard_map.61.refs_1_.refs_2_, bf16[256,2048]{1,0:T(8,128)(2,1)} %copy-done, bf16[256,2048]{1,0:T(8,128)(2,1)} %copy-done.1, ...), custom_call_target="tpu_custom_call" | custom-call | flops 2147483648 | bytes 3145728 | tf_op jit(solution)/shard_map/pallas_call | solution.py:143
  284.7 5.3 %shard_map.66 = bf16[512,1024]{1,0:T(8,128)(2,1)} custom-call(s32[1]{0:T(128)} %bitcast.refs_0_, bf16[256,2048]{1,0:T(8,128)(2,1)} %get-tuple-element.97.refs_0_.refs_1_, bf16[256,2048]{1,0:T(8,128)(2,1)} %shard_map.61.refs_1_.refs_2_, bf16[256,2048]{1,0:T(8,128)(2,1)} %copy-done, bf16[256,2048]{1,0:T(8,128)(2,1)} %copy-done.1, ...), custom_call_target="tpu_custom_call" | custom-call | flops 2147483648 | bytes 3145728 | tf_op jit(solution)/shard_map/pallas_call | solution.py:143
  290.4 10.9 %collective-permute-done.24.refs_5_ = bf16[128,4096]{1,0:T(8,128)(2,1)} collective-permute-done((bf16[128,4096]{1,0:T(8,128)(2,1)}, bf16[128,4096]{1,0:T(8,128)(2,1)}, u32[]{:S(2)}, u32[]{:S(2)}) %collective-permute-start.24) | collective-permute-done | bytes 1048608 | tf_op jit(solution)/shard_map/ppermute | solution.py:379
  304.5 11.8 %shard_map.67.refs_0_ = bf16[512,2048]{1,0:T(8,128)(2,1)} custom-call(bf16[512,2048]{1,0:T(8,128)(2,1)} %get-tuple-element.104.refs_0_, bf16[256,2048]{1,0:T(8,128)(2,1)} %collective-permute-done.15.refs_2_.refs_1_, bf16[256,2048]{1,0:T(8,128)(2,1)} %collective-permute-done.16.refs_3_.refs_2_, bf16[2048,256]{1,0:T(8,128)(2,1)} %collective-permute-done.17.refs_4_.refs_3_, ...), custom_call_target="tpu_custom_call" | custom-call | flops 8589934592 | bytes 10485760 | tf_op jit(solution)/shard_map/pallas_call | solution.py:143
  316.9 10.3 %collective-permute-done.30.refs_1_ = bf16[512,1024]{1,0:T(8,128)(2,1)} collective-permute-done((bf16[512,1024]{1,0:T(8,128)(2,1)}, bf16[512,1024]{1,0:T(8,128)(2,1)}, u32[]{:S(2)}, u32[]{:S(2)}) %collective-permute-start.30) | collective-permute-done | bytes 1048608 | tf_op jit(solution)/shard_map/ppermute | solution.py:379
  327.2 19.9 %shard_map.68.refs_7_ = f32[512,4096]{1,0:T(8,128)} custom-call(bf16[512,2048]{1,0:T(8,128)(2,1)} %shard_map.67.refs_0_, bf16[512,1024]{1,0:T(8,128)(2,1)} %collective-permute-done.30.refs_1_, bf16[2048,4096]{1,0:T(8,128)(2,1)} %refs_2_.5, bf16[256,4096]{1,0:T(8,128)(2,1)} %collective-permute-done.28.refs_3_, ...), custom_call_target="tpu_custom_call" | custom-call | flops 12884901888 | bytes 25165824 | tf_op jit(solution)/shard_map/pallas_call | solution.py:355
  347.1 4.7 %collective-permute-done.29.refs_3_ = bf16[256,4096]{1,0:T(8,128)(2,1)} collective-permute-done((bf16[256,4096]{1,0:T(8,128)(2,1)}, bf16[256,4096]{1,0:T(8,128)(2,1)}, u32[]{:S(2)}, u32[]{:S(2)}) %collective-permute-start.29) | collective-permute-done | bytes 2097184 | tf_op jit(solution)/shard_map/ppermute | solution.py:380
  352.2 21.4 %collective-permute-done.25.refs_5_ = bf16[128,4096]{1,0:T(8,128)(2,1)} collective-permute-done((bf16[128,4096]{1,0:T(8,128)(2,1)}, bf16[128,4096]{1,0:T(8,128)(2,1)}, u32[]{:S(2)}, u32[]{:S(2)}) %collective-permute-start.25) | collective-permute-done | bytes 1048608 | tf_op jit(solution)/shard_map/ppermute | solution.py:380
  379.4 10.1 %shard_map.69 = bf16[512,4096]{1,0:T(8,128)(2,1)} custom-call(bf16[512,1024]{1,0:T(8,128)(2,1)} %copy-done.3, bf16[256,4096]{1,0:T(8,128)(2,1)} %collective-permute-done.26.refs_7_.refs_1_, bf16[256,4096]{1,0:T(8,128)(2,1)} %collective-permute-done.27.refs_8_.refs_2_, bf16[256,4096]{1,0:T(8,128)(2,1)} %collective-permute-done.29.refs_3_, ...), custom_call_target="tpu_custom_call" | custom-call | flops 4294967296 | bytes 8388608 | tf_op jit(solution)/shard_map/pallas_call | solution.py:355
  (75 shorter events, 31.2 us)
Async XLA Ops:
  7.6 50.2 %collective-permute-start = (bf16[256,4096]{1,0:T(8,128)(2,1)}, bf16[256,4096]{1,0:T(8,128)(2,1)}, u32[]{:S(2)}, u32[]{:S(2)}) collective-permute-start(bf16[256,4096]{1,0:T(8,128)(2,1)} %get-tuple-element.57), channel_id=1, source_target_pairs={{0,4},{4,0},{1,5},{5,1},{2,6},{6,2},{3,7},{7,3}} | collective-permute-start | bytes 6291464 | tf_op jit(solution)/shard_map/ppermute | solution.py:379
  45.8 33.4 %collective-permute-start.4 = (bf16[2048,512]{1,0:T(8,128)(2,1)}, bf16[2048,512]{1,0:T(8,128)(2,1)}, u32[]{:S(2)}, u32[]{:S(2)}) collective-permute-start(bf16[2048,512]{1,0:T(8,128)(2,1)} %get-tuple-element.68.refs_3_.refs_4_), channel_id=1, source_target_pairs={{0,1},{1,0},{2,3},{3,2},{4,5},{5,4},{6,7},{7,6}} | collective-permute-start | bytes 6291464 | tf_op jit(solution)/shard_map/ppermute | solution.py:381
  45.8 33.3 %collective-permute-start.3 = (bf16[512,1280]{1,0:T(8,128)(2,1)S(1)}, bf16[512,1280]{1,0:T(8,128)(2,1)}, u32[]{:S(2)}, u32[]{:S(2)}) collective-permute-start(bf16[512,1280]{1,0:T(8,128)(2,1)S(1)} %copy-done.5), channel_id=1, source_target_pairs={{0,1},{1,0},{2,3},{3,2},{4,5},{5,4},{6,7},{7,6}} | collective-permute-start | bytes 3932168 | tf_op jit(solution)/shard_map/ppermute | solution.py:381
  46.3 55.5 %collective-permute-start.1 = (bf16[256,4096]{1,0:T(8,128)(2,1)}, bf16[256,4096]{1,0:T(8,128)(2,1)}, u32[]{:S(2)}, u32[]{:S(2)}) collective-permute-start(bf16[256,4096]{1,0:T(8,128)(2,1)} %get-tuple-element.66), channel_id=1, source_target_pairs={{0,4},{4,0},{1,5},{5,1},{2,6},{6,2},{3,7},{7,3}} | collective-permute-start | bytes 6291464 | tf_op jit(solution)/shard_map/ppermute | solution.py:379
  46.3 69.8 %collective-permute-start.11 = (bf16[2048,512]{1,0:T(8,128)(2,1)}, bf16[2048,512]{1,0:T(8,128)(2,1)}, u32[]{:S(2)}, u32[]{:S(2)}) collective-permute-start(bf16[2048,512]{1,0:T(8,128)(2,1)} %get-tuple-element.68.refs_3_.refs_4_), channel_id=1, source_target_pairs={{0,2},{1,3},{2,0},{3,1},{4,6},{5,7},{6,4},{7,5}} | collective-permute-start | bytes 6291464 | tf_op jit(solution)/shard_map/ppermute | solution.py:380
  77.1 39.6 %collective-permute-start.9 = (bf16[512,768]{1,0:T(8,128)(2,1)}, bf16[512,768]{1,0:T(8,128)(2,1)}, u32[]{:S(2)}, u32[]{:S(2)}) collective-permute-start(bf16[512,768]{1,0:T(8,128)(2,1)} %get-tuple-element.69.refs_1_.refs_2_), channel_id=1, source_target_pairs={{0,2},{1,3},{2,0},{3,1},{4,6},{5,7},{6,4},{7,5}} | collective-permute-start | bytes 2359304 | tf_op jit(solution)/shard_map/ppermute | solution.py:380
  79.1 60.0 %collective-permute-start.10 = (bf16[512,1280]{1,0:T(8,128)(2,1)S(1)}, bf16[512,1280]{1,0:T(8,128)(2,1)}, u32[]{:S(2)}, u32[]{:S(2)}) collective-permute-start(bf16[512,1280]{1,0:T(8,128)(2,1)S(1)} %copy-done.5), channel_id=1, source_target_pairs={{0,2},{1,3},{2,0},{3,1},{4,6},{5,7},{6,4},{7,5}} | collective-permute-start | bytes 3932168 | tf_op jit(solution)/shard_map/ppermute | solution.py:380
  101.8 37.8 %collective-permute-start.5 = (bf16[256,2048]{1,0:T(8,128)(2,1)}, bf16[256,2048]{1,0:T(8,128)(2,1)}, u32[]{:S(2)}, u32[]{:S(2)}) collective-permute-start(bf16[256,2048]{1,0:T(8,128)(2,1)} %get-tuple-element.75.refs_8_.refs_1_), channel_id=1, source_target_pairs={{0,1},{1,0},{2,3},{3,2},{4,5},{5,4},{6,7},{7,6}} | collective-permute-start | bytes 3145736 | tf_op jit(solution)/shard_map/ppermute | solution.py:381
  116.2 37.9 %collective-permute-start.14 = (bf16[2048,512]{1,0:T(8,128)(2,1)}, bf16[2048,512]{1,0:T(8,128)(2,1)}, u32[]{:S(2)}, u32[]{:S(2)}) collective-permute-start(bf16[2048,512]{1,0:T(8,128)(2,1)} %collective-permute-done.11.refs_18_.refs_11_), channel_id=1, source_target_pairs={{0,1},{1,0},{2,3},{3,2},{4,5},{5,4},{6,7},{7,6}} | collective-permute-start | bytes 6291464 | tf_op jit(solution)/shard_map/ppermute | solution.py:381
  149.2 140.8 %collective-permute-start.26 = (bf16[256,4096]{1,0:T(8,128)(2,1)}, bf16[256,4096]{1,0:T(8,128)(2,1)}, u32[]{:S(2)}, u32[]{:S(2)}) collective-permute-start(bf16[256,4096]{1,0:T(8,128)(2,1)} %get-tuple-element.62), channel_id=1, source_target_pairs={{0,4},{4,0},{1,5},{5,1},{2,6},{6,2},{3,7},{7,3}} | collective-permute-start | bytes 6291464 | tf_op jit(solution)/shard_map/ppermute | solution.py:379
  151.0 91.1 %collective-permute-start.28 = (bf16[256,4096]{1,0:T(8,128)(2,1)}, bf16[256,4096]{1,0:T(8,128)(2,1)}, u32[]{:S(2)}, u32[]{:S(2)}) collective-permute-start(bf16[256,4096]{1,0:T(8,128)(2,1)} %get-tuple-element.102), channel_id=1, source_target_pairs={{0,4},{4,0},{1,5},{5,1},{2,6},{6,2},{3,7},{7,3}} | collective-permute-start | bytes 6291464 | tf_op jit(solution)/shard_map/ppermute | solution.py:379
  151.3 37.8 %collective-permute-start.15 = (bf16[256,2048]{1,0:T(8,128)(2,1)}, bf16[256,2048]{1,0:T(8,128)(2,1)}, u32[]{:S(2)}, u32[]{:S(2)}) collective-permute-start(bf16[256,2048]{1,0:T(8,128)(2,1)} %get-tuple-element.75.refs_8_.refs_1_), channel_id=1, source_target_pairs={{0,2},{1,3},{2,0},{3,1},{4,6},{5,7},{6,4},{7,5}} | collective-permute-start | bytes 3145736 | tf_op jit(solution)/shard_map/ppermute | solution.py:380
  153.0 47.1 %collective-permute-start.17 = (bf16[2048,256]{1,0:T(8,128)(2,1)}, bf16[2048,256]{1,0:T(8,128)(2,1)}, u32[]{:S(2)}, u32[]{:S(2)}) collective-permute-start(bf16[2048,256]{1,0:T(8,128)(2,1)} %get-tuple-element.77.refs_10_.refs_3_), channel_id=1, source_target_pairs={{0,2},{1,3},{2,0},{3,1},{4,6},{5,7},{6,4},{7,5}} | collective-permute-start | bytes 3145736 | tf_op jit(solution)/shard_map/ppermute | solution.py:380
  154.1 120.8 %collective-permute-start.19 = (bf16[256,2048]{1,0:T(8,128)(2,1)}, bf16[256,2048]{1,0:T(8,128)(2,1)S(1)}, u32[]{:S(2)}, u32[]{:S(2)}) collective-permute-start(bf16[256,2048]{1,0:T(8,128)(2,1)} %get-tuple-element.76.refs_9_.refs_2_), channel_id=1, source_target_pairs={{0,2},{1,3},{2,0},{3,1},{4,6},{5,7},{6,4},{7,5}} | collective-permute-start | bytes 3145736 | tf_op jit(solution)/shard_map/ppermute | solution.py:380
  189.1 86.4 %collective-permute-start.21 = (bf16[2048,256]{1,0:T(8,128)(2,1)}, bf16[2048,256]{1,0:T(8,128)(2,1)}, u32[]{:S(2)}, u32[]{:S(2)}) collective-permute-start(bf16[2048,256]{1,0:T(8,128)(2,1)} %get-tuple-element.73.refs_11_.refs_4_), channel_id=1, source_target_pairs={{0,2},{1,3},{2,0},{3,1},{4,6},{5,7},{6,4},{7,5}} | collective-permute-start | bytes 3145736 | tf_op jit(solution)/shard_map/ppermute | solution.py:380
  200.1 65.9 %collective-permute-start.16 = (bf16[256,2048]{1,0:T(8,128)(2,1)}, bf16[256,2048]{1,0:T(8,128)(2,1)}, u32[]{:S(2)}, u32[]{:S(2)}) collective-permute-start(bf16[256,2048]{1,0:T(8,128)(2,1)} %collective-permute-done.15.refs_2_.refs_1_), channel_id=1, source_target_pairs={{0,1},{1,0},{2,3},{3,2},{4,5},{5,4},{6,7},{7,6}} | collective-permute-start | bytes 3145736 | tf_op jit(solution)/shard_map/ppermute | solution.py:381
  275.5 25.8 %collective-permute-start.24 = (bf16[128,4096]{1,0:T(8,128)(2,1)}, bf16[128,4096]{1,0:T(8,128)(2,1)}, u32[]{:S(2)}, u32[]{:S(2)}) collective-permute-start(bf16[128,4096]{1,0:T(8,128)(2,1)} %get-tuple-element.98), channel_id=1, source_target_pairs={{0,4},{4,0},{1,5},{5,1},{2,6},{6,2},{3,7},{7,3}} | collective-permute-start | bytes 3145736 | tf_op jit(solution)/shard_map/ppermute | solution.py:379
  277.2 39.7 %collective-permute-start.31 = (bf16[256,4096]{1,0:T(8,128)(2,1)}, bf16[256,4096]{1,0:T(8,128)(2,1)}, u32[]{:S(2)}, u32[]{:S(2)}) collective-permute-start(bf16[256,4096]{1,0:T(8,128)(2,1)} %collective-permute-done.28.refs_3_), channel_id=1, source_target_pairs={{0,1},{1,0},{2,3},{3,2},{4,5},{5,4},{6,7},{7,6}} | collective-permute-start | bytes 6291464 | tf_op jit(solution)/shard_map/ppermute | solution.py:381
  290.0 37.2 %collective-permute-start.27 = (bf16[256,4096]{1,0:T(8,128)(2,1)}, bf16[256,4096]{1,0:T(8,128)(2,1)}, u32[]{:S(2)}, u32[]{:S(2)}) collective-permute-start(bf16[256,4096]{1,0:T(8,128)(2,1)} %collective-permute-done.26.refs_7_.refs_1_), channel_id=1, source_target_pairs={{0,1},{1,0},{2,3},{3,2},{4,5},{5,4},{6,7},{7,6}} | collective-permute-start | bytes 6291464 | tf_op jit(solution)/shard_map/ppermute | solution.py:381
  301.3 25.9 %collective-permute-start.30 = (bf16[512,1024]{1,0:T(8,128)(2,1)}, bf16[512,1024]{1,0:T(8,128)(2,1)}, u32[]{:S(2)}, u32[]{:S(2)}) collective-permute-start(bf16[512,1024]{1,0:T(8,128)(2,1)} %shard_map.65), channel_id=1, source_target_pairs={{0,4},{4,0},{1,5},{5,1},{2,6},{6,2},{3,7},{7,3}} | collective-permute-start | bytes 3145736 | tf_op jit(solution)/shard_map/ppermute | solution.py:379
  303.0 48.8 %collective-permute-start.29 = (bf16[256,4096]{1,0:T(8,128)(2,1)}, bf16[256,4096]{1,0:T(8,128)(2,1)}, u32[]{:S(2)}, u32[]{:S(2)}) collective-permute-start(bf16[256,4096]{1,0:T(8,128)(2,1)} %collective-permute-done.28.refs_3_), channel_id=1, source_target_pairs={{0,2},{1,3},{2,0},{3,1},{4,6},{5,7},{6,4},{7,5}} | collective-permute-start | bytes 6291464 | tf_op jit(solution)/shard_map/ppermute | solution.py:380
  316.4 57.2 %collective-permute-start.25 = (bf16[128,4096]{1,0:T(8,128)(2,1)}, bf16[128,4096]{1,0:T(8,128)(2,1)}, u32[]{:S(2)}, u32[]{:S(2)}) collective-permute-start(bf16[128,4096]{1,0:T(8,128)(2,1)} %collective-permute-done.24.refs_5_), channel_id=1, source_target_pairs={{0,2},{1,3},{2,0},{3,1},{4,6},{5,7},{6,4},{7,5}} | collective-permute-start | bytes 3145736 | tf_op jit(solution)/shard_map/ppermute | solution.py:380
  351.9 27.5 %collective-permute-start.33 = (bf16[256,4096]{1,0:T(8,128)(2,1)}, bf16[256,4096]{1,0:T(8,128)(2,1)}, u32[]{:S(2)}, u32[]{:S(2)}) collective-permute-start(bf16[256,4096]{1,0:T(8,128)(2,1)} %collective-permute-done.29.refs_3_), channel_id=1, source_target_pairs={{0,1},{1,0},{2,3},{3,2},{4,5},{5,4},{6,7},{7,6}} | collective-permute-start | bytes 6291464 | tf_op jit(solution)/shard_map/ppermute | solution.py:381
  351.9 25.6 %collective-permute-start.23 = (bf16[512,1024]{1,0:T(8,128)(2,1)S(1)}, bf16[512,1024]{1,0:T(8,128)(2,1)S(1)}, u32[]{:S(2)}, u32[]{:S(2)}) collective-permute-start(bf16[512,1024]{1,0:T(8,128)(2,1)S(1)} %copy-done.2), channel_id=1, source_target_pairs={{0,4},{4,0},{1,5},{5,1},{2,6},{6,2},{3,7},{7,3}} | collective-permute-start | bytes 3145736 | tf_op jit(solution)/shard_map/ppermute | solution.py:379
  (18 other events, 208.4 us)
